TPU v7x, 32 devices: a whole 2x2x4 slice. The times are simulated.
32 devices in a mesh: dp: 8 (over y, x, core), tensor: 4 (over z).
Axes of the slice: x: 2, y: 2, z: 4, core: 2. Of those that a mesh axis runs over, the one named last changes fastest.
Arguments:
- tokens: bfloat16 [2048, 2048], P('dp'), may hold values from -6 to 6
- norm_attn_gain: float32 [2048], replicated, may hold values from 0.5 to 1.5
- query_weight: bfloat16 [2048, 3072], P(None, 'tensor'), may hold values from -0.125 to 0.125
- latent_down: bfloat16 [2048, 576], replicated, may hold values from -0.125 to 0.125
- latent_gain: float32 [512], replicated, may hold values from 0.5 to 1.5
- latent_up: bfloat16 [512, 4096], P(None, 'tensor'), may hold values from -0.25 to 0.25
- out_weight: bfloat16 [2048, 2048], P('tensor'), may hold values from -2 to 2
- norm_ffn_gain: float32 [2048], replicated, may hold values from 0.5 to 1.5
- router_weight: bfloat16 [2048, 16], replicated, may hold values from -0.125 to 0.125
- shared_gate: bfloat16 [2048, 2816], P(None, 'tensor'), may hold values from -0.125 to 0.125
- shared_up: bfloat16 [2048, 2816], P(None, 'tensor'), may hold values from -0.125 to 0.125
- shared_down: bfloat16 [2816, 2048], P('tensor'), may hold values from -0.109375 to 0.109375
- expert_gate: bfloat16 [16, 2048, 1408], P('dp', None, 'tensor'), may hold values from -0.125 to 0.125
- expert_up: bfloat16 [16, 2048, 1408], P('dp', None, 'tensor'), may hold values from -0.125 to 0.125
- expert_down: bfloat16 [16, 1408, 2048], P('dp', 'tensor'), may hold values from -0.15625 to 0.15625
- expert_ids: int32 [2048, 6], P('dp'), may hold values from 0 to 15, all different within a row; in each aligned block of 256 rows (0 to 255, 256 to 511, ...) at most 192 rows name the same one
- out_grad: bfloat16 [2048, 2048], P('dp'), may hold values from -6 to 6
Outputs:
- block_out: bfloat16 [2048, 2048], P('dp')
- tokens_grad: bfloat16 [2048, 2048], P('dp')
- norm_attn_gain_grad: float32 [2048], P('dp')
- query_weight_grad: float32 [2048, 3072], P('dp', 'tensor')
- latent_down_grad: float32 [2048, 576], P('dp')
- latent_gain_grad: float32 [512], P('dp')
- latent_up_grad: float32 [512, 4096], P('dp', 'tensor')
- out_weight_grad: float32 [2048, 2048], P('tensor', 'dp')
- norm_ffn_gain_grad: float32 [2048], P('dp')
- router_weight_grad: float32 [2048, 16], P('dp')
- shared_gate_grad: float32 [2048, 2816], P('dp', 'tensor')
- shared_up_grad: float32 [2048, 2816], P('dp', 'tensor')
- shared_down_grad: float32 [2816, 2048], P('tensor', 'dp')
- expert_gate_grad: float32 [16, 2048, 1408], P('dp', None, 'tensor')
- expert_up_grad: float32 [16, 2048, 1408], P('dp', None, 'tensor')
- expert_down_grad: float32 [16, 1408, 2048], P('dp', 'tensor')
Inputs may be any that keep to these rules, and one draw needn't show every extreme that they name: `expert_ids`: each row names 6 different experts; in the rows of one device (aligned blocks of 256 rows) no expert is named more than 192 times.
All inputs are finite; a program needn't handle non-finite values.
Results may differ from a plain program's by a relative error of at most 0.023.
Values may be sent and summed in bfloat16 or wider, within the bound.
A program may use at most 320 MiB of HBM per device.

v0:
```python
import jax
import jax.numpy as jnp
from jax import lax
from jax.sharding import PartitionSpec as P

NOPE = 128
ROPE = 64
VD = 128
R = 512
SEQ_DEVS = 8


eps = 1e-06
route_scale = 2.446
rope_base = 50000.0
masked_score = -1e30
highest = lax.Precision.HIGHEST


def from_behind(value, axis, steps):
    count = lax.axis_size(axis)
    initial, last = (max(0, -steps), min(count, count - steps))
    return lax.ppermute(value, axis, [(source, source + steps) for source in range(initial, last)])


def mat_dot(left, right):
    return jnp.dot(left, right, preferred_element_type=jnp.float32)


def rotation(positions):
    half_width = ROPE // 2
    frequency = rope_base ** (-jnp.arange(half_width, dtype=jnp.float32) / half_width)
    angles = positions.astype(jnp.float32)[:, None] * frequency[None, :]
    return (jnp.cos(angles), jnp.sin(angles))


def rotate(values, cos_table, sin_table):
    half_width = values.shape[-1] // 2
    first_half = values[..., :half_width]
    second_half = values[..., half_width:]
    return jnp.concatenate(
        [
            first_half * cos_table - second_half * sin_table,
            second_half * cos_table + first_half * sin_table,
        ],
        -1,
    )


def unrotate(upstream, cos_table, sin_table):
    half_width = upstream.shape[-1] // 2
    first_half = upstream[..., :half_width]
    second_half = upstream[..., half_width:]
    return jnp.concatenate(
        [
            first_half * cos_table + second_half * sin_table,
            second_half * cos_table - first_half * sin_table,
        ],
        -1,
    )


def rms_forward(values, gain_vec):
    inv_rms = lax.rsqrt(jnp.mean(values * values, axis=-1, keepdims=True) + eps)
    return (values * inv_rms * gain_vec, inv_rms)


def rms_backward(values, inv_rms, gain_vec, upstream):
    scaled = upstream * gain_vec
    inner_mean = jnp.mean(values * scaled, axis=-1, keepdims=True)
    return (
        inv_rms * scaled - values * inv_rms**3 * inner_mean,
        jnp.sum(upstream * values * inv_rms, axis=0),
    )


def silu_slope(values):
    logistic = jax.nn.sigmoid(values)
    return logistic * (1.0 + values * (1.0 - logistic))


def send_rows(buffer):
    return lax.all_to_all(buffer, "dp", split_axis=0, concat_axis=0, tiled=True)


def bring_back(buffer, local_part):
    buffer = lax.all_to_all(
        buffer.astype(jnp.bfloat16), "dp", split_axis=0, concat_axis=0, tiled=True
    ).astype(buffer.dtype)
    return (buffer, local_part)


def fetch(returned, buffer_place, tok_rows, top_count):
    flat_rows = returned.reshape(-1, returned.shape[-1])
    return jnp.take(flat_rows, buffer_place, axis=0).reshape(
        tok_rows, top_count, returned.shape[-1]
    )


def shards(
    tokens,
    norm_attn_gain,
    query_weight,
    latent_down,
    latent_gain,
    latent_up,
    out_weight,
    norm_ffn_gain,
    router_weight,
    shared_gate,
    shared_up,
    shared_down,
    expert_gate,
    expert_up,
    expert_down,
    expert_ids,
    out_grad,
):
    tok_rows = tokens.shape[0]
    model_width = tokens.shape[1]
    head_count = out_weight.shape[0] // VD
    groups = lax.axis_size("dp")
    stride = groups // SEQ_DEVS
    local_experts = expert_gate.shape[0]
    experts = local_experts * groups
    top_count = expert_ids.shape[1]
    capacity = 2 * tok_rows * top_count // experts
    seq_stretch = lax.axis_index("dp") // stride
    residual_in = tokens.astype(jnp.float32)
    normed_in, inv_one = rms_forward(residual_in, norm_attn_gain)
    normed_low = normed_in.astype(jnp.bfloat16)
    query_pos = seq_stretch * tok_rows + jnp.arange(tok_rows)
    cos_table, sin_table = rotation(query_pos)
    factor = (NOPE + ROPE) ** (-0.5)
    query = mat_dot(normed_low, query_weight).reshape(tok_rows, head_count, NOPE + ROPE)
    query = (
        jnp.concatenate(
            [
                query[..., :NOPE],
                rotate(query[..., NOPE:], cos_table[:, None, :], sin_table[:, None, :]),
            ],
            -1,
        )
        * factor
    )
    query_low = query.astype(jnp.bfloat16)
    compressed = mat_dot(normed_low, latent_down)
    latent_normed, inv_latent = rms_forward(compressed[:, :R], latent_gain)
    key_rope = rotate(compressed[:, R:], cos_table, sin_table)
    own_latent = jnp.concatenate([latent_normed, key_rope], -1).astype(jnp.bfloat16)
    earlier = [
        from_behind(own_latent, "dp", (SEQ_DEVS - 1 - block_index) * stride)
        for block_index in range(SEQ_DEVS - 1)
    ]
    keys_latent = jnp.concatenate(earlier + [own_latent], 0)
    key_count = keys_latent.shape[0]
    expanded = (
        mat_dot(keys_latent[:, :R], latent_up)
        .reshape(key_count, head_count, NOPE + VD)
        .astype(jnp.bfloat16)
    )
    key_pos = (seq_stretch - (SEQ_DEVS - 1)) * tok_rows + jnp.arange(key_count)
    visible = (key_pos[None, :] >= 0) & (key_pos[None, :] <= query_pos[:, None])

    def attention_scores():
        raw_scores = jnp.einsum(
            "qhd,khd->hqk",
            query_low[..., :NOPE],
            expanded[..., :NOPE],
            preferred_element_type=jnp.float32,
        )
        raw_scores = raw_scores + jnp.einsum(
            "qhd,kd->hqk",
            query_low[..., NOPE:],
            keys_latent[:, R:],
            preferred_element_type=jnp.float32,
        )
        return jnp.where(visible[None], raw_scores, masked_score)

    scores = attention_scores()
    top_score = jnp.max(scores, -1, keepdims=True)
    exp_scores = jnp.exp(scores - top_score)
    exp_total = jnp.sum(exp_scores, -1, keepdims=True)
    log_total = top_score + jnp.log(exp_total)
    probs_low = (exp_scores / exp_total).astype(jnp.bfloat16)
    heads_out = jnp.einsum(
        "hqk,khd->qhd", probs_low, expanded[..., NOPE:], preferred_element_type=jnp.float32
    )
    heads_low = heads_out.reshape(tok_rows, head_count * VD).astype(jnp.bfloat16)
    attn = lax.psum(mat_dot(heads_low, out_weight), "tensor")
    hidden = residual_in + attn
    ffn_in, inv_two = rms_forward(hidden, norm_ffn_gain)
    ffn_low = ffn_in.astype(jnp.bfloat16)
    router = router_weight.astype(jnp.float32)
    router_gates = jax.nn.sigmoid(
        jnp.dot(ffn_in, router, precision=highest, preferred_element_type=jnp.float32)
    )
    pick_table = (expert_ids[..., None] == jnp.arange(experts)[None, None, :]).astype(jnp.float32)
    chosen = jnp.sum(pick_table * router_gates[:, None, :], -1)
    chosen_sum = jnp.sum(chosen, -1, keepdims=True)
    route_weight = route_scale * chosen / chosen_sum
    flat_ids = expert_ids.reshape(-1)
    pick_count = flat_ids.shape[0]
    member = (flat_ids[:, None] == jnp.arange(experts)[None, :]).astype(jnp.int32)
    before_count = jnp.cumsum(member, 0) - member
    slot_index = jnp.sum(before_count * member, 1)
    buffer_place = flat_ids * capacity + slot_index
    source = (
        jnp.full((experts * capacity,), pick_count, jnp.int32)
        .at[buffer_place]
        .set(jnp.arange(pick_count, dtype=jnp.int32))
    )
    token_of = source // top_count
    weight_of = jnp.concatenate([route_weight.reshape(-1), jnp.zeros((1,), jnp.float32)])[source]
    padded_in = jnp.concatenate([ffn_low, jnp.zeros((1, model_width), jnp.bfloat16)], 0)
    arrived = send_rows(padded_in[token_of].reshape(experts, capacity, model_width))
    arrived = arrived.reshape(groups, local_experts, capacity, model_width)
    gate_act = jnp.einsum(
        "secd,edf->secf", arrived, expert_gate, preferred_element_type=jnp.float32
    )
    up_act = jnp.einsum("secd,edf->secf", arrived, expert_up, preferred_element_type=jnp.float32)
    act_low = (jax.nn.silu(gate_act) * up_act).astype(jnp.bfloat16)
    expert_out = jnp.einsum(
        "secf,efd->secd", act_low, expert_down, preferred_element_type=jnp.float32
    )
    expert_out = expert_out.reshape(experts, capacity, model_width)
    shared_gate_act = mat_dot(ffn_low, shared_gate)
    shared_up_act = mat_dot(ffn_low, shared_up)
    shared_low = (jax.nn.silu(shared_gate_act) * shared_up_act).astype(jnp.bfloat16)
    shared_out = mat_dot(shared_low, shared_down)
    returned, local_part = bring_back(expert_out, shared_out)
    fetched = fetch(returned, buffer_place, tok_rows, top_count)
    routed_part = local_part + jnp.einsum("tk,tkd->td", route_weight, fetched)
    grad_full = out_grad.astype(jnp.float32)
    weight_grad_part = jnp.einsum("td,tkd->tk", grad_full, fetched)
    moe_out, weight_grad = (
        lax.psum(routed_part.astype(jnp.bfloat16), "tensor").astype(jnp.float32),
        lax.psum(weight_grad_part.astype(jnp.bfloat16), "tensor").astype(jnp.float32),
    )
    block_out = (hidden + moe_out).astype(jnp.bfloat16)
    padded_grad = jnp.concatenate([out_grad, jnp.zeros((1, model_width), jnp.bfloat16)], 0)
    grad_send = (padded_grad[token_of].astype(jnp.float32) * weight_of[:, None]).astype(
        jnp.bfloat16
    )
    grad_arrived = send_rows(grad_send.reshape(experts, capacity, model_width))
    grad_arrived = grad_arrived.reshape(groups, local_experts, capacity, model_width)
    act_grad = jnp.einsum(
        "secd,efd->secf", grad_arrived, expert_down, preferred_element_type=jnp.float32
    )
    expert_down_grad = jnp.einsum(
        "secf,secd->efd", act_low, grad_arrived, preferred_element_type=jnp.float32
    )
    gate_grad = (act_grad * up_act * silu_slope(gate_act)).astype(jnp.bfloat16)
    up_grad = (act_grad * jax.nn.silu(gate_act)).astype(jnp.bfloat16)
    expert_gate_grad = jnp.einsum(
        "secd,secf->edf", arrived, gate_grad, preferred_element_type=jnp.float32
    )
    expert_up_grad = jnp.einsum(
        "secd,secf->edf", arrived, up_grad, preferred_element_type=jnp.float32
    )
    input_rows = jnp.einsum(
        "secf,edf->secd", gate_grad, expert_gate, preferred_element_type=jnp.float32
    )
    input_rows = input_rows + jnp.einsum(
        "secf,edf->secd", up_grad, expert_up, preferred_element_type=jnp.float32
    )
    input_rows = input_rows.reshape(experts, capacity, model_width)
    shared_act_grad = mat_dot(out_grad, shared_down.T)
    shared_down_grad = mat_dot(shared_low.T, out_grad)
    shared_gate_low = (shared_act_grad * shared_up_act * silu_slope(shared_gate_act)).astype(
        jnp.bfloat16
    )
    shared_up_low = (shared_act_grad * jax.nn.silu(shared_gate_act)).astype(jnp.bfloat16)
    shared_gate_grad = mat_dot(ffn_low.T, shared_gate_low)
    shared_up_grad = mat_dot(ffn_low.T, shared_up_low)
    shared_in = mat_dot(shared_gate_low, shared_gate.T) + mat_dot(shared_up_low, shared_up.T)
    returned_grad, local_grad = bring_back(input_rows, shared_in)
    hidden_part = local_grad + jnp.sum(fetch(returned_grad, buffer_place, tok_rows, top_count), 1)
    norm_grad = lax.psum(hidden_part.astype(jnp.bfloat16), "tensor").astype(jnp.float32)
    inner_sum = jnp.sum(weight_grad * chosen, -1, keepdims=True)
    chosen_grad = route_scale * (weight_grad / chosen_sum - inner_sum / (chosen_sum * chosen_sum))
    logit_pick = chosen_grad * chosen * (1.0 - chosen)
    logit_grad = jnp.sum(pick_table * logit_pick[..., None], 1)
    router_grad = jnp.dot(
        ffn_in.T, logit_grad, precision=highest, preferred_element_type=jnp.float32
    )
    norm_grad = norm_grad + jnp.dot(
        logit_grad, router.T, precision=highest, preferred_element_type=jnp.float32
    )
    hidden_extra, norm_ffn_grad = rms_backward(hidden, inv_two, norm_ffn_gain, norm_grad)
    hidden_grad = grad_full + hidden_extra
    attn_grad_low = hidden_grad.astype(jnp.bfloat16)
    out_weight_grad = mat_dot(heads_low.T, attn_grad_low)
    heads_grad = (
        mat_dot(attn_grad_low, out_weight.T).astype(jnp.bfloat16).reshape(tok_rows, head_count, VD)
    )
    attn_probs = jnp.exp(attention_scores() - log_total)
    probs_low = attn_probs.astype(jnp.bfloat16)
    value_grad = jnp.einsum(
        "hqk,qhd->khd", probs_low, heads_grad, preferred_element_type=jnp.float32
    )
    prob_grad = jnp.einsum(
        "qhd,khd->hqk", heads_grad, expanded[..., NOPE:], preferred_element_type=jnp.float32
    )
    row_delta = jnp.sum(attn_probs * prob_grad, -1, keepdims=True)
    score_grad = (attn_probs * (prob_grad - row_delta)).astype(jnp.bfloat16)
    nope_grad = jnp.einsum(
        "hqk,khd->qhd", score_grad, expanded[..., :NOPE], preferred_element_type=jnp.float32
    )
    rope_grad = jnp.einsum(
        "hqk,kd->qhd", score_grad, keys_latent[:, R:], preferred_element_type=jnp.float32
    )
    key_nope_grad = jnp.einsum(
        "hqk,qhd->khd", score_grad, query_low[..., :NOPE], preferred_element_type=jnp.float32
    )
    key_rope_grad = jnp.einsum(
        "hqk,qhd->kd", score_grad, query_low[..., NOPE:], preferred_element_type=jnp.float32
    )
    expand_grad = (
        jnp.concatenate([key_nope_grad, value_grad], -1)
        .reshape(key_count, head_count * (NOPE + VD))
        .astype(jnp.bfloat16)
    )
    latent_up_grad = mat_dot(keys_latent[:, :R].T, expand_grad)
    latent_grad = jnp.concatenate([mat_dot(expand_grad, latent_up.T), key_rope_grad], -1)
    own_grad = latent_grad[(SEQ_DEVS - 1) * tok_rows :]
    for block_index in range(SEQ_DEVS - 1):
        piece_grad = latent_grad[block_index * tok_rows : (block_index + 1) * tok_rows]
        own_grad = own_grad + from_behind(
            piece_grad.astype(jnp.bfloat16), "dp", -(SEQ_DEVS - 1 - block_index) * stride
        ).astype(piece_grad.dtype)
    normed_part, latent_gain_grad = rms_backward(
        compressed[:, :R], inv_latent, latent_gain, own_grad[:, :R]
    )
    compressed_grad = jnp.concatenate(
        [normed_part, unrotate(own_grad[:, R:], cos_table, sin_table)], -1
    )
    query_grad = (
        jnp.concatenate(
            [nope_grad, unrotate(rope_grad, cos_table[:, None, :], sin_table[:, None, :])], -1
        )
        * factor
    )
    query_grad_low = query_grad.reshape(tok_rows, head_count * (NOPE + ROPE)).astype(jnp.bfloat16)
    query_weight_grad = mat_dot(normed_low.T, query_grad_low)
    input_part = mat_dot(query_grad_low, query_weight.T)
    input_sum, compressed_sum, latent_gain_grad = (
        lax.psum(input_part.astype(jnp.bfloat16), "tensor").astype(jnp.float32),
        lax.psum(compressed_grad.astype(jnp.bfloat16), "tensor").astype(jnp.float32),
        lax.psum(latent_gain_grad.astype(jnp.bfloat16), "tensor").astype(jnp.float32),
    )
    compressed_low = compressed_sum.astype(jnp.bfloat16)
    latent_down_grad = mat_dot(normed_low.T, compressed_low)
    normed_grad = input_sum + mat_dot(compressed_low, latent_down.T)
    input_extra, norm_attn_grad = rms_backward(residual_in, inv_one, norm_attn_gain, normed_grad)
    tokens_grad = (hidden_grad + input_extra).astype(jnp.bfloat16)
    reduced = (
        lax.psum_scatter(
            norm_attn_grad.astype(jnp.bfloat16), "dp", scatter_dimension=0, tiled=True
        ).astype(jnp.float32),
        lax.psum_scatter(
            query_weight_grad.astype(jnp.bfloat16), "dp", scatter_dimension=0, tiled=True
        ).astype(jnp.float32),
        lax.psum_scatter(
            latent_down_grad.astype(jnp.bfloat16), "dp", scatter_dimension=0, tiled=True
        ).astype(jnp.float32),
        lax.psum_scatter(
            latent_gain_grad.astype(jnp.bfloat16), "dp", scatter_dimension=0, tiled=True
        ).astype(jnp.float32),
        lax.psum_scatter(
            latent_up_grad.astype(jnp.bfloat16), "dp", scatter_dimension=0, tiled=True
        ).astype(jnp.float32),
        lax.psum_scatter(
            out_weight_grad.astype(jnp.bfloat16), "dp", scatter_dimension=1, tiled=True
        ).astype(jnp.float32),
        lax.psum_scatter(
            norm_ffn_grad.astype(jnp.bfloat16), "dp", scatter_dimension=0, tiled=True
        ).astype(jnp.float32),
        lax.psum_scatter(
            router_grad.astype(jnp.bfloat16), "dp", scatter_dimension=0, tiled=True
        ).astype(jnp.float32),
        lax.psum_scatter(
            shared_gate_grad.astype(jnp.bfloat16), "dp", scatter_dimension=0, tiled=True
        ).astype(jnp.float32),
        lax.psum_scatter(
            shared_up_grad.astype(jnp.bfloat16), "dp", scatter_dimension=0, tiled=True
        ).astype(jnp.float32),
        lax.psum_scatter(
            shared_down_grad.astype(jnp.bfloat16), "dp", scatter_dimension=1, tiled=True
        ).astype(jnp.float32),
    )
    return (
        block_out,
        tokens_grad,
        reduced[0],
        reduced[1],
        reduced[2],
        reduced[3],
        reduced[4],
        reduced[5],
        reduced[6],
        reduced[7],
        reduced[8],
        reduced[9],
        reduced[10],
        expert_gate_grad,
        expert_up_grad,
        expert_down_grad,
    )


def solution(mesh):
    in_specs = (
        P("dp", None),
        P(),
        P(None, "tensor"),
        P(),
        P(),
        P(None, "tensor"),
        P("tensor", None),
        P(),
        P(),
        P(None, "tensor"),
        P(None, "tensor"),
        P("tensor", None),
        P("dp", None, "tensor"),
        P("dp", None, "tensor"),
        P("dp", "tensor", None),
        P("dp", None),
        P("dp", None),
    )
    out_specs = (
        P("dp", None),
        P("dp", None),
        P("dp"),
        P("dp", "tensor"),
        P("dp", None),
        P("dp"),
        P("dp", "tensor"),
        P("tensor", "dp"),
        P("dp"),
        P("dp", None),
        P("dp", "tensor"),
        P("dp", "tensor"),
        P("tensor", "dp"),
        P("dp", None, "tensor"),
        P("dp", None, "tensor"),
        P("dp", "tensor", None),
    )
    return jax.shard_map(shards, mesh=mesh, in_specs=in_specs, out_specs=out_specs, check_vma=False)
```

profile of v0, /device:TPU:0, one launch (start us, length us, event | category | flops | bytes accessed | tf_op | source)
XLA Modules:
  0.0 1296.6 jit_solution(15203414017455644162)
XLA Ops:
  91.5 76.6 %all-reduce.11.cloned.1.call-done = f32[256,2048]{1,0:T(8,128)} async-done(((f32[256,2048]{1,0:T(8,128)}), f32[256,2048]{1,0:T(8,128)}) %all-reduce.11.cloned.1.call-update) | async-done | bytes 2097168 | tf_op jit(solution)/shard_map/psum | solution.py:190
  174.0 25.2 %gather_fusion = bf16[3072,2048]{1,0:T(8,128)(2,1)} fusion(bf16[257,2048]{1,0:T(8,128)(2,1)} %concatenate.36, s32[3072]{0:T(1024)S(1)} %get-tuple-element.59), kind=kCustom, calls=%fused_computation.2 | custom fusion | bytes 25178112 | tf_op jit(solution)/shard_map/gather | solution.py:216
  206.9 25.2 %gather_fusion.1 = bf16[3072,2048]{1,0:T(8,128)(2,1)} fusion(bf16[257,2048]{1,0:T(8,128)(2,1)} %concatenate.37, s32[3072]{0:T(1024)S(1)} %get-tuple-element.59), kind=kCustom, calls=%fused_computation.3 | custom fusion | bytes 25178112 | tf_op jit(solution)/shard_map/gather | solution.py:242
  236.0 17.4 %gather_fusion.2 = f32[3072]{0:T(1024)S(1)} fusion(f32[1537]{0:T(1024)S(1)} %pad_maximum_fusion.4, s32[3072]{0:T(1024)S(1)} %get-tuple-element.58), kind=kCustom, calls=%fused_computation.4 | custom fusion | bytes 36864 | tf_op jit(solution)/shard_map/gather | solution.py:214
  253.5 11.2 fusion
  264.7 78.9 %all-to-all-done = bf16[16,192,2048]{2,1,0:T(8,128)(2,1)} async-done(((bf16[16,192,2048]{2,1,0:T(8,128)(2,1)}), bf16[16,192,2048]{2,1,0:T(8,128)(2,1)}, u32[]{:S(2)}, u32[]{:S(2)}) %all-to-all-start) | async-done | bytes 12582944 | tf_op jit(solution)/shard_map/all_to_all | solution.py:83
  348.9 12.0 fusion.6
  361.0 11.2 fusion.8
  372.2 115.7 %all-to-all-done.2 = bf16[16,192,2048]{2,1,0:T(8,128)(2,1)} async-done(((bf16[16,192,2048]{2,1,0:T(8,128)(2,1)}), bf16[16,192,2048]{2,1,0:T(8,128)(2,1)}, u32[]{:S(2)}, u32[]{:S(2)}) %all-to-all-start.2) | async-done | bytes 12582944 | tf_op jit(solution)/shard_map/all_to_all | solution.py:83
  487.9 14.7 %fusion.16 = (bf16[8,2,192,352]{3,2,0,1:T(8,128)(2,1)}, bf16[8,2,192,352]{3,2,0,1:T(8,128)(2,1)S(1)}, bf16[8,2,192,352]{3,2,0,1:T(8,128)(2,1)}) fusion(f32[2,8,192,352]{3,2,1,0:T(8,128)} %fusion.8, f32[2,8,192,352]{3,2,1,0:T(8,128)} %fusion.6, bf16[2,352,2048]{2,1,0:T(8,128)(2,1)} %param.33, bf16[8,2,192,2048]{3,2,1,0:T(8,128)(2,1)} %bitcast.23), kind=kOutput, calls=%fused_computation.39 | convolution fusion | flops 4445405184 | bytes 30605312 | tf_op jit(solution)/shard_map/secd,efd->secf/dot_general | solution.py:247
  502.6 11.8 fusion.35
  514.4 15.9 %fusion.1 = bf16[8,2,192,2048]{3,2,0,1:T(8,128)(2,1)} fusion(f32[2,8,192,2048]{3,2,1,0:T(8,128)} %fusion.35, bf16[8,2,192,352]{3,2,0,1:T(8,128)(2,1)} %get-tuple-element.35, bf16[2,2048,352]{1,2,0:T(8,128)(2,1)} %param.32), kind=kOutput, calls=%fused_computation.9 | convolution fusion | flops 4441767936 | bytes 42795008 | tf_op jit(solution)/shard_map/secf,edf->secd/dot_general | solution.py:264
  530.3 10.7 copy.130
  569.3 116.1 %all-to-all-done.3 = bf16[16,192,2048]{2,1,0:T(8,128)(2,1)} async-done(((bf16[16,192,2048]{2,1,0:T(8,128)(2,1)}), bf16[16,192,2048]{2,1,0:T(8,128)(2,1)}, u32[]{:S(2)}, u32[]{:S(2)}) %all-to-all-start.3) | async-done | bytes 12582944 | tf_op jit(solution)/shard_map/all_to_all | solution.py:87
  690.8 14.6 %bitcast_convert_fusion = f32[3072,2048]{1,0:T(8,128)} fusion(bf16[16,192,2048]{2,1,0:T(8,128)(2,1)} %all-to-all-done.3), kind=kLoop, calls=%fused_computation.10 | loop fusion | flops 6291456 | bytes 37748736 | tf_op jit(solution)/shard_map/reshape | solution.py:94
  705.4 20.7 %gather_fusion.4 = f32[1536,2048]{1,0:T(8,128)} fusion(f32[3072,2048]{1,0:T(8,128)} %bitcast_convert_fusion, s32[2048]{0:T(1024)S(1)} %pad_clamp_fusion), kind=kCustom, calls=%fused_computation.1.clone | custom fusion | bytes 25171968 | tf_op jit(solution)/shard_map/jit(_take)/gather | solution.py:95
  726.2 10.0 broadcast_select_fusion
  736.2 15.0 %reshape.347 = f32[256,6,2048]{2,1,0:T(8,128)} reshape(f32[1536,2048]{1,0:T(8,128)} %broadcast_select_fusion) | data formatting | bytes 25165824 | tf_op jit(solution)/shard_map/reshape | solution.py:95
  779.1 50.6 %all-to-all-done.1 = bf16[16,192,2048]{2,1,0:T(8,128)(2,1)} async-done(((bf16[16,192,2048]{2,1,0:T(8,128)(2,1)}), bf16[16,192,2048]{2,1,0:T(8,128)(2,1)}, u32[]{:S(2)}, u32[]{:S(2)}) %all-to-all-start.1) | async-done | bytes 12582944 | tf_op jit(solution)/shard_map/all_to_all | solution.py:87
  829.8 19.9 %gather_fusion.3 = bf16[1536,2048]{1,0:T(8,128)(2,1)} fusion(bf16[3072,2048]{1,0:T(8,128)(2,1)} %bitcast.133, s32[2048]{0:T(1024)S(1)} %pad_clamp_fusion), kind=kCustom, calls=%fused_computation.clone | custom fusion | bytes 12589056 | tf_op jit(solution)/shard_map/jit(_take)/gather | solution.py:95
  856.3 11.1 reshape.343
  887.1 10.4 psum.52
  956.9 12.2 collective-permute-done.10
  999.3 10.1 convolution_bitcast_fusion
  1009.4 65.8 %all-reduce.15.cloned.1.call-done = (bf16[256,2048]{1,0:T(8,128)(2,1)}, bf16[256,576]{0,1:T(8,128)(2,1)}, bf16[256,2048]{1,0:T(8,128)(2,1)}) async-done(((bf16[256,2048]{1,0:T(8,128)(2,1)}, bf16[256,576]{0,1:T(8,128)(2,1)}, bf16[256,2048]{1,0:T(8,128)(2,1)}), (bf16[256,2048]{1,0:T(8,128)(2,1)}, bf16[256,576]{0,1:T(8,128)(2,1)}, bf16[256,2048]{1,0:T(8,128)(2,1)})) %all-reduce.15.cloned.1.call-update) | async-done | bytes 2392080 | tf_op jit(solution)/shard_map/psum | solution.py:237
  1078.9 10.1 convolution_bitcast_fusion.1
  1089.0 10.4 fusion.27
  1110.4 37.9 %reduce-scatter.13.cloned.1.call-done = bf16[64,1024]{1,0:T(8,128)(2,1)} async-done(((bf16[512,1024]{1,0:T(8,128)(2,1)}), bf16[64,1024]{1,0:T(8,128)(2,1)}) %reduce-scatter.13.cloned.1.call-update) | async-done | bytes 131088 | tf_op jit(solution)/shard_map/reduce_scatter | solution.py:370
  1154.9 12.8 all-reduce.5
  1167.8 11.7 psum.56
  1194.5 47.6 %reduce-scatter.9.cloned.1.call-done = bf16[256,768]{1,0:T(8,128)(2,1)} async-done(((bf16[2048,768]{1,0:T(8,128)(2,1)}), bf16[256,768]{1,0:T(8,128)(2,1)}) %reduce-scatter.9.cloned.1.call-update) | async-done | bytes 393232 | tf_op jit(solution)/shard_map/reduce_scatter | solution.py:361
  1244.0 43.8 %reduce-scatter.11.cloned.1.call-done = bf16[256,576]{0,1:T(8,128)(2,1)} async-done(((bf16[2048,576]{0,1:T(8,128)(2,1)}), bf16[256,576]{0,1:T(8,128)(2,1)}) %reduce-scatter.11.cloned.1.call-update) | async-done | bytes 294928 | tf_op jit(solution)/shard_map/reduce_scatter | solution.py:364
  (371 shorter events, 322.1 us)
Async XLA Ops:
  7.2 160.9 %all-reduce.11.cloned.1.call-start = ((), (), s32[]{:S(2)}) async-start(), calls=%async_computation.12 | async-start | bytes 4194304 | tf_op jit(solution)/shard_map/psum | solution.py:190
  15.0 48.5 %collective-permute-start.6 = (bf16[256,576]{0,1:T(8,128)(2,1)}, bf16[256,576]{0,1:T(8,128)(2,1)}, u32[]{:S(2)}, u32[]{:S(2)}) collective-permute-start(bf16[256,576]{0,1:T(8,128)(2,1)} %pad_maximum_fusion.2), channel_id=1, source_target_pairs={{0,4},{4,8},{8,12},{12,16},{16,20},{20,24},{24,28},{1,5},{5,9},{9,... | collective-permute-start | bytes 884744 | tf_op jit(solution)/shard_map/ppermute | solution.py:23
  18.1 44.3 %collective-permute-start.5 = (bf16[256,576]{0,1:T(8,128)(2,1)}, bf16[256,576]{0,1:T(8,128)(2,1)}, u32[]{:S(2)}, u32[]{:S(2)}) collective-permute-start(bf16[256,576]{0,1:T(8,128)(2,1)} %pad_maximum_fusion.2), channel_id=1, source_target_pairs={{0,8},{4,12},{8,16},{12,20},{16,24},{20,28},{1,9},{5,13},{9,17},{1... | collective-permute-start | bytes 884744 | tf_op jit(solution)/shard_map/ppermute | solution.py:23
  22.5 32.5 %collective-permute-start.2 = (bf16[256,576]{0,1:T(8,128)(2,1)}, bf16[256,576]{0,1:T(8,128)(2,1)}, u32[]{:S(2)}, u32[]{:S(2)}) collective-permute-start(bf16[256,576]{0,1:T(8,128)(2,1)} %pad_maximum_fusion.2), channel_id=1, source_target_pairs={{0,20},{4,24},{8,28},{1,21},{5,25},{9,29},{2,22},{6,26},{10,30},{3... | collective-permute-start | bytes 884744 | tf_op jit(solution)/shard_map/ppermute | solution.py:23
  25.6 26.9 %collective-permute-start.1 = (bf16[256,576]{0,1:T(8,128)(2,1)}, bf16[256,576]{0,1:T(8,128)(2,1)}, u32[]{:S(2)}, u32[]{:S(2)}) collective-permute-start(bf16[256,576]{0,1:T(8,128)(2,1)} %pad_maximum_fusion.2), channel_id=1, source_target_pairs={{0,24},{4,28},{1,25},{5,29},{2,26},{6,30},{3,27},{7,31}} | collective-permute-start | bytes 884744 | tf_op jit(solution)/shard_map/ppermute | solution.py:23
  27.6 22.4 %collective-permute-start = (bf16[256,576]{0,1:T(8,128)(2,1)}, bf16[256,576]{0,1:T(8,128)(2,1)}, u32[]{:S(2)}, u32[]{:S(2)}) collective-permute-start(bf16[256,576]{0,1:T(8,128)(2,1)} %pad_maximum_fusion.2), channel_id=1, source_target_pairs={{0,28},{1,29},{2,30},{3,31}} | collective-permute-start | bytes 884744 | tf_op jit(solution)/shard_map/ppermute | solution.py:23
  50.1 12.3 collective-permute-start.3
  52.5 9.9 collective-permute-start.4
  79.0 91.4 %copy-start.54 = (s32[1536]{0:T(1024)}, s32[1536]{0:T(1024)S(1)}, u32[]{:S(2)}) copy-start(s32[1536]{0:T(1024)S(1)} %eq.41) | copy-start | bytes 18436
  84.4 87.3 %copy-start.41 = (f32[2048]{0:T(1024)S(1)}, f32[2048]{0:T(1024)}, u32[]{:S(2)}) copy-start(f32[2048]{0:T(1024)} %param.26) | copy-start | bytes 24580
  84.8 87.2 %copy-start.56 = (s32[1536]{0:T(1024)}, s32[1536]{0:T(1024)S(1)}, u32[]{:S(2)}) copy-start(s32[1536]{0:T(1024)S(1)} %fusion.110) | copy-start | bytes 18436
  199.3 144.3 %all-to-all-start = ((bf16[16,192,2048]{2,1,0:T(8,128)(2,1)}), bf16[16,192,2048]{2,1,0:T(8,128)(2,1)}, u32[]{:S(2)}, u32[]{:S(2)}) async-start(bf16[16,192,2048]{2,1,0:T(8,128)(2,1)} %bitcast.199), calls=%async_computation | async-start | bytes 25165824 | tf_op jit(solution)/shard_map/all_to_all | solution.py:83
  343.6 144.3 %all-to-all-start.2 = ((bf16[16,192,2048]{2,1,0:T(8,128)(2,1)}), bf16[16,192,2048]{2,1,0:T(8,128)(2,1)}, u32[]{:S(2)}, u32[]{:S(2)}) async-start(bf16[16,192,2048]{2,1,0:T(8,128)(2,1)} %fusion), calls=%async_computation.2 | async-start | bytes 25165824 | tf_op jit(solution)/shard_map/all_to_all | solution.py:83
  541.0 144.4 %all-to-all-start.3 = ((bf16[16,192,2048]{2,1,0:T(8,128)(2,1)}), bf16[16,192,2048]{2,1,0:T(8,128)(2,1)}, u32[]{:S(2)}, u32[]{:S(2)}) async-start(bf16[16,192,2048]{2,1,0:T(8,128)(2,1)} %bitcast.198), calls=%async_computation.3 | async-start | bytes 25165824 | tf_op jit(solution)/shard_map/all_to_all | solution.py:87
  685.5 144.3 %all-to-all-start.1 = ((bf16[16,192,2048]{2,1,0:T(8,128)(2,1)}), bf16[16,192,2048]{2,1,0:T(8,128)(2,1)}, u32[]{:S(2)}, u32[]{:S(2)}) async-start(bf16[16,192,2048]{2,1,0:T(8,128)(2,1)} %bitcast.197), calls=%async_computation.1 | async-start | bytes 25165824 | tf_op jit(solution)/shard_map/all_to_all | solution.py:87
  690.8 206.8 %all-reduce.13.cloned.1.call-start = ((), (), s32[]{:S(2)}) async-start(), calls=%async_computation.13 | async-start | bytes 2097152 | tf_op jit(solution)/shard_map/psum | solution.py:279
  766.1 227.5 %reduce-scatter.19.cloned.1.call-start = ((), (), s32[]{:S(2)}) async-start(), calls=%async_computation.19 | async-start | bytes 3244032 | tf_op jit(solution)/shard_map/reduce_scatter | solution.py:382
  770.0 225.5 %reduce-scatter.21.cloned.1.call-start = ((), (), s32[]{:S(2)}) async-start(), calls=%async_computation.20 | async-start | bytes 3244032 | tf_op jit(solution)/shard_map/reduce_scatter | solution.py:385
  773.8 223.6 %reduce-scatter.23.cloned.1.call-start = ((), (), s32[]{:S(2)}) async-start(), calls=%async_computation.21 | async-start | bytes 3244032 | tf_op jit(solution)/shard_map/reduce_scatter | solution.py:388
  779.1 296.1 %all-reduce.15.cloned.1.call-start = ((), (), s32[]{:S(2)}) async-start(), calls=%async_computation.22 | async-start | bytes 4784128 | tf_op jit(solution)/shard_map/psum | solution.py:237
  927.0 13.1 %collective-permute-start.7 = (bf16[256,576]{0,1:T(8,128)(2,1)}, bf16[256,576]{0,1:T(8,128)(2,1)}, u32[]{:S(2)}, u32[]{:S(2)}) collective-permute-start(bf16[256,576]{0,1:T(8,128)(2,1)} %get-tuple-element.38), channel_id=1, source_target_pairs={{28,0},{29,1},{30,2},{31,3}} | collective-permute-start | bytes 884744 | tf_op jit(solution)/shard_map/ppermute | solution.py:23
  928.3 13.2 %collective-permute-start.13 = (bf16[256,576]{0,1:T(8,128)(2,1)}, bf16[256,576]{0,1:T(8,128)(2,1)}, u32[]{:S(2)}, u32[]{:S(2)}) collective-permute-start(bf16[256,576]{0,1:T(8,128)(2,1)} %get-tuple-element.39), channel_id=1, source_target_pairs={{4,0},{8,4},{12,8},{16,12},{20,16},{24,20},{28,24},{5,1},{9,5},{13... | collective-permute-start | bytes 884744 | tf_op jit(solution)/shard_map/ppermute | solution.py:23
  935.9 17.8 %collective-permute-start.12 = (bf16[256,576]{0,1:T(8,128)(2,1)}, bf16[256,576]{0,1:T(8,128)(2,1)S(1)}, u32[]{:S(2)}, u32[]{:S(2)}) collective-permute-start(bf16[256,576]{0,1:T(8,128)(2,1)} %get-tuple-element.40), channel_id=1, source_target_pairs={{8,0},{12,4},{16,8},{20,12},{24,16},{28,20},{9,1},{13,5},{17,9},{2... | collective-permute-start | bytes 884744 | tf_op jit(solution)/shard_map/ppermute | solution.py:23
  937.4 19.4 %collective-permute-start.11 = (bf16[256,576]{0,1:T(8,128)(2,1)}, bf16[256,576]{0,1:T(8,128)(2,1)S(1)}, u32[]{:S(2)}, u32[]{:S(2)}) collective-permute-start(bf16[256,576]{0,1:T(8,128)(2,1)} %get-tuple-element.41), channel_id=1, source_target_pairs={{12,0},{16,4},{20,8},{24,12},{28,16},{13,1},{17,5},{21,9},{25,13},... | collective-permute-start | bytes 884744 | tf_op jit(solution)/shard_map/ppermute | solution.py:23
  938.9 30.2 %collective-permute-start.10 = (bf16[256,576]{0,1:T(8,128)(2,1)}, bf16[256,576]{0,1:T(8,128)(2,1)S(1)}, u32[]{:S(2)}, u32[]{:S(2)}) collective-permute-start(bf16[256,576]{0,1:T(8,128)(2,1)} %get-tuple-element.42), channel_id=1, source_target_pairs={{16,0},{20,4},{24,8},{28,12},{17,1},{21,5},{25,9},{29,13},{18,2},{... | collective-permute-start | bytes 884744 | tf_op jit(solution)/shard_map/ppermute | solution.py:23
  940.2 29.3 %collective-permute-start.9 = (bf16[256,576]{0,1:T(8,128)(2,1)}, bf16[256,576]{0,1:T(8,128)(2,1)S(1)}, u32[]{:S(2)}, u32[]{:S(2)}) collective-permute-start(bf16[256,576]{0,1:T(8,128)(2,1)} %get-tuple-element.43), channel_id=1, source_target_pairs={{20,0},{24,4},{28,8},{21,1},{25,5},{29,9},{22,2},{26,6},{30,10},{2... | collective-permute-start | bytes 884744 | tf_op jit(solution)/shard_map/ppermute | solution.py:23
  941.5 28.0 %collective-permute-start.8 = (bf16[256,576]{0,1:T(8,128)(2,1)}, bf16[256,576]{0,1:T(8,128)(2,1)S(1)}, u32[]{:S(2)}, u32[]{:S(2)}) collective-permute-start(bf16[256,576]{0,1:T(8,128)(2,1)} %get-tuple-element.44), channel_id=1, source_target_pairs={{24,0},{28,4},{25,1},{29,5},{26,2},{30,6},{27,3},{31,7}} | collective-permute-start | bytes 884744 | tf_op jit(solution)/shard_map/ppermute | solution.py:23
  972.9 136.3 %reduce-scatter.17.cloned.1.call-start = ((), (), s32[]{:S(2)}) async-start(), calls=%async_computation.18 | async-start | bytes 73728 | tf_op jit(solution)/shard_map/reduce_scatter | solution.py:379
  976.6 171.7 %reduce-scatter.13.cloned.1.call-start = ((), (), s32[]{:S(2)}) async-start(), calls=%async_computation.16 | async-start | bytes 1179648 | tf_op jit(solution)/shard_map/reduce_scatter | solution.py:370
  982.8 209.9 %reduce-scatter.15.cloned.1.call-start = ((), (), s32[]{:S(2)}) async-start(), calls=%async_computation.17 | async-start | bytes 2359296 | tf_op jit(solution)/shard_map/reduce_scatter | solution.py:373
  986.6 255.5 %reduce-scatter.9.cloned.1.call-start = ((), (), s32[]{:S(2)}) async-start(), calls=%async_computation.14 | async-start | bytes 3538944 | tf_op jit(solution)/shard_map/reduce_scatter | solution.py:361
  990.7 297.1 %reduce-scatter.11.cloned.1.call-start = ((), (), s32[]{:S(2)}) async-start(), calls=%async_computation.15 | async-start | bytes 2654208 | tf_op jit(solution)/shard_map/reduce_scatter | solution.py:364
  (84 other events, 888.9 us)
Sparse Core Ops, SparseCore 0:
  78.8 89.2 all-reduce.10
  766.2 51.4 all-reduce.12
  821.1 43.9 reduce-scatter.18
  868.4 44.7 reduce-scatter.20
  916.4 59.9 reduce-scatter.22
  979.3 95.8 all-reduce.14
  1078.8 30.3 reduce-scatter.16
  1112.3 35.9 reduce-scatter.12
  1151.6 41.1 reduce-scatter.14
  1196.0 46.0 reduce-scatter.8
  1245.4 42.3 reduce-scatter.10
where the time goes:
time: 1300 us
  waiting for transfers between devices  681 us (52%)
  matrix products  216 us (17%)
  local copies, waits for them, and re-layouts  196 us (15%)
  other arithmetic  102 us (8%)
  starting transfers between devices  49.4 us (4%)
  blocking collectives  34.9 us (3%)
  between operations  17.1 us (1%)
    all_to_all x2, waiting for transfers between devices, send_rows(): return lax.all_to_all(buffer, 'dp', split_axis=0, concat_axis=0, tiled=True)  195 us
    all_to_all x2, waiting for transfers between devices, bring_back(): lax.all_to_all(buffer.astype(jnp.bfloat16), 'dp', split_axis=0, concat_ax...  167 us
    psum x1, waiting for transfers between devices, shards(): attn = lax.psum(mat_dot(heads_low, out_weight), 'tensor')  76.6 us
    psum x1, waiting for transfers between devices, shards(): lax.psum(routed_part.astype(jnp.bfloat16), 'tensor').astype(jnp.float32)  65.8 us
    dot_general x21, matrix products, mat_dot(): return jnp.dot(left, right, preferred_element_type=jnp.float32)  64.7 us
    reduce_scatter x1, waiting for transfers between devices, shards(): lax.psum_scatter(query_weight_grad.astype(jnp.bfloat16), 'dp', scatter_di...  47.6 us
    reduce_scatter x1, waiting for transfers between devices, shards(): lax.psum_scatter(latent_down_grad.astype(jnp.bfloat16), 'dp', scatter_dim...  43.8 us
    gather x2, local copies, waits for them, and re-layouts, fetch(): jnp.take(flat_rows, buffer_place, axis=0)  40.6 us
  transfers between devices with their start and end apart: 29, of which 16 were waited for; matrix products, arithmetic and copies ran while one was open for 31% of the time, Pallas kernels for 0%

commit v1 on v0

v1 whole, which is shorter than its diff:
```python
import jax
import jax.numpy as jnp
from jax import lax
from jax.experimental import pallas as pl
from jax.experimental.pallas import tpu as pltpu
from jax.sharding import PartitionSpec as P

NOPE = 128
ROPE = 64
VD = 128
R = 512
SEQ_DEVS = 8


eps = 1e-06
route_scale = 2.446
rope_base = 50000.0
masked_score = -1e30
highest = lax.Precision.HIGHEST
BOTH = ("dp", "tensor")


def from_behind(value, axis, steps):
    count = lax.axis_size(axis)
    initial, last = (max(0, -steps), min(count, count - steps))
    return lax.ppermute(value, axis, [(source, source + steps) for source in range(initial, last)])


def mat_dot(left, right):
    return jnp.dot(left, right, preferred_element_type=jnp.float32)


def contract_rows(left, right):
    return lax.dot_general(left, right, (((0,), (0,)), ((), ())), preferred_element_type=jnp.float32)


def contract_cols(left, right):
    return lax.dot_general(left, right, (((1,), (1,)), ((), ())), preferred_element_type=jnp.float32)


def rotation(positions):
    half_width = ROPE // 2
    frequency = rope_base ** (-jnp.arange(half_width, dtype=jnp.float32) / half_width)
    angles = positions.astype(jnp.float32)[:, None] * frequency[None, :]
    return (jnp.cos(angles), jnp.sin(angles))


def rotate(values, cos_table, sin_table):
    half_width = values.shape[-1] // 2
    first_half = values[..., :half_width]
    second_half = values[..., half_width:]
    return jnp.concatenate(
        [
            first_half * cos_table - second_half * sin_table,
            second_half * cos_table + first_half * sin_table,
        ],
        -1,
    )


def unrotate(upstream, cos_table, sin_table):
    return rotate(upstream, cos_table, -sin_table)


def rms_forward(values, gain_vec):
    inv_rms = lax.rsqrt(jnp.mean(values * values, axis=-1, keepdims=True) + eps)
    return (values * inv_rms * gain_vec, inv_rms)


def rms_backward(values, inv_rms, gain_vec, upstream):
    scaled = upstream * gain_vec
    inner_mean = jnp.mean(values * scaled, axis=-1, keepdims=True)
    return (
        inv_rms * scaled - values * inv_rms**3 * inner_mean,
        jnp.sum(upstream * values * inv_rms, axis=0),
    )


def low(value):
    return value.astype(jnp.bfloat16)


def gather(value, axes):
    return lax.all_gather(value, axes, tiled=True)


def scatter(value, axes, dimension=0):
    return lax.psum_scatter(
        low(value), axes, scatter_dimension=dimension, tiled=True
    ).astype(jnp.float32)


MESH = pl.DeviceIdType.MESH
PLANE = 8
DEPTH = 4


class Place:
    def __init__(self):
        self.me = lax.axis_index("dp")
        self.z = lax.axis_index("tensor")
        self.core = self.me % 2
        self.chip = self.me // 2
        self.chip_x = self.chip + 1 - 2 * (self.chip % 2)
        self.chip_y = (self.chip + 2) % 4
        self.chip_xy = 3 - self.chip
        self.sibling = self.me + 1 - 2 * self.core
        self.near_x = 2 * self.chip_x + self.core
        self.near_y = 2 * self.chip_y + self.core
        self.across = 2 * self.chip_xy + self.core
        self.levels = [self.z + 1 - 2 * (self.z % 2), (self.z + 2) % 4, 3 - self.z]


def push(src, dst, sems, index, **target):
    send, recv = sems
    return pltpu.make_async_remote_copy(
        src_ref=src,
        dst_ref=dst,
        send_sem=send.at[index],
        recv_sem=recv.at[index],
        device_id=target,
        device_id_type=MESH,
    )


def add_rows(target, sources):
    rows = target.shape[0]
    step = 16

    def one(k, carry):
        at = pl.ds(pl.multiple_of(k * step, step), step)
        acc = sources[0][at, :].astype(jnp.float32)
        for source in sources[1:]:
            acc = acc + source[at, :].astype(jnp.float32)
        target[at, :] = acc.astype(target.dtype)
        return carry

    lax.fori_loop(0, rows // step, one, 0)


def sem_pair(count):
    return [pltpu.SemaphoreType.DMA((count,)), pltpu.SemaphoreType.DMA((count,))]


class GatherPlane:
    def __init__(self, value, with_z):
        self.with_z = with_z
        self.inputs = [value]
        self.units = DEPTH if with_z else value.shape[0]
        rows, width = value.shape[-2:]
        self.in_specs = [pl.BlockSpec(memory_space=pltpu.VMEM)]
        self.outputs = [
            jax.ShapeDtypeStruct((PLANE, self.units, rows, width), value.dtype)
        ]
        self.out_specs = [pl.BlockSpec(memory_space=pl.ANY)]
        self.scratch = (
            sem_pair(7 * self.units)
            + sem_pair(DEPTH - 1)
            + [pltpu.SemaphoreType.DMA((1,))]
        )

    def steps(self, place, inputs, outputs, scratch):
        (x,), (out,) = inputs, outputs
        sems, z_sems, local = scratch[0:2], scratch[2:4], scratch[4]
        me, units = place.me, self.units
        sends = []
        if self.with_z:
            order = [place.z] + place.levels
            keep = pltpu.make_async_copy(x, out.at[me, place.z], local.at[0])
            arrivals = []
            for k, level in enumerate(place.levels):
                copy = push(x, out.at[me, place.z], z_sems, k, tensor=level)
                copy.start()
                sends.append(copy)
                here = out.at[me, level]
                arrivals.append(push(here, here, z_sems, k, tensor=level))
        else:
            order = list(range(units))
            keep = pltpu.make_async_copy(x, out.at[me], local.at[0])
        keep.start()

        def message(p, kind, slot, target, src=None):
            spot = out.at[slot, order[p]]
            return push(spot if src is None else src, spot, sems, 7 * p + kind, dp=target)

        def launch(*args, **kwargs):
            copy = message(*args, **kwargs)
            copy.start()
            sends.append(copy)

        def stage_own(p):
            if self.with_z:
                src = x if p == 0 else None
                if p > 0:
                    arrivals[p - 1].wait_recv()
            else:
                src = x.at[p]
            pair = [(0, place.near_x), (1, place.near_y)]
            for kind, target in pair if p % 2 == 0 else pair[::-1]:
                launch(p, kind, me, target, src)
            launch(p, 3, me, place.sibling, src)

        def stage_near(p):
            def from_x():
                message(p, 0, place.near_x, place.near_x).wait_recv()
                if p % 2 == 0:
                    launch(p, 2, place.near_x, place.near_y)
                launch(p, 4, place.near_x, place.sibling)

            def from_y():
                message(p, 1, place.near_y, place.near_y).wait_recv()
                if p % 2 == 1:
                    launch(p, 2, place.near_y, place.near_x)
                launch(p, 5, place.near_y, place.sibling)

            for part in (from_x, from_y) if p % 2 == 0 else (from_y, from_x):
                part()

        def stage_across(p):
            message(p, 2, place.across, place.near_x).wait_recv()
            launch(p, 6, place.across, place.sibling)

        for p in range(units + 2):
            if p < units:
                stage_own(p)
            yield
            if 0 <= p - 1 < units:
                stage_near(p - 1)
            if 0 <= p - 2 < units:
                stage_across(p - 2)
            yield
        keep.wait()
        base = place.sibling
        for p in range(units):
            for kind, chip in (
                (3, place.chip),
                (4, place.chip_x),
                (5, place.chip_y),
                (6, place.chip_xy),
            ):
                message(p, kind, 2 * chip + 1 - place.core, base).wait_recv()
        for copy in sends:
            copy.wait_send()


class ScatterPlane:
    def __init__(self, value, with_z, spread=False):
        self.with_z, self.spread = with_z, spread
        _, self.units, rows, width = value.shape
        self.inputs = [value.reshape(4, 2, self.units, rows, width)]
        self.in_specs = [pl.BlockSpec(memory_space=pltpu.VMEM)]
        units = self.units
        shape = (rows, width) if with_z else (units, rows, width)
        kind = jnp.float32
        if spread:
            shape, kind = (DEPTH, rows, width), jnp.bfloat16
        self.outputs = [jax.ShapeDtypeStruct(shape, kind)]
        self.out_specs = [pl.BlockSpec(memory_space=pltpu.VMEM)]
        buffer = pltpu.VMEM((units, rows, width), value.dtype)
        self.scratch = (
            sem_pair(4 * units)
            + [pltpu.VMEM((units, 4, rows, width), value.dtype)]
            + [buffer] * 6
        )
        if with_z:
            level = pltpu.VMEM((DEPTH - 1, rows, width), value.dtype)
            self.scratch += sem_pair(DEPTH - 1) + [level] * 2
        if spread:
            self.scratch += sem_pair(DEPTH - 1) + [pltpu.VMEM((rows, width), value.dtype)]

    def steps(self, place, inputs, outputs, scratch):
        (part,), (out,) = inputs, outputs
        sems, beside = scratch[0:2], scratch[2]
        d_send, d_recv, x_send, x_recv, y_send, y_recv = scratch[3:9]
        units, core = self.units, place.core
        if self.with_z:
            z_sems, z_send, z_recv = scratch[9:11], scratch[11], scratch[12]
            near, far, other = place.levels
            order = [far, other, near, place.z]
        else:
            order = list(range(units))
        sends = []

        def launch(copy):
            copy.start()
            sends.append(copy)

        def across(p):
            target = place.near_x if p % 2 == 0 else place.near_y
            return push(d_send.at[p], d_recv.at[p], sems, 4 * p + 1, dp=target)

        def to_x(p):
            return push(x_send.at[p], x_recv.at[p], sems, 4 * p + 2, dp=place.near_x)

        def to_y(p):
            return push(y_send.at[p], y_recv.at[p], sems, 4 * p + 3, dp=place.near_y)

        def to_sibling(p):
            return push(
                part.at[:, 1 - core, order[p]],
                beside.at[p],
                sems,
                4 * p,
                dp=place.sibling,
            )

        def both(p, chip):
            return [part.at[chip, core, order[p]], beside.at[p, chip]]

        for p in range(units):
            launch(to_sibling(p))

        def stage_one(p):
            to_sibling(p).wait_recv()
            add_rows(d_send.at[p], both(p, place.chip_xy))
            launch(across(p))
            if p % 2 == 0:
                add_rows(x_send.at[p], both(p, place.chip_x))
                launch(to_x(p))
            else:
                add_rows(y_send.at[p], both(p, place.chip_y))
                launch(to_y(p))

        def stage_two(p):
            across(p).wait_recv()
            if p % 2 == 0:
                add_rows(y_send.at[p], both(p, place.chip_y) + [d_recv.at[p]])
                launch(to_y(p))
            else:
                add_rows(x_send.at[p], both(p, place.chip_x) + [d_recv.at[p]])
                launch(to_x(p))

        def to_level(p):
            return push(z_send.at[p], z_recv.at[p], z_sems, p, tensor=order[p])

        def stage_three(p):
            to_x(p).wait_recv()
            to_y(p).wait_recv()
            pieces = both(p, place.chip) + [x_recv.at[p], y_recv.at[p]]
            if not self.with_z:
                add_rows(out.at[p], pieces)
            elif p < units - 1:
                add_rows(z_send.at[p], pieces)
                launch(to_level(p))
            else:
                for k in range(DEPTH - 1):
                    to_level(k).wait_recv()
                pieces += [z_recv.at[k] for k in range(DEPTH - 1)]
                add_rows(scratch[15] if self.spread else out, pieces)

        for p in range(units + 2):
            if p < units:
                stage_one(p)
            yield
            if 0 <= p - 1 < units:
                stage_two(p - 1)
            if 0 <= p - 2 < units:
                stage_three(p - 2)
            yield
        if self.spread:
            yield from spread_levels(place, scratch[15], out, scratch[13:15], sends)
        for copy in sends:
            copy.wait_send()


def spread_levels(place, own, out, z_sems, sends):
    arrivals = []
    for k, level in enumerate(place.levels):
        copy = push(own, out.at[place.z], z_sems, k, tensor=level)
        copy.start()
        sends.append(copy)
        arrivals.append(push(own, out.at[level], z_sems, k, tensor=level))
    out[place.z] = own[...]
    yield
    for copy in arrivals:
        copy.wait_recv()


class GatherLevels:
    def __init__(self, value):
        self.inputs = [value]
        self.in_specs = [pl.BlockSpec(memory_space=pltpu.VMEM)]
        self.outputs = [jax.ShapeDtypeStruct((DEPTH,) + value.shape, value.dtype)]
        self.out_specs = [pl.BlockSpec(memory_space=pltpu.VMEM)]
        self.scratch = sem_pair(DEPTH - 1)

    def steps(self, place, inputs, outputs, scratch):
        sends = []
        yield from spread_levels(place, inputs[0], outputs[0], scratch[0:2], sends)
        for copy in sends:
            copy.wait_send()


class ScatterLevels:
    def __init__(self, value):
        _, rows, width = value.shape
        self.inputs = [value]
        self.in_specs = [pl.BlockSpec(memory_space=pltpu.VMEM)]
        self.outputs = [jax.ShapeDtypeStruct((rows, width), jnp.float32)]
        self.out_specs = [pl.BlockSpec(memory_space=pltpu.VMEM)]
        self.scratch = sem_pair(DEPTH - 1) + [pltpu.VMEM((DEPTH - 1, rows, width), value.dtype)]

    def steps(self, place, inputs, outputs, scratch):
        part, z_sems, landed = inputs[0], scratch[0:2], scratch[2]
        copies = [
            push(part.at[level], landed.at[k], z_sems, k, tensor=level)
            for k, level in enumerate(place.levels)
        ]
        for copy in copies:
            copy.start()
        yield
        yield
        yield
        for copy in copies:
            copy.wait_recv()
        add_rows(outputs[0], [part.at[place.z]] + [landed.at[k] for k in range(DEPTH - 1)])
        for copy in copies:
            copy.wait_send()


def exchange(tasks, collective_id, name):
    def kernel(*refs):
        place = Place()
        barrier = pltpu.get_barrier_semaphore()
        for target in (place.sibling, place.near_x, place.near_y):
            pl.semaphore_signal(
                barrier, inc=1, device_id={"dp": target}, device_id_type=MESH
            )
        for target in place.levels:
            pl.semaphore_signal(
                barrier, inc=1, device_id={"tensor": target}, device_id_type=MESH
            )
        pl.semaphore_wait(barrier, 6)
        refs = list(refs)

        def take(counts):
            return [[refs.pop(0) for _ in range(count)] for count in counts]

        inputs = take([len(task.inputs) for task in tasks])
        outputs = take([len(task.outputs) for task in tasks])
        scratch = take([len(task.scratch) for task in tasks])
        running = [
            task.steps(place, a, b, c)
            for task, a, b, c in zip(tasks, inputs, outputs, scratch)
        ]
        while running:
            for walk in list(running):
                if next(walk, running) is running:
                    running.remove(walk)

    def flat(pieces):
        return [one for piece in pieces for one in piece]

    moved = sum(one.size * one.dtype.itemsize for task in tasks for one in task.inputs)
    return pl.pallas_call(
        kernel,
        name=name,
        out_shape=flat(task.outputs for task in tasks),
        in_specs=flat(task.in_specs for task in tasks),
        out_specs=flat(task.out_specs for task in tasks),
        scratch_shapes=flat(task.scratch for task in tasks),
        compiler_params=pltpu.CompilerParams(
            collective_id=collective_id, has_side_effects=True, vmem_limit_bytes=56 << 20
        ),
        cost_estimate=pl.CostEstimate(flops=0, bytes_accessed=4 * moved, transcendentals=0),
    )(*flat(task.inputs for task in tasks))


def shards(
    tokens,
    norm_attn_gain,
    query_weight,
    latent_down,
    latent_gain,
    latent_up,
    out_weight,
    norm_ffn_gain,
    router_weight,
    shared_gate,
    shared_up,
    shared_down,
    expert_gate,
    expert_up,
    expert_down,
    expert_ids,
    out_grad,
):
    tok_rows, model_width = tokens.shape
    head_count = out_weight.shape[0] // VD
    groups = lax.axis_size("dp")
    parts = lax.axis_size("tensor")
    my_group = lax.axis_index("dp")
    my_part = lax.axis_index("tensor")
    stride = groups // SEQ_DEVS
    local_experts, _, units = expert_gate.shape
    experts = local_experts * groups
    rows = tok_rows // parts
    shared_units = shared_gate.shape[1] // groups
    used_units = local_experts * units + shared_units
    spare_units = -used_units % 128
    seq_stretch = my_group // stride
    direct = groups == PLANE and parts == DEPTH

    grad_all = gather(out_grad, "dp")

    residual_in = tokens.astype(jnp.float32)
    normed_in, inv_one = rms_forward(residual_in, norm_attn_gain)
    normed_low = low(normed_in)
    query_pos = seq_stretch * tok_rows + jnp.arange(tok_rows)
    cos_table, sin_table = rotation(query_pos)
    factor = (NOPE + ROPE) ** (-0.5)
    compressed = mat_dot(normed_low, latent_down)
    latent_normed, inv_latent = rms_forward(compressed[:, :R], latent_gain)
    key_rope = rotate(compressed[:, R:], cos_table, sin_table)
    own_latent = low(jnp.concatenate([latent_normed, key_rope], -1))
    if direct:
        halves = own_latent.reshape(2, tok_rows // 2, R + ROPE)
        (keys_latent,) = exchange([GatherPlane(halves, False)], 0, "gather_keys")
        keys_latent = keys_latent.reshape(groups * tok_rows, R + ROPE)
        key_pos = jnp.arange(keys_latent.shape[0])
    elif stride == 1:
        keys_latent = gather(own_latent, "dp")
        key_pos = jnp.arange(keys_latent.shape[0])
    else:
        earlier = [
            from_behind(own_latent, "dp", (SEQ_DEVS - 1 - block_index) * stride)
            for block_index in range(SEQ_DEVS - 1)
        ]
        keys_latent = jnp.concatenate(earlier + [own_latent], 0)
        key_pos = (seq_stretch - (SEQ_DEVS - 1)) * tok_rows + jnp.arange(keys_latent.shape[0])
    key_count = keys_latent.shape[0]
    query = mat_dot(normed_low, query_weight).reshape(tok_rows, head_count, NOPE + ROPE)
    query = (
        jnp.concatenate(
            [
                query[..., :NOPE],
                rotate(query[..., NOPE:], cos_table[:, None, :], sin_table[:, None, :]),
            ],
            -1,
        )
        * factor
    )
    query_low = low(query)
    expanded = low(mat_dot(keys_latent[:, :R], latent_up)).reshape(
        key_count, head_count, NOPE + VD
    )
    visible = (key_pos[None, :] >= 0) & (key_pos[None, :] <= query_pos[:, None])

    def attention_scores():
        raw_scores = jnp.einsum(
            "qhd,khd->hqk",
            query_low[..., :NOPE],
            expanded[..., :NOPE],
            preferred_element_type=jnp.float32,
        )
        raw_scores = raw_scores + jnp.einsum(
            "qhd,kd->hqk",
            query_low[..., NOPE:],
            keys_latent[:, R:],
            preferred_element_type=jnp.float32,
        )
        return jnp.where(visible[None], raw_scores, masked_score)

    scores = attention_scores()
    top_score = jnp.max(scores, -1, keepdims=True)
    exp_scores = jnp.exp(scores - top_score)
    exp_total = jnp.sum(exp_scores, -1, keepdims=True)
    log_total = top_score + jnp.log(exp_total)
    probs_low = low(exp_scores / exp_total)
    heads_out = jnp.einsum(
        "hqk,khd->qhd", probs_low, expanded[..., NOPE:], preferred_element_type=jnp.float32
    )
    heads_low = low(heads_out.reshape(tok_rows, head_count * VD))
    attn = mat_dot(heads_low, out_weight)
    if direct:
        (attn,) = exchange(
            [ScatterLevels(low(attn).reshape(parts, rows, model_width))], 1, "scatter_attn"
        )
    else:
        attn = scatter(attn, "tensor")

    def own_rows(value):
        return lax.dynamic_slice_in_dim(value, my_part * rows, rows, 0)

    hidden = own_rows(residual_in) + attn
    ffn_in, inv_two = rms_forward(hidden, norm_ffn_gain)
    ffn_low = low(ffn_in)
    router = router_weight.astype(jnp.float32)
    router_gates = jax.nn.sigmoid(
        jnp.dot(ffn_in, router, precision=highest, preferred_element_type=jnp.float32)
    )
    picked = jnp.any(
        own_rows(expert_ids)[..., None] == jnp.arange(experts)[None, None, :], 1
    ).astype(jnp.float32)
    chosen = picked * router_gates
    chosen_sum = jnp.sum(chosen, -1, keepdims=True)
    route = route_scale * chosen / chosen_sum
    route_high = low(route)
    route_rest = low(route - route_high.astype(jnp.float32))
    routes = jnp.concatenate([route_high, route_rest], 1)
    if direct:
        routes = jnp.pad(routes, ((0, 0), (0, 128 - 2 * experts)))
        ffn_all, routes = exchange(
            [GatherPlane(ffn_low, True), GatherPlane(routes, True)], 2, "gather_ffn"
        )
        ffn_all = ffn_all.reshape(-1, model_width)
        routes = routes.reshape(-1, 128)
    else:
        ffn_all = gather(jnp.concatenate([ffn_low, routes], 1), BOTH)
        routes = ffn_all[:, model_width:]
        ffn_all = ffn_all[:, :model_width]
    route_all = routes[:, :experts].astype(jnp.float32) + routes[
        :, experts : 2 * experts
    ].astype(jnp.float32)
    token_count = ffn_all.shape[0]
    route_own = lax.dynamic_slice_in_dim(route_all, my_group * local_experts, local_experts, 1)

    def joined(expert_weight, shared_weight):
        own = lax.dynamic_slice_in_dim(shared_weight, my_group * shared_units, shared_units, 1)
        pieces = [expert_weight[e] for e in range(local_experts)]
        return jnp.concatenate(
            pieces + [own, jnp.zeros((model_width, spare_units), jnp.bfloat16)], 1
        )

    gate_weight = joined(expert_gate, shared_gate)
    up_weight = joined(expert_up, shared_up)
    down_weight = jnp.concatenate(
        [expert_down[e] for e in range(local_experts)]
        + [
            lax.dynamic_slice_in_dim(shared_down, my_group * shared_units, shared_units, 0),
            jnp.zeros((spare_units, model_width), jnp.bfloat16),
        ],
        0,
    )
    scale = jnp.concatenate(
        [
            jnp.broadcast_to(route_own[:, e : e + 1], (token_count, units))
            for e in range(local_experts)
        ]
        + [jnp.ones((token_count, shared_units + spare_units), jnp.float32)],
        1,
    )
    plain_grad = contract_cols(grad_all, down_weight)
    gate_act = mat_dot(ffn_all, gate_weight)
    up_act = mat_dot(ffn_all, up_weight)
    logistic = jax.nn.sigmoid(gate_act)
    silu = gate_act * logistic
    act = silu * up_act
    act_low = low(act * scale)
    act_grad = plain_grad * scale
    gate_grad = low(act_grad * up_act * logistic * (1.0 + gate_act * (1.0 - logistic)))
    up_grad = low(act_grad * silu)
    weight_dots = act * plain_grad
    weight_grad = jnp.stack(
        [
            jnp.sum(weight_dots[:, e * units : (e + 1) * units], 1)
            for e in range(local_experts)
        ],
        1,
    )
    weight_grad = lax.dynamic_update_slice_in_dim(
        jnp.zeros((token_count, experts), jnp.bfloat16),
        low(weight_grad),
        my_group * local_experts,
        1,
    )
    ffn_grad = contract_cols(gate_grad, gate_weight) + contract_cols(up_grad, up_weight)
    if direct:
        weight_grad = jnp.pad(weight_grad, ((0, 0), (0, 128 - experts)))
        ffn_grad, weight_grad = exchange(
            [
                ScatterPlane(low(ffn_grad).reshape(groups, parts, rows, model_width), True),
                ScatterPlane(weight_grad.reshape(groups, parts, rows, 128), True),
            ],
            3,
            "scatter_ffn",
        )
        weight_grad = weight_grad[:, :experts]
    else:
        ffn_grad = scatter(jnp.concatenate([low(ffn_grad), weight_grad], 1), BOTH)
        weight_grad = ffn_grad[:, model_width:]
        ffn_grad = ffn_grad[:, :model_width]
    moe_out = scatter(scatter(mat_dot(act_low, down_weight), "dp"), "tensor")
    block_out = gather(low(hidden + moe_out), "tensor")

    down_grad = contract_rows(act_low, grad_all)
    gate_weight_grad = contract_rows(ffn_all, gate_grad)
    up_weight_grad = contract_rows(ffn_all, up_grad)
    expert_down_grad = down_grad[: local_experts * units].reshape(local_experts, units, -1)
    expert_gate_grad = jnp.stack(
        [gate_weight_grad[:, e * units : (e + 1) * units] for e in range(local_experts)]
    )
    expert_up_grad = jnp.stack(
        [up_weight_grad[:, e * units : (e + 1) * units] for e in range(local_experts)]
    )

    def swap(value):
        return lax.all_to_all(low(value), "dp", split_axis=0, concat_axis=1, tiled=True).astype(
            jnp.float32
        )

    first = local_experts * units
    shared_gate_grad = swap(gate_weight_grad[:, first:used_units])
    shared_up_grad = swap(up_weight_grad[:, first:used_units])
    shared_down_grad = lax.all_to_all(
        low(down_grad[first:used_units]), "dp", split_axis=1, concat_axis=0, tiled=True
    ).astype(jnp.float32)

    inner_sum = jnp.sum(weight_grad * chosen, -1, keepdims=True)
    chosen_grad = route_scale * (weight_grad / chosen_sum - inner_sum / (chosen_sum * chosen_sum))
    logit_grad = chosen_grad * chosen * (1.0 - chosen)
    router_grad = jnp.dot(
        ffn_in.T, logit_grad, precision=highest, preferred_element_type=jnp.float32
    )
    norm_grad = ffn_grad + jnp.dot(
        logit_grad, router.T, precision=highest, preferred_element_type=jnp.float32
    )
    hidden_extra, norm_ffn_grad = rms_backward(hidden, inv_two, norm_ffn_gain, norm_grad)
    hidden_grad = own_rows(out_grad).astype(jnp.float32) + hidden_extra
    if direct:
        (attn_grad_low,) = exchange([GatherLevels(low(hidden_grad))], 4, "gather_hidden")
        attn_grad_low = attn_grad_low.reshape(tok_rows, model_width)
    else:
        attn_grad_low = gather(low(hidden_grad), "tensor")

    out_weight_grad = scatter(contract_rows(heads_low, attn_grad_low), "dp", 1)
    heads_grad = low(contract_cols(attn_grad_low, out_weight)).reshape(tok_rows, head_count, VD)
    attn_probs = jnp.exp(attention_scores() - log_total)
    probs_low = low(attn_probs)
    value_grad = jnp.einsum(
        "hqk,qhd->khd", probs_low, heads_grad, preferred_element_type=jnp.float32
    )
    prob_grad = jnp.einsum(
        "qhd,khd->hqk", heads_grad, expanded[..., NOPE:], preferred_element_type=jnp.float32
    )
    row_delta = jnp.sum(attn_probs * prob_grad, -1, keepdims=True)
    score_grad = low(attn_probs * (prob_grad - row_delta))
    nope_grad = jnp.einsum(
        "hqk,khd->qhd", score_grad, expanded[..., :NOPE], preferred_element_type=jnp.float32
    )
    rope_grad = jnp.einsum(
        "hqk,kd->qhd", score_grad, keys_latent[:, R:], preferred_element_type=jnp.float32
    )
    key_nope_grad = jnp.einsum(
        "hqk,qhd->khd", score_grad, query_low[..., :NOPE], preferred_element_type=jnp.float32
    )
    key_rope_grad = jnp.einsum(
        "hqk,qhd->kd", score_grad, query_low[..., NOPE:], preferred_element_type=jnp.float32
    )
    expand_grad = low(
        jnp.concatenate([key_nope_grad, value_grad], -1).reshape(
            key_count, head_count * (NOPE + VD)
        )
    )
    latent_up_grad = contract_rows(keys_latent[:, :R], expand_grad)
    latent_grad = jnp.concatenate([contract_cols(expand_grad, latent_up), key_rope_grad], -1)
    query_grad = (
        jnp.concatenate(
            [nope_grad, unrotate(rope_grad, cos_table[:, None, :], sin_table[:, None, :])], -1
        )
        * factor
    )
    query_grad_low = low(query_grad.reshape(tok_rows, head_count * (NOPE + ROPE)))
    query_weight_grad = contract_rows(normed_low, query_grad_low)
    input_part = contract_cols(query_grad_low, query_weight)
    if direct:
        own_grad, input_sum, query_weight_grad, latent_up_grad = exchange(
            [
                ScatterPlane(low(latent_grad).reshape(groups, parts, rows, R + ROPE), True),
                ScatterLevels(low(input_part).reshape(parts, rows, model_width)),
                ScatterPlane(low(query_weight_grad).reshape(groups, 2, model_width // 16, -1), False),
                ScatterPlane(low(latent_up_grad).reshape(groups, 2, R // 16, -1), False),
            ],
            5,
            "scatter_latent",
        )
        query_weight_grad = query_weight_grad.reshape(model_width // groups, -1)
        latent_up_grad = latent_up_grad.reshape(R // groups, -1)
    else:
        if stride == 1:
            own_grad = scatter(scatter(latent_grad, "dp"), "tensor")
        else:
            own_grad = latent_grad[(SEQ_DEVS - 1) * tok_rows :]
            for block_index in range(SEQ_DEVS - 1):
                piece_grad = latent_grad[block_index * tok_rows : (block_index + 1) * tok_rows]
                own_grad = own_grad + from_behind(
                    low(piece_grad), "dp", -(SEQ_DEVS - 1 - block_index) * stride
                ).astype(piece_grad.dtype)
            own_grad = scatter(own_grad, "tensor")
        input_sum = scatter(input_part, "tensor")
        query_weight_grad = scatter(query_weight_grad, "dp")
        latent_up_grad = scatter(latent_up_grad, "dp")
    compressed_own = own_rows(compressed)
    normed_part, latent_gain_grad = rms_backward(
        compressed_own[:, :R], own_rows(inv_latent), latent_gain, own_grad[:, :R]
    )
    compressed_grad = low(
        jnp.concatenate(
            [normed_part, unrotate(own_grad[:, R:], own_rows(cos_table), own_rows(sin_table))], -1
        )
    )
    latent_down_grad = contract_rows(own_rows(normed_low), compressed_grad)
    normed_grad = input_sum + contract_cols(compressed_grad, latent_down)
    input_extra, norm_attn_grad = rms_backward(
        own_rows(residual_in), own_rows(inv_one), norm_attn_gain, normed_grad
    )
    tokens_grad = low(hidden_grad + input_extra)
    small = [norm_attn_grad, latent_gain_grad, norm_ffn_grad, router_grad]
    sizes = [one.size // groups for one in small]
    small = jnp.concatenate([one.reshape(groups, -1) for one in small], 1)
    if direct:
        small = jnp.pad(low(small), ((0, 0), (0, parts * 2048 - small.shape[1])))
        latent_down_grad, small, tokens_grad = exchange(
            [
                ScatterPlane(
                    low(latent_down_grad).reshape(groups, parts, rows, R + ROPE), True, True
                ),
                ScatterPlane(small.reshape(groups, parts, 16, 128), True, True),
                GatherLevels(tokens_grad),
            ],
            6,
            "scatter_last",
        )
        latent_down_grad = latent_down_grad.reshape(-1, R + ROPE).astype(jnp.float32)
        small = small.reshape(-1).astype(jnp.float32)
        tokens_grad = tokens_grad.reshape(tok_rows, model_width)
    else:
        latent_down_grad = lax.psum(scatter(latent_down_grad, "dp"), "tensor")
        small = lax.psum(scatter(small, "dp"), "tensor").reshape(-1)
        tokens_grad = gather(tokens_grad, "tensor")
    offsets = [sum(sizes[:k]) for k in range(len(sizes))]
    norm_attn_grad, latent_gain_grad, norm_ffn_grad, router_grad = [
        small[start : start + size] for start, size in zip(offsets, sizes)
    ]

    return (
        block_out,
        tokens_grad,
        norm_attn_grad,
        query_weight_grad,
        latent_down_grad,
        latent_gain_grad,
        latent_up_grad,
        out_weight_grad,
        norm_ffn_grad,
        router_grad.reshape(-1, experts),
        shared_gate_grad,
        shared_up_grad,
        shared_down_grad,
        expert_gate_grad,
        expert_up_grad,
        expert_down_grad,
    )


def solution(mesh):
    in_specs = (
        P("dp", None),
        P(),
        P(None, "tensor"),
        P(),
        P(),
        P(None, "tensor"),
        P("tensor", None),
        P(),
        P(),
        P(None, "tensor"),
        P(None, "tensor"),
        P("tensor", None),
        P("dp", None, "tensor"),
        P("dp", None, "tensor"),
        P("dp", "tensor", None),
        P("dp", None),
        P("dp", None),
    )
    out_specs = (
        P("dp", None),
        P("dp", None),
        P("dp"),
        P("dp", "tensor"),
        P("dp", None),
        P("dp"),
        P("dp", "tensor"),
        P("tensor", "dp"),
        P("dp"),
        P("dp", None),
        P("dp", "tensor"),
        P("dp", "tensor"),
        P("tensor", "dp"),
        P("dp", None, "tensor"),
        P("dp", None, "tensor"),
        P("dp", "tensor", None),
    )
    return jax.shard_map(shards, mesh=mesh, in_specs=in_specs, out_specs=out_specs, check_vma=False)
```

time: 1300 us -> 735 us (0.57)
  waiting for transfers between devices: 681 us -> 2.78 us
  Pallas kernels: 0 us -> 319 us
  local copies, waits for them, and re-layouts: 196 us -> 116 us
  other arithmetic: 102 us -> 64 us
  starting transfers between devices: 49.4 us -> 12.4 us
  blocking collectives: 34.9 us -> 0 us
  matrix products: 216 us -> 194 us
    all_to_all x4 -> x3, waiting for transfers between devices: 361 us -> 2 us  [the longest x2 2 us: swap(): lax.all_to_all(low(value), 'dp', split_axis=0, concat_axis=1, tiled=True)]
    pallas_call x0 -> x7, Pallas kernels: none -> 319 us  [exchange(): pl.pallas_call(kernel, name=name, out_shape=flat((task.outputs for task i...]
    reduce_scatter x8 -> x3, waiting for transfers between devices: 146 us -> 0.01 us  [scatter(): lax.psum_scatter(low(value), axes, scatter_dimension=dimension, tiled=True)]
    psum x3 -> x0, waiting for transfers between devices: 142 us -> none  [the longest x1 76.6 us: shards(): attn = lax.psum(mat_dot(heads_low, out_weight), 'tensor')]
    gather x5 -> x0, local copies, waits for them, and re-layouts: 108 us -> none  [the longest x2 40.6 us: fetch(): jnp.take(flat_rows, buffer_place, axis=0)]
    ppermute x14 -> x0, waiting for transfers between devices: 31 us -> none  [from_behind(): lax.ppermute(value, axis, [(source, source + steps) for source in range(i...]
    ppermute x14 -> x0, starting transfers between devices: 27.3 us -> none  [from_behind(): lax.ppermute(value, axis, [(source, source + steps) for source in range(i...]
    reshape x3 -> x5, local copies, waits for them, and re-layouts: 26.9 us -> 4.18 us  [the longest x4 3.1 us: shards(): small = jnp.concatenate([one.reshape(groups, -1) for one in small], 1)]
  transfers between devices with their start and end apart: 29 -> 8, of which waited for: 16 -> 1; matrix products, arithmetic and copies ran while one was open for 31% -> 39% of each run, Pallas kernels for 0% -> 41%
where the time goes in v1:
time: 735 us; the launch traced here: 724 us
  Pallas kernels  319 us (43%)
  matrix products  194 us (26%)
  local copies, waits for them, and re-layouts  116 us (16%)
  other arithmetic  64 us (9%)
  between operations  15.1 us (2%)
  starting transfers between devices  12.4 us (2%)
    pallas_call x7, Pallas kernels, exchange(): pl.pallas_call(kernel, name=name, out_shape=flat((task.outputs for task i...  319 us
    dot_general x7, matrix products, contract_cols(): lax.dot_general(left, right, (((1,), (1,)), ((), ())), preferred_element_...  70.2 us
    dot_general x7, matrix products, mat_dot(): return jnp.dot(left, right, preferred_element_type=jnp.float32)  50.3 us
    dot_general x7, matrix products, contract_rows(): lax.dot_general(left, right, (((0,), (0,)), ((), ())), preferred_element_...  43.7 us
    unnamed x186, local copies, waits for them, and re-layouts  34 us
    convert_element_type x4, local copies, waits for them, and re-layouts, low(): return value.astype(jnp.bfloat16)  20.9 us
    convert_element_type x9, other arithmetic, low(): return value.astype(jnp.bfloat16)  16.2 us
  transfers between devices with their start and end apart: 8, of which 1 were waited for; matrix products, arithmetic and copies ran while one was open for 39% of the time, Pallas kernels for 41%

profile of v1, /device:TPU:0, one launch (start us, length us, event | category | flops | bytes accessed | tf_op | source)
XLA Modules:
  0.0 723.8 jit_solution(10274489154129998391)
XLA Ops:
  35.5 34.6 %gather_keys.1 = bf16[8,2,128,576]{3,2,1,0:T(8,128)(2,1)} custom-call(bf16[2,128,576]{2,1,0:T(8,128)(2,1)} %pad_maximum_fusion.3.refs_0_), custom_call_target="tpu_custom_call" | custom-call | bytes 1179648 | tf_op jit(solution)/shard_map/gather_keys/pallas_call | solution.py:455
  85.3 23.9 %scatter_attn.1 = f32[64,2048]{1,0:T(8,128)} custom-call(bf16[4,64,2048]{2,1,0:T(8,128)(2,1)} %bitcast.180), custom_call_target="tpu_custom_call" | custom-call | bytes 4194304 | tf_op jit(solution)/shard_map/scatter_attn/pallas_call | solution.py:455
  113.3 55.5 %gather_ffn.1 = (bf16[8,4,64,2048]{3,2,1,0:T(8,128)(2,1)}, bf16[8,4,64,128]{3,2,1,0:T(8,128)(2,1)}) custom-call(bf16[64,2048]{1,0:T(8,128)(2,1)} %fusion.41.refs_0_, bf16[64,128]{1,0:T(8,128)(2,1)} %fusion.61.refs_1_), custom_call_target="tpu_custom_call" | custom-call | bytes 1114112 | tf_op jit(solution)/shard_map/gather_ffn/pallas_call | solution.py:455
  188.5 13.5 %fusion.70 = f32[2048,896]{0,1:T(8,128)} fusion(bf16[2048,2048]{1,0:T(8,128)(2,1)} %bitcast.214, bf16[2048,88]{0,1:T(8,128)(2,1)S(1)} %get-tuple-element.186, bf16[2048,352]{0,1:T(8,128)(2,1)S(1)} %get-tuple-element.147, bf16[2048,352]{0,1:T(8,128)(2,1)S(1)} %get-tuple-element.146, bf16[896]{0:T(1024)(128)(2,1)S(1)} %pad.45.clone), kind=kOutput, calls=%fused_computation.177 | convolution fusion | flops 7530872832 | bytes 18974464 | tf_op jit(solution)/shard_map/dot_general | solution.py:30
  202.1 12.6 %fusion.72 = f32[2048,896]{0,1:T(8,128)} fusion(bf16[2048,2048]{1,0:T(8,128)(2,1)S(1)} %bitcast.218, bf16[2048,88]{0,1:T(8,128)(2,1)S(1)} %get-tuple-element.187, bf16[2048,352]{0,1:T(8,128)(2,1)S(1)} %get-tuple-element.145, bf16[2048,352]{0,1:T(8,128)(2,1)S(1)} %get-tuple-element.144, bf16[896]{0:T(1024)(128)(2,1)S(1)} %pad.45.clone), kind=kOutput, calls=%fused_computation.179 | convolution fusion | flops 7530872832 | bytes 18974464 | tf_op jit(solution)/shard_map/dot_general | solution.py:30
  219.4 24.7 %bitcast_multiply_fusion = (f32[2048,896]{0,1:T(8,128)}, bf16[2048,896]{0,1:T(8,128)(2,1)}, bf16[2048,896]{0,1:T(8,128)(2,1)}, bf16[2048,896]{0,1:T(8,128)(2,1)}) fusion(f32[2048,896]{0,1:T(8,128)} %fusion.70, f32[2048,896]{0,1:T(8,128)} %fusion.72, f32[896]{0:T(1024)} %pad.37.clone, f32[2048,352]{0,1:T(8,128)} %broadcast_in_dim.35, ...), kind=kOutput, calls=%fused_computation.15 | convolution fusion | flops 7567572992 | bytes 50435328 | tf_op jit(solution)/shard_map/dot_general | solution.py:38
  244.1 13.9 %convolution_convert_fusion = bf16[2048,2048]{1,0:T(8,128)(2,1)} fusion(bf16[2048,896]{0,1:T(8,128)(2,1)} %get-tuple-element.136, bf16[88,2048]{1,0:T(8,128)(2,1)S(1)} %constant_dynamic-slice_fusion.2, bf16[352,2048]{1,0:T(8,128)(2,1)} %get-tuple-element.143, bf16[352,2048]{1,0:T(8,128)(2,1)} %get-tuple-element.142, bf16[896]{0:T(1024)(128)(2,1)S(1)} %copy-done.68), kind=kOutput, calls=%fused_computation.9 | convolution fusion | flops 7535067136 | bytes 15304448 | tf_op jit(solution)/shard_map/dot_general | solution.py:30
  261.3 3.9 slice_reduce_fusion.1
  266.3 11.0 %fusion.83 = f32[896,2048]{1,0:T(8,128)S(1)} fusion(bf16[2048,896]{0,1:T(8,128)(2,1)S(1)} %copy-done.76, bf16[2048,2048]{1,0:T(8,128)(2,1)} %all-gather.5.cloned.1.call-done), kind=kOutput, calls=%fused_computation.190 | convolution fusion | flops 7516192768 | bytes 19398656 | tf_op jit(solution)/shard_map/dot_general | solution.py:34
  281.0 3.6 all-to-all-start.2
  287.4 5.3 dynamic_update_slice.3
  294.6 15.4 %fusion.71 = f32[2048,2048]{1,0:T(8,128)} fusion(bf16[2048,896]{0,1:T(8,128)(2,1)} %get-tuple-element.135, bf16[2048,88]{0,1:T(8,128)(2,1)} %copy-done.42, bf16[2048,352]{0,1:T(8,128)(2,1)} %copy-done.31, bf16[2048,352]{0,1:T(8,128)(2,1)} %copy-done.30, bf16[896]{0:T(1024)(128)(2,1)S(1)} %copy-done.69), kind=kOutput, calls=%fused_computation.178 | convolution fusion | flops 7530872832 | bytes 23693056 | tf_op jit(solution)/shard_map/dot_general | solution.py:38
  310.1 16.0 %add_convert_fusion = bf16[2048,2048]{1,0:T(8,128)(2,1)} fusion(f32[2048,2048]{1,0:T(8,128)} %fusion.71, bf16[2048,896]{0,1:T(8,128)(2,1)} %get-tuple-element.137, bf16[2048,88]{0,1:T(8,128)(2,1)S(1)} %copy-done.41, bf16[2048,352]{0,1:T(8,128)(2,1)S(1)} %copy-done.29, bf16[2048,352]{0,1:T(8,128)(2,1)S(1)} %copy-done.27, bf16[896]{0:T(1024)(128)(2,1)S(1)} %copy-done.69), kind=kOutput, calls=%fused_computation | convolution fusion | flops 7539261440 | bytes 32081664 | tf_op jit(solution)/shard_map/dot_general | solution.py:38
  326.1 61.9 %scatter_ffn.1 = (f32[64,2048]{1,0:T(8,128)}, f32[64,128]{1,0:T(8,128)}) custom-call(bf16[4,2,4,64,2048]{4,3,2,1,0:T(8,128)(2,1)} %bitcast.166, bf16[4,2,4,64,128]{4,3,2,1,0:T(8,128)(2,1)} %bitcast.184), custom_call_target="tpu_custom_call" | custom-call | bytes 35651584 | tf_op jit(solution)/shard_map/scatter_ffn/pallas_call | solution.py:455
  389.4 11.6 %fusion.85 = f32[2048,896]{0,1:T(8,128)S(1)} fusion(bf16[2048,896]{0,1:T(8,128)(2,1)} %get-tuple-element.137, bf16[2048,2048]{1,0:T(8,128)(2,1)} %bitcast.215), kind=kOutput, calls=%fused_computation.192 | convolution fusion | flops 7516192768 | bytes 19398656 | tf_op jit(solution)/shard_map/dot_general | solution.py:34
  406.5 9.9 %fusion.84 = f32[2048,896]{0,1:T(8,128)} fusion(bf16[2048,896]{0,1:T(8,128)(2,1)S(1)} %copy-done.75, bf16[2048,2048]{1,0:T(8,128)(2,1)S(1)} %bitcast.221), kind=kOutput, calls=%fused_computation.191 | convolution fusion | flops 7516192768 | bytes 19398656 | tf_op jit(solution)/shard_map/dot_general | solution.py:34
  419.8 6.0 slice_bitcast_fusion.3
  438.7 4.1 all-to-all-start.1
  442.8 6.0 pad_maximum_fusion.1
  450.7 4.1 all-to-all-start
  455.3 5.9 pad_maximum_fusion
  468.5 24.5 %gather_hidden.1 = bf16[4,64,2048]{2,1,0:T(8,128)(2,1)} custom-call(bf16[64,2048]{1,0:T(8,128)(2,1)} %get-tuple-element.130.refs_0_), custom_call_target="tpu_custom_call" | custom-call | bytes 1048576 | tf_op jit(solution)/shard_map/gather_hidden/pallas_call | solution.py:455
  499.6 6.5 fusion.11
  506.1 4.7 multiply_reduce_fusion
  526.9 4.9 maximum_convert_fusion
  531.8 7.6 %copy.187 = bf16[2048,4,256]{2,1,0:T(4,128)(2,1)} copy(bf16[2048,4,256]{0,2,1:T(8,128)(2,1)} %maximum_convert_fusion) | data formatting | bytes 8388608 | tf_op jit(solution)/shard_map/convert_element_type | solution.py:80
  539.4 7.7 %convert_element_type.219 = bf16[4,2,4,64,1024]{4,3,2,1,0:T(8,128)(2,1)} reshape(bf16[2048,4,256]{2,1,0:T(4,128)(2,1)} %copy.187) | data formatting | bytes 8388608 | tf_op jit(solution)/shard_map/convert_element_type | solution.py:80
  549.7 5.2 convolution_convert_fusion.8
  558.3 3.7 pad_maximum_fusion.2.refs_0_
  564.7 60.3 %scatter_latent.1 = (f32[64,576]{1,0:T(8,128)}, f32[64,2048]{1,0:T(8,128)}, f32[2,128,768]{2,1,0:T(8,128)}, f32[2,32,1024]{2,1,0:T(8,128)}) custom-call(bf16[4,2,4,64,576]{4,3,2,1,0:T(8,128)(2,1)} %pad_maximum_fusion.2.refs_0_, bf16[4,64,2048]{2,1,0:T(8,128)(2,1)} %bitcast.194, bf16[4,2,2,128,768]{4,3,2,1,0:T(8,128)(2,1)} %bitcast.163, ...), custom_call_target="tpu_custom_call" | custom-call | bytes 30408704 | tf_op jit(solution)/shard_map/scatter_latent/pallas_call | solution.py:455
  635.7 4.4 copy.195
  642.3 58.5 %scatter_last.1 = (bf16[4,64,576]{2,1,0:T(8,128)(2,1)}, bf16[4,16,128]{2,1,0:T(8,128)(2,1)}, bf16[4,64,2048]{2,1,0:T(8,128)(2,1)}) custom-call(bf16[4,2,4,64,576]{4,3,2,1,0:T(8,128)(2,1)} %bitcast.165, bf16[4,2,4,16,128]{4,3,2,1,0:T(8,128)(2,1)} %bitcast.206, bf16[64,2048]{1,0:T(8,128)(2,1)} %add_convert_fusion.1.refs_2_), custom_call_target="tpu_custom_call" | custom-call | bytes 11010048 | tf_op jit(solution)/shard_map/scatter_last/pallas_call | solution.py:455
  (321 shorter events, 177.3 us)
Async XLA Ops:
  7.2 207.6 %all-gather.5.cloned.1.call-start = ((), (), s32[]{:S(2)}) async-start(), calls=%async_computation.9 | async-start | bytes 9437184 | tf_op jit(solution)/shard_map/all_gather | solution.py:84
  7.9 408.4 %reduce-scatter.4.cloned.1.call-start = ((), (), s32[]{:S(2)}) async-start(), calls=%async_computation.6 | async-start | bytes 9437184 | tf_op jit(solution)/shard_map/reduce_scatter | solution.py:88
  32.3 37.8 %copy-start.22 = (f32[256,4,32]{2,0,1:T(8,128)S(1)}, f32[256,4,32]{2,0,1:T(8,128)}, u32[]{:S(2)}) copy-start(f32[256,4,32]{2,0,1:T(8,128)} %copy.217) | copy-start | bytes 393220
  32.3 37.8 %copy-start.23 = (f32[256,4,32]{2,0,1:T(8,128)S(1)}, f32[256,4,32]{2,0,1:T(8,128)}, u32[]{:S(2)}) copy-start(f32[256,4,32]{2,0,1:T(8,128)} %copy.216) | copy-start | bytes 393220
  32.3 37.9 %copy-start.25 = (f32[256,4,128]{2,0,1:T(8,128)S(1)}, f32[256,4,128]{2,0,1:T(8,128)}, u32[]{:S(2)}) copy-start(f32[256,4,128]{2,0,1:T(8,128)} %copy.215) | copy-start | bytes 1572868
  34.6 36.2 %copy-start.32 = (f32[256,32]{1,0:T(8,128)}, f32[256,32]{1,0:T(8,128)S(1)}, u32[]{:S(2)}) copy-start(f32[256,32]{1,0:T(8,128)S(1)} %get-tuple-element.173) | copy-start | bytes 98308
  34.6 36.2 %copy-start.39 = (f32[256,32]{1,0:T(8,128)}, f32[256,32]{1,0:T(8,128)S(1)}, u32[]{:S(2)}) copy-start(f32[256,32]{1,0:T(8,128)S(1)} %get-tuple-element.170) | copy-start | bytes 98308
  34.6 36.2 %copy-start.74 = (bf16[512,1024]{1,0:T(8,128)(2,1)S(1)}, bf16[512,1024]{1,0:T(8,128)(2,1)}, u32[]{:S(2)}) copy-start(bf16[512,1024]{1,0:T(8,128)(2,1)} %param.22) | copy-start | bytes 3145732
  83.5 27.6 %copy-start.46 = (bf16[2048,16]{0,1:T(8,128)(2,1)S(1)}, bf16[2048,16]{0,1:T(8,128)(2,1)}, u32[]{:S(2)}) copy-start(bf16[2048,16]{0,1:T(8,128)(2,1)} %param.25) | copy-start | bytes 196612
  83.5 27.6 %copy-start.47 = (f32[2048]{0:T(1024)S(1)}, f32[2048]{0:T(1024)}, u32[]{:S(2)}) copy-start(f32[2048]{0:T(1024)} %param.24) | copy-start | bytes 24580
  111.1 66.2 %copy-start.53 = (f32[64]{0:T(128)}, f32[64]{0:T(128)S(1)}, u32[]{:S(2)}) copy-start(f32[64]{0:T(128)S(1)} %get-tuple-element.175) | copy-start | bytes 772
  111.7 65.6 %copy-start.56 = (f32[64]{0:T(128)}, f32[64]{0:T(128)S(1)}, u32[]{:S(2)}) copy-start(f32[64]{0:T(128)S(1)} %get-tuple-element.178) | copy-start | bytes 772
  177.3 24.8 %copy-start.67 = (bf16[896]{0:T(1024)(128)(2,1)}, bf16[896]{0:T(1024)(128)(2,1)S(1)}, u32[]{:S(2)}) copy-start(bf16[896]{0:T(1024)(128)(2,1)S(1)} %pad.45.clone) | copy-start | bytes 5380
  180.2 21.8 %copy-start.42 = (bf16[2048,88]{0,1:T(8,128)(2,1)}, bf16[2048,88]{0,1:T(8,128)(2,1)S(1)}, u32[]{:S(2)}) copy-start(bf16[2048,88]{0,1:T(8,128)(2,1)S(1)} %get-tuple-element.187) | copy-start | bytes 1081348
  183.8 18.3 %copy-start.30 = (bf16[2048,352]{0,1:T(8,128)(2,1)}, bf16[2048,352]{0,1:T(8,128)(2,1)S(1)}, u32[]{:S(2)}) copy-start(bf16[2048,352]{0,1:T(8,128)(2,1)S(1)} %get-tuple-element.144) | copy-start | bytes 4325380
  183.8 18.3 %copy-start.31 = (bf16[2048,352]{0,1:T(8,128)(2,1)}, bf16[2048,352]{0,1:T(8,128)(2,1)S(1)}, u32[]{:S(2)}) copy-start(bf16[2048,352]{0,1:T(8,128)(2,1)S(1)} %get-tuple-element.145) | copy-start | bytes 4325380
  219.4 24.7 %copy-start.68 = (bf16[896]{0:T(1024)(128)(2,1)S(1)}, bf16[896]{0:T(1024)(128)(2,1)}, u32[]{:S(2)}) copy-start(bf16[896]{0:T(1024)(128)(2,1)} %copy-done.67) | copy-start | bytes 5380
  281.0 157.6 %all-to-all-start.2 = ((bf16[88,8,256]{2,0,1:T(8,128)(2,1)}), bf16[88,8,256]{2,0,1:T(8,128)(2,1)S(1)}, u32[]{:S(2)}, u32[]{:S(2)}) async-start(bf16[88,8,256]{2,0,1:T(8,128)(2,1)} %bitcast.188), calls=%async_computation.5 | async-start | bytes 720896 | tf_op jit(solution)/shard_map/all_to_all | solution.py:705
  284.7 181.3 %reduce-scatter.6.cloned.1.call-start = ((), (), s32[]{:S(2)}) async-start(), calls=%async_computation.7 | async-start | bytes 1310720 | tf_op jit(solution)/shard_map/reduce_scatter | solution.py:88
  326.1 62.7 %copy-start.57 = (f32[64]{0:T(128)S(1)}, f32[64]{0:T(128)}, u32[]{:S(2)}) copy-start(f32[64]{0:T(128)} %copy-done.56) | copy-start | bytes 772
  326.1 80.4 %slice-start.6 = ((s8[8388608]{0:T(1024)(128)(4,1)}), s8[4194304]{0:T(1024)(128)(4,1)S(1)}, s32[]{:S(2)}) async-start(s8[8388608]{0:T(1024)(128)(4,1)} %bitcast.219), calls=%async_computation.17 | async-start | bytes 8388608
  438.7 12.1 %all-to-all-start.1 = ((bf16[8,256,88]{1,2,0:T(8,128)(2,1)}), bf16[8,256,88]{1,2,0:T(8,128)(2,1)}, u32[]{:S(2)}, u32[]{:S(2)}) async-start(bf16[8,256,88]{1,2,0:T(8,128)(2,1)} %bitcast.190), calls=%async_computation.4 | async-start | bytes 720896 | tf_op jit(solution)/shard_map/all_to_all | solution.py:698
  450.7 13.3 %all-to-all-start = ((bf16[8,256,88]{1,2,0:T(8,128)(2,1)}), bf16[8,256,88]{1,2,0:T(8,128)(2,1)}, u32[]{:S(2)}, u32[]{:S(2)}) async-start(bf16[8,256,88]{1,2,0:T(8,128)(2,1)} %bitcast.189), calls=%async_computation.3 | async-start | bytes 720896 | tf_op jit(solution)/shard_map/all_to_all | solution.py:698
  454.8 254.2 %all-gather.3.cloned.1.call-start = ((), (), s32[]{:S(2)}) async-start(), calls=%async_computation.8 | async-start | bytes 1310720 | tf_op jit(solution)/shard_map/all_gather | solution.py:84
  464.0 32.5 %copy-start.37 = (bf16[4,128,256]{2,1,0:T(8,128)(2,1)S(1)}, bf16[4,128,256]{2,1,0:T(8,128)(2,1)}, u32[]{:S(2)}) copy-start(bf16[4,128,256]{2,1,0:T(8,128)(2,1)} %copy-done.36) | copy-start | bytes 786436
  521.0 188.1 %reduce-scatter.8.cloned.1.call-start = ((), (), s32[]{:S(2)}) async-start(), calls=%async_computation.10 | async-start | bytes 2359296 | tf_op jit(solution)/shard_map/reduce_scatter | solution.py:88
  564.7 60.3 %copy-start.34 = (f32[64,512]{1,0:T(8,128)S(1)}, f32[64,512]{1,0:T(8,128)}, u32[]{:S(2)}) copy-start(f32[64,512]{1,0:T(8,128)} %copy.223) | copy-start | bytes 393220
  564.7 60.3 %copy-start.51 = (f32[512]{0:T(512)S(1)}, f32[512]{0:T(512)}, u32[]{:S(2)}) copy-start(f32[512]{0:T(512)} %param.21) | copy-start | bytes 6148
  564.7 60.4 %copy-start.64 = (f32[64]{0:T(128)S(1)}, f32[64]{0:T(128)}, u32[]{:S(2)}) copy-start(f32[64]{0:T(128)} %get-tuple-element.129) | copy-start | bytes 772
  564.7 62.5 %copy-start.71 = (f32[64]{0:T(128)S(1)}, f32[64]{0:T(128)}, u32[]{:S(2)}) copy-start(f32[64]{0:T(128)} %get-tuple-element.128) | copy-start | bytes 772
  564.7 63.5 %copy-start.49 = (f32[2048]{0:T(1024)S(1)}, f32[2048]{0:T(1024)}, u32[]{:S(2)}) copy-start(f32[2048]{0:T(1024)} %param.18) | copy-start | bytes 24580
  564.7 63.5 %copy-start.63 = (f32[64]{0:T(128)S(1)}, f32[64]{0:T(128)}, u32[]{:S(2)}) copy-start(f32[64]{0:T(128)} %get-tuple-element.127) | copy-start | bytes 772
  (61 other events, 444.3 us)
Sparse Core Ops, SparseCore 0:
  9.9 67.5 all-gather.4
  258.2 73.0 reduce-scatter.3
  416.5 27.4 reduce-scatter.5
  521.1 30.9 all-gather.2
  558.4 52.7 reduce-scatter.7

commit v2 on v1

--- a/solution.py
+++ b/solution.py
@@ -1,3 +1,5 @@
+import functools
+
 import jax
 import jax.numpy as jnp
 from jax import lax
@@ -273,6 +275,7 @@
         sems, beside = scratch[0:2], scratch[2]
         d_send, d_recv, x_send, x_recv, y_send, y_recv = scratch[3:9]
         units, core = self.units, place.core
+        other_core = 1 - core
         if self.with_z:
             z_sems, z_send, z_recv = scratch[9:11], scratch[11], scratch[12]
             near, far, other = place.levels
@@ -281,9 +284,9 @@
             order = list(range(units))
         sends = []
 
-        def launch(copy):
-            copy.start()
-            sends.append(copy)
+        def launch(make, p):
+            make(p).start()
+            sends.append((make, p))
 
         def across(p):
             target = place.near_x if p % 2 == 0 else place.near_y
@@ -297,7 +300,7 @@
 
         def to_sibling(p):
             return push(
-                part.at[:, 1 - core, order[p]],
+                part.at[:, other_core, order[p]],
                 beside.at[p],
                 sems,
                 4 * p,
@@ -307,28 +310,25 @@
         def both(p, chip):
             return [part.at[chip, core, order[p]], beside.at[p, chip]]
 
-        for p in range(units):
-            launch(to_sibling(p))
-
         def stage_one(p):
             to_sibling(p).wait_recv()
             add_rows(d_send.at[p], both(p, place.chip_xy))
-            launch(across(p))
+            launch(across, p)
             if p % 2 == 0:
                 add_rows(x_send.at[p], both(p, place.chip_x))
-                launch(to_x(p))
+                launch(to_x, p)
             else:
                 add_rows(y_send.at[p], both(p, place.chip_y))
-                launch(to_y(p))
+                launch(to_y, p)
 
         def stage_two(p):
             across(p).wait_recv()
             if p % 2 == 0:
                 add_rows(y_send.at[p], both(p, place.chip_y) + [d_recv.at[p]])
-                launch(to_y(p))
+                launch(to_y, p)
             else:
                 add_rows(x_send.at[p], both(p, place.chip_x) + [d_recv.at[p]])
-                launch(to_x(p))
+                launch(to_x, p)
 
         def to_level(p):
             return push(z_send.at[p], z_recv.at[p], z_sems, p, tensor=order[p])
@@ -341,13 +341,17 @@
                 add_rows(out.at[p], pieces)
             elif p < units - 1:
                 add_rows(z_send.at[p], pieces)
-                launch(to_level(p))
+                launch(to_level, p)
             else:
                 for k in range(DEPTH - 1):
                     to_level(k).wait_recv()
                 pieces += [z_recv.at[k] for k in range(DEPTH - 1)]
                 add_rows(scratch[15] if self.spread else out, pieces)
 
+        yield
+        for p in range(units):
+            launch(to_sibling, p)
+        yield
         for p in range(units + 2):
             if p < units:
                 stage_one(p)
@@ -356,11 +360,15 @@
                 stage_two(p - 1)
             if 0 <= p - 2 < units:
                 stage_three(p - 2)
-            yield
+            if p < units + 1:
+                yield
         if self.spread:
-            yield from spread_levels(place, scratch[15], out, scratch[13:15], sends)
-        for copy in sends:
-            copy.wait_send()
+            copies = []
+            yield from spread_levels(place, scratch[15], out, scratch[13:15], copies)
+            for copy in copies:
+                copy.wait_send()
+        for make, p in sends:
+            make(p).wait_send()
 
 
 def spread_levels(place, own, out, z_sems, sends):
@@ -418,19 +426,19 @@
             copy.wait_send()
 
 
+def greet(place):
+    barrier = pltpu.get_barrier_semaphore()
+    for target in (place.sibling, place.near_x, place.near_y):
+        pl.semaphore_signal(barrier, inc=1, device_id={"dp": target}, device_id_type=MESH)
+    for target in place.levels:
+        pl.semaphore_signal(barrier, inc=1, device_id={"tensor": target}, device_id_type=MESH)
+    pl.semaphore_wait(barrier, 6)
+
+
 def exchange(tasks, collective_id, name):
     def kernel(*refs):
         place = Place()
-        barrier = pltpu.get_barrier_semaphore()
-        for target in (place.sibling, place.near_x, place.near_y):
-            pl.semaphore_signal(
-                barrier, inc=1, device_id={"dp": target}, device_id_type=MESH
-            )
-        for target in place.levels:
-            pl.semaphore_signal(
-                barrier, inc=1, device_id={"tensor": target}, device_id_type=MESH
-            )
-        pl.semaphore_wait(barrier, 6)
+        greet(place)
         refs = list(refs)
 
         def take(counts):
@@ -464,6 +472,529 @@
         ),
         cost_estimate=pl.CostEstimate(flops=0, bytes_accessed=4 * moved, transcendentals=0),
     )(*flat(task.inputs for task in tasks))
+
+
+KEY_BLOCK = 256
+
+
+def dot_nt(left, right):
+    return lax.dot_general(left, right, (((1,), (1,)), ((), ())), preferred_element_type=jnp.float32)
+
+
+def dot_tn(left, right):
+    return lax.dot_general(left, right, (((0,), (0,)), ((), ())), preferred_element_type=jnp.float32)
+
+
+def turn(values, cos_wide, sin_wide):
+    half = values.shape[1] // 2
+    swapped = jnp.concatenate([values[:, half:], values[:, :half]], 1)
+    return values * cos_wide + swapped * sin_wide
+
+
+def block_of(k):
+    return pl.ds(pl.multiple_of(k * KEY_BLOCK, KEY_BLOCK), KEY_BLOCK)
+
+
+def masked_block(q_nope, q_rope, kv_ref, keys_ref, base, k, h):
+    at = block_of(k)
+    wide = NOPE + VD
+    scores = dot_nt(q_nope, kv_ref[at, wide * h : wide * h + NOPE])
+    scores = scores + dot_nt(q_rope, keys_ref[at, R : R + ROPE])
+    key_pos = k * KEY_BLOCK + lax.broadcasted_iota(jnp.int32, scores.shape, 1)
+    query_pos = base + lax.broadcasted_iota(jnp.int32, scores.shape, 0)
+    return jnp.where(key_pos <= query_pos, scores, masked_score)
+
+
+def attend_kernel(
+    base_ref, x_ref, wq_ref, keys_ref, wup_ref, wo_ref, cos_ref, sin_ref,
+    q_ref, kv_ref, o_ref, lse_ref, attn_ref, s_ref, sum_ref,
+):
+    base = base_ref[0]
+    rows = x_ref.shape[0]
+    blocks = keys_ref.shape[0] // KEY_BLOCK
+    factor = (NOPE + ROPE) ** (-0.5)
+    query = jnp.dot(x_ref[...], wq_ref[...], preferred_element_type=jnp.float32) * factor
+
+    def expand(k, carry):
+        at = block_of(k)
+        kv_ref[at, :] = jnp.dot(
+            keys_ref[at, :R], wup_ref[...], preferred_element_type=jnp.float32
+        ).astype(jnp.bfloat16)
+        return carry
+
+    lax.fori_loop(0, blocks, expand, 0)
+    for h in range(2):
+        start = h * (NOPE + ROPE)
+        q_nope = query[:, start : start + NOPE].astype(jnp.bfloat16)
+        q_rope = turn(
+            query[:, start + NOPE : start + NOPE + ROPE], cos_ref[...], sin_ref[...]
+        ).astype(jnp.bfloat16)
+        q_ref[:, 256 * h : 256 * h + NOPE] = q_nope
+        q_ref[:, 256 * h + NOPE : 256 * h + NOPE + ROPE] = q_rope
+        q_ref[:, 256 * h + NOPE + ROPE : 256 * (h + 1)] = jnp.zeros(
+            (rows, 256 - NOPE - ROPE), jnp.bfloat16
+        )
+
+        def first(k, top, h=h, q_nope=q_nope, q_rope=q_rope):
+            scores = masked_block(q_nope, q_rope, kv_ref, keys_ref, base, k, h)
+            s_ref[k] = scores
+            return jnp.maximum(top, jnp.maximum(scores[:, :128], scores[:, 128:]))
+
+        top = lax.fori_loop(0, blocks, first, jnp.full((rows, 128), masked_score, jnp.float32))
+        top = jnp.max(top, 1, keepdims=True)
+
+        def second(k, carry, h=h, top=top):
+            total, acc = carry
+            weights = jnp.exp(s_ref[k] - top)
+            total = total + weights[:, :128] + weights[:, 128:]
+            value = kv_ref[block_of(k), 256 * h + NOPE : 256 * (h + 1)]
+            acc = acc + jnp.dot(
+                weights.astype(jnp.bfloat16), value, preferred_element_type=jnp.float32
+            )
+            return total, acc
+
+        zero = jnp.zeros((rows, 128), jnp.float32)
+        total, acc = lax.fori_loop(0, blocks, second, (zero, zero))
+        total = jnp.sum(total, 1, keepdims=True)
+        o_ref[:, VD * h : VD * (h + 1)] = (acc / total).astype(jnp.bfloat16)
+        lse_ref[:, 128 * h : 128 * (h + 1)] = jnp.broadcast_to(top + jnp.log(total), (rows, 128))
+    part = jnp.dot(o_ref[...], wo_ref[...], preferred_element_type=jnp.float32)
+
+    @pl.when(pl.program_id(0) == 0)
+    def _():
+        sum_ref[...] = part
+
+    @pl.when(pl.program_id(0) > 0)
+    def _():
+        sum_ref[...] += part
+
+    @pl.when(pl.program_id(0) == pl.num_programs(0) - 1)
+    def _():
+        attn_ref[...] = sum_ref[...].astype(jnp.bfloat16)
+
+
+def whole_block(shape):
+    return pl.BlockSpec(shape, lambda i: (0,) * len(shape))
+
+
+def column_block(shape):
+    return pl.BlockSpec(shape, lambda i: (0, i))
+
+
+def attend(base, x, wq, keys, wup, wo, cos_wide, sin_wide):
+    rows, width = x.shape
+    heads = wo.shape[0] // VD
+    count = keys.shape[0]
+    struct = jax.ShapeDtypeStruct
+    return pl.pallas_call(
+        attend_kernel,
+        name="attend",
+        grid=(heads // 2,),
+        in_specs=[
+            pl.BlockSpec(memory_space=pltpu.SMEM),
+            whole_block((rows, width)),
+            column_block((width, 2 * (NOPE + ROPE))),
+            whole_block(keys.shape),
+            column_block((R, 2 * (NOPE + VD))),
+            pl.BlockSpec((2 * VD, width), lambda i: (i, 0)),
+            whole_block(cos_wide.shape),
+            whole_block(sin_wide.shape),
+        ],
+        out_specs=[
+            column_block((rows, 512)),
+            column_block((count, 512)),
+            column_block((rows, 2 * VD)),
+            column_block((rows, 256)),
+            whole_block((rows, width)),
+        ],
+        out_shape=[
+            struct((rows, heads * 256), jnp.bfloat16),
+            struct((count, heads * 256), jnp.bfloat16),
+            struct((rows, heads * VD), jnp.bfloat16),
+            struct((rows, heads * 128), jnp.float32),
+            struct((rows, width), jnp.bfloat16),
+        ],
+        scratch_shapes=[
+            pltpu.VMEM((count // KEY_BLOCK, rows, KEY_BLOCK), jnp.float32),
+            pltpu.VMEM((rows, width), jnp.float32),
+        ],
+        compiler_params=pltpu.CompilerParams(vmem_limit_bytes=48 << 20),
+        cost_estimate=pl.CostEstimate(
+            flops=7 * 10**9, bytes_accessed=20 << 20, transcendentals=2 << 20
+        ),
+    )(base, x, wq, keys, wup, wo, cos_wide, sin_wide)
+
+
+def attend_back_kernel(
+    base_ref, q_ref, kv_ref, keys_ref, lse_ref, da_ref, wo_ref, wup_ref, cos_ref, sin_ref,
+    dq_ref, dup_ref, dlat_ref, p_ref, dp_ref, dkv_ref, lat_ref, rope_ref, up_ref, acc_ref,
+):
+    base = base_ref[0]
+    rows = q_ref.shape[0]
+    blocks = keys_ref.shape[0] // KEY_BLOCK
+    factor = (NOPE + ROPE) ** (-0.5)
+    step = pl.program_id(0)
+
+    @pl.when(step == 0)
+    def _():
+        lat_ref[...] = jnp.zeros_like(lat_ref)
+        rope_ref[...] = jnp.zeros_like(rope_ref)
+
+    up_ref[...] = jnp.zeros_like(up_ref)
+    acc_ref[...] = jnp.zeros_like(acc_ref)
+    d_out = dot_nt(da_ref[...], wo_ref[...]).astype(jnp.bfloat16)
+    deltas = []
+    for h in range(2):
+        q_nope = q_ref[:, 256 * h : 256 * h + NOPE]
+        q_rope = q_ref[:, 256 * h + NOPE : 256 * h + NOPE + ROPE]
+        lse = lse_ref[:, 128 * h : 128 * h + 1]
+        d_head = d_out[:, VD * h : VD * (h + 1)]
+
+        def first(k, delta, h=h, q_nope=q_nope, q_rope=q_rope, lse=lse, d_head=d_head):
+            at = block_of(k)
+            scores = masked_block(q_nope, q_rope, kv_ref, keys_ref, base, k, h)
+            probs = jnp.exp(scores - lse)
+            d_probs = dot_nt(d_head, kv_ref[at, 256 * h + NOPE : 256 * (h + 1)])
+            p_ref[h, k] = probs
+            dp_ref[h, k] = d_probs
+            dkv_ref[at, 256 * h + NOPE : 256 * (h + 1)] = dot_tn(
+                probs.astype(jnp.bfloat16), d_head
+            ).astype(jnp.bfloat16)
+            both = probs * d_probs
+            return delta + both[:, :128] + both[:, 128:]
+
+        delta = lax.fori_loop(0, blocks, first, jnp.zeros((rows, 128), jnp.float32))
+        deltas.append(jnp.sum(delta, 1, keepdims=True))
+
+    def second(k, carry):
+        at = block_of(k)
+        for h in range(2):
+            q_nope = q_ref[:, 256 * h : 256 * h + NOPE]
+            q_rope = q_ref[:, 256 * h + NOPE : 256 * h + NOPE + ROPE]
+            d_scores = (p_ref[h, k] * (dp_ref[h, k] - deltas[h])).astype(jnp.bfloat16)
+            acc_ref[:, 256 * h : 256 * h + NOPE] += jnp.dot(
+                d_scores, kv_ref[at, 256 * h : 256 * h + NOPE], preferred_element_type=jnp.float32
+            )
+            acc_ref[:, 256 * h + NOPE : 256 * h + NOPE + ROPE] += jnp.dot(
+                d_scores, keys_ref[at, R : R + ROPE], preferred_element_type=jnp.float32
+            )
+            dkv_ref[at, 256 * h : 256 * h + NOPE] = dot_tn(d_scores, q_nope).astype(jnp.bfloat16)
+            rope_ref[at, :] += dot_tn(d_scores, q_rope)
+        d_kv = dkv_ref[at, :]
+        lat_ref[at, :] += dot_nt(d_kv, wup_ref[...])
+        up_ref[...] += dot_tn(keys_ref[at, :R], d_kv)
+        return carry
+
+    lax.fori_loop(0, blocks, second, 0)
+    pieces = []
+    for h in range(2):
+        pieces.append(acc_ref[:, 256 * h : 256 * h + NOPE])
+        pieces.append(
+            turn(
+                acc_ref[:, 256 * h + NOPE : 256 * h + NOPE + ROPE], cos_ref[...], -sin_ref[...]
+            )
+        )
+    dq_ref[...] = (jnp.concatenate(pieces, 1) * factor).astype(jnp.bfloat16)
+    dup_ref[...] = up_ref[...].astype(jnp.bfloat16)
+
+    @pl.when(step == pl.num_programs(0) - 1)
+    def _():
+        dlat_ref[:, :R] = lat_ref[...].astype(jnp.bfloat16)
+        dlat_ref[:, R:] = rope_ref[...].astype(jnp.bfloat16)
+
+
+def attend_back(base, q, kv, keys, lse, d_attn, wo, wup, cos_wide, sin_wide):
+    rows, width = d_attn.shape
+    heads = wo.shape[0] // VD
+    count = keys.shape[0]
+    blocks = count // KEY_BLOCK
+    struct = jax.ShapeDtypeStruct
+    square = pltpu.VMEM((2, blocks, rows, KEY_BLOCK), jnp.float32)
+    return pl.pallas_call(
+        attend_back_kernel,
+        name="attend_back",
+        grid=(heads // 2,),
+        in_specs=[
+            pl.BlockSpec(memory_space=pltpu.SMEM),
+            column_block((rows, 512)),
+            column_block((count, 512)),
+            whole_block(keys.shape),
+            column_block((rows, 256)),
+            whole_block(d_attn.shape),
+            pl.BlockSpec((2 * VD, width), lambda i: (i, 0)),
+            column_block((R, 2 * (NOPE + VD))),
+            whole_block(cos_wide.shape),
+            whole_block(sin_wide.shape),
+        ],
+        out_specs=[
+            column_block((rows, 2 * (NOPE + ROPE))),
+            column_block((R, 2 * (NOPE + VD))),
+            whole_block(keys.shape),
+        ],
+        out_shape=[
+            struct((rows, heads * (NOPE + ROPE)), jnp.bfloat16),
+            struct((R, heads * (NOPE + VD)), jnp.bfloat16),
+            struct(keys.shape, jnp.bfloat16),
+        ],
+        scratch_shapes=[
+            square,
+            square,
+            pltpu.VMEM((count, 512), jnp.bfloat16),
+            pltpu.VMEM((count, R), jnp.float32),
+            pltpu.VMEM((count, ROPE), jnp.float32),
+            pltpu.VMEM((R, 512), jnp.float32),
+            pltpu.VMEM((rows, 512), jnp.float32),
+        ],
+        compiler_params=pltpu.CompilerParams(vmem_limit_bytes=56 << 20),
+        cost_estimate=pl.CostEstimate(
+            flops=10**10, bytes_accessed=20 << 20, transcendentals=2 << 20
+        ),
+    )(base, q, kv, keys, lse, d_attn, wo, wup, cos_wide, sin_wide)
+
+
+def kept(shape, **kwargs):
+    return pl.BlockSpec(shape, lambda i: (0,) * len(shape), pipeline_mode=pl.Buffered(1), **kwargs)
+
+
+def expert_kernel(
+    experts, first_ref, x_ref, g_ref, route_ref, eg_ref, eu_ref, ed_ref, sg_ref, su_ref, sd_ref,
+    act_ref, turned_ref, dx_ref, dw_ref, weight_ref, gate_ref, up_ref, plain_ref, dgu_ref,
+):
+    local_experts, units, _ = eg_ref.shape
+    shared_units = sg_ref.shape[0]
+    wide = act_ref.shape[1]
+    rows = x_ref.shape[0]
+    taken = local_experts * units
+
+    @pl.when(pl.program_id(0) == 0)
+    def _():
+        for k, (routed, shared) in enumerate(
+            ((eg_ref, sg_ref), (eu_ref, su_ref), (ed_ref, sd_ref))
+        ):
+            start = k * wide
+            for e in range(local_experts):
+                weight_ref[start + e * units : start + (e + 1) * units, :] = routed[e]
+            weight_ref[start + taken : start + taken + shared_units, :] = shared[...]
+            weight_ref[start + taken + shared_units : start + wide, :] = jnp.zeros(
+                (wide - taken - shared_units, weight_ref.shape[1]), jnp.bfloat16
+            )
+
+    plain_ref[...] = dot_nt(g_ref[...], weight_ref[2 * wide :, :])
+    gate_ref[...] = dot_nt(x_ref[...], weight_ref[:wide, :])
+    up_ref[...] = dot_nt(x_ref[...], weight_ref[wide : 2 * wide, :])
+    step = 16
+
+    def piece(k, carry):
+        at = pl.ds(pl.multiple_of(k * step, step), step)
+        gate, up, plain = gate_ref[at, :], up_ref[at, :], plain_ref[at, :]
+        column = lax.broadcasted_iota(jnp.int32, gate.shape, 1)
+        lane = lax.broadcasted_iota(jnp.int32, (step, 128), 1)
+        routes = route_ref[at, :].astype(jnp.float32)
+        scale = jnp.ones(gate.shape, jnp.float32)
+        for e in reversed(range(local_experts)):
+            mine = lax.rem(lane, experts) == first_ref[0] + e
+            weight = jnp.sum(jnp.where(mine, routes, 0.0), 1, keepdims=True)
+            scale = jnp.where(column < (e + 1) * units, weight, scale)
+        logistic = 1.0 / (1.0 + jnp.exp(-gate))
+        silu = gate * logistic
+        act = silu * up
+        act_ref[at, :] = (act * scale).astype(jnp.bfloat16)
+        d_act = plain * scale
+        dgu_ref[at, :wide] = (
+            d_act * up * logistic * (1.0 + gate * (1.0 - logistic))
+        ).astype(jnp.bfloat16)
+        dgu_ref[at, wide:] = (d_act * silu).astype(jnp.bfloat16)
+        dots = act * plain
+        out = jnp.zeros((step, 128), jnp.float32)
+        for e in range(local_experts):
+            inside = (column >= e * units) & (column < (e + 1) * units)
+            total = jnp.sum(jnp.where(inside, dots, 0.0), 1, keepdims=True)
+            out = jnp.where(lane == first_ref[0] + e, total, out)
+        dw_ref[at, :] = out.astype(jnp.bfloat16)
+        return carry
+
+    lax.fori_loop(0, rows // step, piece, 0)
+    turned_ref[: 2 * wide, :] = dgu_ref[...].T
+    turned_ref[2 * wide :, :] = act_ref[...].T
+    dx_ref[...] = jnp.dot(
+        dgu_ref[...], weight_ref[: 2 * wide, :], preferred_element_type=jnp.float32
+    ).astype(jnp.bfloat16)
+
+
+def run_experts(experts, first, x, g, route, eg, eu, ed, sg, su, sd):
+    tokens, width = x.shape
+    local_experts, units, _ = eg.shape
+    wide = -(-(local_experts * units + sg.shape[0]) // 128) * 128
+    rows = 256
+    struct = jax.ShapeDtypeStruct
+
+    def row_block(columns):
+        return pl.BlockSpec((rows, columns), lambda i: (i, 0))
+
+    return pl.pallas_call(
+        functools.partial(expert_kernel, experts),
+        name="experts",
+        grid=(tokens // rows,),
+        in_specs=[
+            pl.BlockSpec(memory_space=pltpu.SMEM),
+            row_block(width),
+            row_block(width),
+            row_block(128),
+        ]
+        + [kept(one.shape) for one in (eg, eu, ed, sg, su, sd)],
+        out_specs=[
+            row_block(wide),
+            pl.BlockSpec((3 * wide, rows), lambda i: (0, i)),
+            row_block(width),
+            row_block(128),
+        ],
+        out_shape=[
+            struct((tokens, wide), jnp.bfloat16),
+            struct((3 * wide, tokens), jnp.bfloat16),
+            struct((tokens, width), jnp.bfloat16),
+            struct((tokens, 128), jnp.bfloat16),
+        ],
+        scratch_shapes=[pltpu.VMEM((3 * wide, width), jnp.bfloat16)]
+        + [pltpu.VMEM((rows, wide), jnp.float32)] * 3
+        + [pltpu.VMEM((rows, 2 * wide), jnp.bfloat16)],
+        compiler_params=pltpu.CompilerParams(vmem_limit_bytes=58 << 20),
+        cost_estimate=pl.CostEstimate(
+            flops=10 * tokens * width * wide, bytes_accessed=50 << 20, transcendentals=2 << 20
+        ),
+    )(first, x, g, route, eg, eu, ed, sg, su, sd)
+
+
+def weight_step(ins, outs, extra):
+    x_ref, g_ref, act_ref, turned_ref, ed_ref, sd_ref = ins
+    eg_ref, eu_ref, edg_ref, shared_ref, sum_ref = outs
+    (wd_ref,) = extra
+    local_experts, units, _ = edg_ref.shape
+    shared_units = shared_ref.shape[1]
+    wide = act_ref.shape[1]
+    taken = local_experts * units
+
+    @pl.when(pl.program_id(0) == 0)
+    def _():
+        wd_ref[...] = jnp.zeros_like(wd_ref)
+
+    def gradient(k, routed, right):
+        part = jnp.dot(
+            turned_ref[k * wide : (k + 1) * wide, :],
+            right[...],
+            preferred_element_type=jnp.float32,
+        )
+        for e in range(local_experts):
+            routed[e] = part[e * units : (e + 1) * units]
+        shared_ref[k] = part[taken : taken + shared_units].astype(jnp.bfloat16)
+
+    @pl.when(lax.rem(pl.program_id(0), 2) == 0)
+    def _():
+        gradient(0, eg_ref, x_ref)
+        gradient(1, eu_ref, x_ref)
+
+    @pl.when(lax.rem(pl.program_id(0), 2) == 1)
+    def _():
+        for e in range(local_experts):
+            wd_ref[e * units : (e + 1) * units, :] = ed_ref[e]
+        wd_ref[taken : taken + shared_units, :] = sd_ref[...]
+        sum_ref[...] = jnp.dot(
+            act_ref[...], wd_ref[...], preferred_element_type=jnp.float32
+        ).astype(jnp.bfloat16)
+        gradient(2, edg_ref, g_ref)
+
+
+SLOTS = (0, 1, 1, 2, 4, 4, 7, 7, 10, 10, 13, 13, 16)
+
+
+def run_weights(x, g, act, turned, ed, sd, tasks, collective_id):
+    tokens, width = x.shape
+    local_experts, units, _ = ed.shape
+    shared_units = sd.shape[0]
+    wide = act.shape[1]
+    columns = 256
+    steps = 2 * (width // columns)
+    struct = jax.ShapeDtypeStruct
+
+    def column(shape):
+        return pl.BlockSpec(shape, lambda i: (0,) * (len(shape) - 1) + (i // 2,))
+
+    ins = [x, g, act, turned, ed, sd]
+    in_specs = [
+        column((tokens, columns)),
+        column((tokens, columns)),
+        kept(act.shape),
+        kept(turned.shape),
+        column((local_experts, units, columns)),
+        column((shared_units, columns)),
+    ]
+    out_specs = [column((local_experts, units, columns))] * 3 + [
+        column((3, shared_units, columns)),
+        column((tokens, columns)),
+    ]
+    out_shape = [struct((local_experts, units, width), jnp.float32)] * 3 + [
+        struct((3, shared_units, width), jnp.bfloat16),
+        struct((tokens, width), jnp.bfloat16),
+    ]
+    scratch = [pltpu.VMEM((wide, columns), jnp.bfloat16)]
+    own = (len(ins), len(out_specs), len(scratch))
+
+    def kernel(*refs):
+        refs = list(refs)
+
+        def take(counts):
+            return [[refs.pop(0) for _ in range(count)] for count in counts]
+
+        inputs = take([own[0]] + [len(task.inputs) for task in tasks])
+        outputs = take([own[1]] + [len(task.outputs) for task in tasks])
+        extra = take([own[2]] + [len(task.scratch) for task in tasks])
+        running = []
+        if tasks:
+            place = Place()
+            running = [
+                task.steps(place, a, b, c)
+                for task, a, b, c in zip(tasks, inputs[1:], outputs[1:], extra[1:])
+            ]
+            for walk in running:
+                next(walk)
+
+        def rounds(slot, step):
+            @pl.when(pl.program_id(0) == step)
+            def _():
+                if slot == 0:
+                    greet(place)
+                for _ in range(SLOTS.count(slot)):
+                    for walk in running:
+                        next(walk, None)
+
+        if running:
+            for slot in sorted(set(SLOTS) - {steps}):
+                rounds(slot, slot)
+        weight_step(inputs[0], outputs[0], extra[0])
+        if running:
+            rounds(steps, steps - 1)
+
+    for task in tasks:
+        for one in task.inputs:
+            ins.append(one)
+            in_specs.append(kept(one.shape))
+        for one in task.outputs:
+            out_shape.append(one)
+            out_specs.append(kept(one.shape))
+        scratch += task.scratch
+    params = {"collective_id": collective_id, "has_side_effects": True} if tasks else {}
+    return pl.pallas_call(
+        kernel,
+        name="weights",
+        grid=(steps,),
+        in_specs=in_specs,
+        out_specs=out_specs,
+        out_shape=out_shape,
+        scratch_shapes=scratch,
+        compiler_params=pltpu.CompilerParams(vmem_limit_bytes=61 << 20, **params),
+        cost_estimate=pl.CostEstimate(
+            flops=8 * tokens * width * wide, bytes_accessed=60 << 20, transcendentals=0
+        ),
+    )(*ins)
 
 
 def shards(
@@ -501,8 +1032,6 @@
     seq_stretch = my_group // stride
     direct = groups == PLANE and parts == DEPTH
 
-    grad_all = gather(out_grad, "dp")
-
     residual_in = tokens.astype(jnp.float32)
     normed_in, inv_one = rms_forward(residual_in, norm_attn_gain)
     normed_low = low(normed_in)
@@ -529,6 +1058,11 @@
         keys_latent = jnp.concatenate(earlier + [own_latent], 0)
         key_pos = (seq_stretch - (SEQ_DEVS - 1)) * tok_rows + jnp.arange(keys_latent.shape[0])
     key_count = keys_latent.shape[0]
+    if direct:
+        late_grad, keys_latent = lax.optimization_barrier((out_grad, keys_latent))
+        grad_all = gather(late_grad, "dp")
+    else:
+        grad_all = gather(out_grad, "dp")
     query = mat_dot(normed_low, query_weight).reshape(tok_rows, head_count, NOPE + ROPE)
     query = (
         jnp.concatenate(
@@ -571,13 +1105,18 @@
         "hqk,khd->qhd", probs_low, expanded[..., NOPE:], preferred_element_type=jnp.float32
     )
     heads_low = low(heads_out.reshape(tok_rows, head_count * VD))
-    attn = mat_dot(heads_low, out_weight)
     if direct:
+        cos_wide = jnp.concatenate([cos_table, cos_table], 1)
+        sin_wide = jnp.concatenate([-sin_table, sin_table], 1)
+        first_row = jnp.full((1,), my_group * tok_rows, jnp.int32)
+        query_kept, expanded_kept, heads_low, log_kept, attn = attend(
+            first_row, normed_low, query_weight, keys_latent, latent_up, out_weight, cos_wide, sin_wide
+        )
         (attn,) = exchange(
-            [ScatterLevels(low(attn).reshape(parts, rows, model_width))], 1, "scatter_attn"
+            [ScatterLevels(attn.reshape(parts, rows, model_width))], 1, "scatter_attn"
         )
     else:
-        attn = scatter(attn, "tensor")
+        attn = scatter(mat_dot(heads_low, out_weight), "tensor")
 
     def own_rows(value):
         return lax.dynamic_slice_in_dim(value, my_part * rows, rows, 0)
@@ -605,106 +1144,143 @@
         )
         ffn_all = ffn_all.reshape(-1, model_width)
         routes = routes.reshape(-1, 128)
+        token_count = routes.shape[0]
+        first_expert = jnp.full((1,), my_group * local_experts, jnp.int32)
+
+        def own_units(value):
+            return lax.dynamic_slice_in_dim(value, my_group * shared_units, shared_units, 0)
+
+        shared_own = own_units(shared_gate.T), own_units(shared_up.T), own_units(shared_down)
+        act_low, turned, ffn_grad, weight_grad = run_experts(
+            experts,
+            first_expert,
+            ffn_all,
+            grad_all,
+            routes,
+            expert_gate.transpose(0, 2, 1),
+            expert_up.transpose(0, 2, 1),
+            expert_down,
+            *shared_own,
+        )
+        (
+            expert_gate_grad,
+            expert_up_grad,
+            expert_down_grad,
+            shared_grads,
+            moe_out,
+            ffn_grad,
+            weight_grad,
+        ) = run_weights(
+            ffn_all,
+            grad_all,
+            act_low,
+            turned,
+            expert_down,
+            shared_own[2],
+            [
+                ScatterPlane(ffn_grad.reshape(groups, parts, rows, model_width), True),
+                ScatterPlane(weight_grad.reshape(groups, parts, rows, 128), True),
+            ],
+            3,
+        )
+        expert_gate_grad = expert_gate_grad.transpose(0, 2, 1)
+        expert_up_grad = expert_up_grad.transpose(0, 2, 1)
+        shared_grads = lax.all_to_all(
+            shared_grads, "dp", split_axis=2, concat_axis=1, tiled=True
+        ).astype(jnp.float32)
+        shared_gate_grad, shared_up_grad = shared_grads[0].T, shared_grads[1].T
+        shared_down_grad = shared_grads[2]
+        weight_grad = weight_grad[:, :experts]
     else:
         ffn_all = gather(jnp.concatenate([ffn_low, routes], 1), BOTH)
         routes = ffn_all[:, model_width:]
         ffn_all = ffn_all[:, :model_width]
-    route_all = routes[:, :experts].astype(jnp.float32) + routes[
-        :, experts : 2 * experts
-    ].astype(jnp.float32)
-    token_count = ffn_all.shape[0]
-    route_own = lax.dynamic_slice_in_dim(route_all, my_group * local_experts, local_experts, 1)
-
-    def joined(expert_weight, shared_weight):
-        own = lax.dynamic_slice_in_dim(shared_weight, my_group * shared_units, shared_units, 1)
-        pieces = [expert_weight[e] for e in range(local_experts)]
-        return jnp.concatenate(
-            pieces + [own, jnp.zeros((model_width, spare_units), jnp.bfloat16)], 1
-        )
-
-    gate_weight = joined(expert_gate, shared_gate)
-    up_weight = joined(expert_up, shared_up)
-    down_weight = jnp.concatenate(
-        [expert_down[e] for e in range(local_experts)]
-        + [
-            lax.dynamic_slice_in_dim(shared_down, my_group * shared_units, shared_units, 0),
-            jnp.zeros((spare_units, model_width), jnp.bfloat16),
-        ],
-        0,
-    )
-    scale = jnp.concatenate(
-        [
-            jnp.broadcast_to(route_own[:, e : e + 1], (token_count, units))
-            for e in range(local_experts)
-        ]
-        + [jnp.ones((token_count, shared_units + spare_units), jnp.float32)],
-        1,
-    )
-    plain_grad = contract_cols(grad_all, down_weight)
-    gate_act = mat_dot(ffn_all, gate_weight)
-    up_act = mat_dot(ffn_all, up_weight)
-    logistic = jax.nn.sigmoid(gate_act)
-    silu = gate_act * logistic
-    act = silu * up_act
-    act_low = low(act * scale)
-    act_grad = plain_grad * scale
-    gate_grad = low(act_grad * up_act * logistic * (1.0 + gate_act * (1.0 - logistic)))
-    up_grad = low(act_grad * silu)
-    weight_dots = act * plain_grad
-    weight_grad = jnp.stack(
-        [
-            jnp.sum(weight_dots[:, e * units : (e + 1) * units], 1)
-            for e in range(local_experts)
-        ],
-        1,
-    )
-    weight_grad = lax.dynamic_update_slice_in_dim(
-        jnp.zeros((token_count, experts), jnp.bfloat16),
-        low(weight_grad),
-        my_group * local_experts,
-        1,
-    )
-    ffn_grad = contract_cols(gate_grad, gate_weight) + contract_cols(up_grad, up_weight)
-    if direct:
-        weight_grad = jnp.pad(weight_grad, ((0, 0), (0, 128 - experts)))
-        ffn_grad, weight_grad = exchange(
+        route_all = routes[:, :experts].astype(jnp.float32) + routes[
+            :, experts : 2 * experts
+        ].astype(jnp.float32)
+        token_count = ffn_all.shape[0]
+        route_own = lax.dynamic_slice_in_dim(route_all, my_group * local_experts, local_experts, 1)
+
+        def joined(expert_weight, shared_weight):
+            own = lax.dynamic_slice_in_dim(shared_weight, my_group * shared_units, shared_units, 1)
+            pieces = [expert_weight[e] for e in range(local_experts)]
+            return jnp.concatenate(
+                pieces + [own, jnp.zeros((model_width, spare_units), jnp.bfloat16)], 1
+            )
+
+        gate_weight = joined(expert_gate, shared_gate)
+        up_weight = joined(expert_up, shared_up)
+        down_weight = jnp.concatenate(
+            [expert_down[e] for e in range(local_experts)]
+            + [
+                lax.dynamic_slice_in_dim(shared_down, my_group * shared_units, shared_units, 0),
+                jnp.zeros((spare_units, model_width), jnp.bfloat16),
+            ],
+            0,
+        )
+        scale = jnp.concatenate(
             [
-                ScatterPlane(low(ffn_grad).reshape(groups, parts, rows, model_width), True),
-                ScatterPlane(weight_grad.reshape(groups, parts, rows, 128), True),
+                jnp.broadcast_to(route_own[:, e : e + 1], (token_count, units))
+                for e in range(local_experts)
+            ]
+            + [jnp.ones((token_count, shared_units + spare_units), jnp.float32)],
+            1,
+        )
+        plain_grad = contract_cols(grad_all, down_weight)
+        gate_act = mat_dot(ffn_all, gate_weight)
+        up_act = mat_dot(ffn_all, up_weight)
+        logistic = jax.nn.sigmoid(gate_act)
+        silu = gate_act * logistic
+        act = silu * up_act
+        act_low = low(act * scale)
+        act_grad = plain_grad * scale
+        gate_grad = low(act_grad * up_act * logistic * (1.0 + gate_act * (1.0 - logistic)))
+        up_grad = low(act_grad * silu)
+        weight_dots = act * plain_grad
+        weight_grad = jnp.stack(
+            [
+                jnp.sum(weight_dots[:, e * units : (e + 1) * units], 1)
+                for e in range(local_experts)
             ],
-            3,
-            "scatter_ffn",
-        )
-        weight_grad = weight_grad[:, :experts]
-    else:
+            1,
+        )
+        weight_grad = lax.dynamic_update_slice_in_dim(
+            jnp.zeros((token_count, experts), jnp.bfloat16),
+            low(weight_grad),
+            my_group * local_experts,
+            1,
+        )
+        ffn_grad = contract_cols(gate_grad, gate_weight) + contract_cols(up_grad, up_weight)
         ffn_grad = scatter(jnp.concatenate([low(ffn_grad), weight_grad], 1), BOTH)
         weight_grad = ffn_grad[:, model_width:]
         ffn_grad = ffn_grad[:, :model_width]
-    moe_out = scatter(scatter(mat_dot(act_low, down_weight), "dp"), "tensor")
+        moe_out = mat_dot(act_low, down_weight)
+
+        down_grad = contract_rows(act_low, grad_all)
+        gate_weight_grad = contract_rows(ffn_all, gate_grad)
+        up_weight_grad = contract_rows(ffn_all, up_grad)
+        expert_down_grad = down_grad[: local_experts * units].reshape(local_experts, units, -1)
+        expert_gate_grad = jnp.stack(
+            [gate_weight_grad[:, e * units : (e + 1) * units] for e in range(local_experts)]
+        )
+        expert_up_grad = jnp.stack(
+            [up_weight_grad[:, e * units : (e + 1) * units] for e in range(local_experts)]
+        )
+
+        def swap(value):
+            return lax.all_to_all(low(value), "dp", split_axis=0, concat_axis=1, tiled=True).astype(
+                jnp.float32
+            )
+
+        first = local_experts * units
+        shared_gate_grad = swap(gate_weight_grad[:, first:used_units])
+        shared_up_grad = swap(up_weight_grad[:, first:used_units])
+        shared_down_grad = lax.all_to_all(
+            low(down_grad[first:used_units]), "dp", split_axis=1, concat_axis=0, tiled=True
+        ).astype(jnp.float32)
+
+    moe_out = scatter(scatter(moe_out, "dp"), "tensor")
     block_out = gather(low(hidden + moe_out), "tensor")
-
-    down_grad = contract_rows(act_low, grad_all)
-    gate_weight_grad = contract_rows(ffn_all, gate_grad)
-    up_weight_grad = contract_rows(ffn_all, up_grad)
-    expert_down_grad = down_grad[: local_experts * units].reshape(local_experts, units, -1)
-    expert_gate_grad = jnp.stack(
-        [gate_weight_grad[:, e * units : (e + 1) * units] for e in range(local_experts)]
-    )
-    expert_up_grad = jnp.stack(
-        [up_weight_grad[:, e * units : (e + 1) * units] for e in range(local_experts)]
-    )
-
-    def swap(value):
-        return lax.all_to_all(low(value), "dp", split_axis=0, concat_axis=1, tiled=True).astype(
-            jnp.float32
-        )
-
-    first = local_experts * units
-    shared_gate_grad = swap(gate_weight_grad[:, first:used_units])
-    shared_up_grad = swap(up_weight_grad[:, first:used_units])
-    shared_down_grad = lax.all_to_all(
-        low(down_grad[first:used_units]), "dp", split_axis=1, concat_axis=0, tiled=True
-    ).astype(jnp.float32)
 
     inner_sum = jnp.sum(weight_grad * chosen, -1, keepdims=True)
     chosen_grad = route_scale * (weight_grad / chosen_sum - inner_sum / (chosen_sum * chosen_sum))
@@ -724,43 +1300,57 @@
         attn_grad_low = gather(low(hidden_grad), "tensor")
 
     out_weight_grad = scatter(contract_rows(heads_low, attn_grad_low), "dp", 1)
-    heads_grad = low(contract_cols(attn_grad_low, out_weight)).reshape(tok_rows, head_count, VD)
-    attn_probs = jnp.exp(attention_scores() - log_total)
-    probs_low = low(attn_probs)
-    value_grad = jnp.einsum(
-        "hqk,qhd->khd", probs_low, heads_grad, preferred_element_type=jnp.float32
-    )
-    prob_grad = jnp.einsum(
-        "qhd,khd->hqk", heads_grad, expanded[..., NOPE:], preferred_element_type=jnp.float32
-    )
-    row_delta = jnp.sum(attn_probs * prob_grad, -1, keepdims=True)
-    score_grad = low(attn_probs * (prob_grad - row_delta))
-    nope_grad = jnp.einsum(
-        "hqk,khd->qhd", score_grad, expanded[..., :NOPE], preferred_element_type=jnp.float32
-    )
-    rope_grad = jnp.einsum(
-        "hqk,kd->qhd", score_grad, keys_latent[:, R:], preferred_element_type=jnp.float32
-    )
-    key_nope_grad = jnp.einsum(
-        "hqk,qhd->khd", score_grad, query_low[..., :NOPE], preferred_element_type=jnp.float32
-    )
-    key_rope_grad = jnp.einsum(
-        "hqk,qhd->kd", score_grad, query_low[..., NOPE:], preferred_element_type=jnp.float32
-    )
-    expand_grad = low(
-        jnp.concatenate([key_nope_grad, value_grad], -1).reshape(
-            key_count, head_count * (NOPE + VD)
-        )
-    )
-    latent_up_grad = contract_rows(keys_latent[:, :R], expand_grad)
-    latent_grad = jnp.concatenate([contract_cols(expand_grad, latent_up), key_rope_grad], -1)
-    query_grad = (
-        jnp.concatenate(
-            [nope_grad, unrotate(rope_grad, cos_table[:, None, :], sin_table[:, None, :])], -1
-        )
-        * factor
-    )
-    query_grad_low = low(query_grad.reshape(tok_rows, head_count * (NOPE + ROPE)))
+    if direct:
+        query_grad_low, latent_up_grad, latent_grad = attend_back(
+            first_row,
+            query_kept,
+            expanded_kept,
+            keys_latent,
+            log_kept,
+            attn_grad_low,
+            out_weight,
+            latent_up,
+            cos_wide,
+            sin_wide,
+        )
+    else:
+        heads_grad = low(contract_cols(attn_grad_low, out_weight)).reshape(tok_rows, head_count, VD)
+        attn_probs = jnp.exp(attention_scores() - log_total)
+        probs_low = low(attn_probs)
+        value_grad = jnp.einsum(
+            "hqk,qhd->khd", probs_low, heads_grad, preferred_element_type=jnp.float32
+        )
+        prob_grad = jnp.einsum(
+            "qhd,khd->hqk", heads_grad, expanded[..., NOPE:], preferred_element_type=jnp.float32
+        )
+        row_delta = jnp.sum(attn_probs * prob_grad, -1, keepdims=True)
+        score_grad = low(attn_probs * (prob_grad - row_delta))
+        nope_grad = jnp.einsum(
+            "hqk,khd->qhd", score_grad, expanded[..., :NOPE], preferred_element_type=jnp.float32
+        )
+        rope_grad = jnp.einsum(
+            "hqk,kd->qhd", score_grad, keys_latent[:, R:], preferred_element_type=jnp.float32
+        )
+        key_nope_grad = jnp.einsum(
+            "hqk,qhd->khd", score_grad, query_low[..., :NOPE], preferred_element_type=jnp.float32
+        )
+        key_rope_grad = jnp.einsum(
+            "hqk,qhd->kd", score_grad, query_low[..., NOPE:], preferred_element_type=jnp.float32
+        )
+        expand_grad = low(
+            jnp.concatenate([key_nope_grad, value_grad], -1).reshape(
+                key_count, head_count * (NOPE + VD)
+            )
+        )
+        latent_up_grad = contract_rows(keys_latent[:, :R], expand_grad)
+        latent_grad = jnp.concatenate([contract_cols(expand_grad, latent_up), key_rope_grad], -1)
+        query_grad = (
+            jnp.concatenate(
+                [nope_grad, unrotate(rope_grad, cos_table[:, None, :], sin_table[:, None, :])], -1
+            )
+            * factor
+        )
+        query_grad_low = low(query_grad.reshape(tok_rows, head_count * (NOPE + ROPE)))
     query_weight_grad = contract_rows(normed_low, query_grad_low)
     input_part = contract_cols(query_grad_low, query_weight)
     if direct:

time: 735 us -> 686 us (0.933); the launches traced: 724 us -> 684 us
  matrix products: 194 us -> 19.1 us
  Pallas kernels: 319 us -> 467 us
  waiting for transfers between devices: 2.78 us -> 90.2 us
  local copies, waits for them, and re-layouts: 116 us -> 60.7 us
  other arithmetic: 64 us -> 28.5 us
  starting transfers between devices: 12.4 us -> 4.14 us
    pallas_call x0 -> x4, Pallas kernels: none -> 202 us  [the longest x1 70.3 us: run_weights(): pl.pallas_call(kernel, name='weights', grid=(steps,), in_specs=in_specs,...]
    reduce_scatter x3, waiting for transfers between devices: 0.01 us -> 69.6 us  [scatter(): lax.psum_scatter(low(value), axes, scatter_dimension=dimension, tiled=True)]
    dot_general x7 -> x2, matrix products: 70.2 us -> 5.76 us  [contract_cols(): lax.dot_general(left, right, (((1,), (1,)), ((), ())), preferred_element_...]
    pallas_call x7 -> x6, Pallas kernels: 319 us -> 266 us  [exchange(): pl.pallas_call(kernel, name=name, out_shape=flat((task.outputs for task i...]
    dot_general x7 -> x1, matrix products: 50.3 us -> 0.81 us  [mat_dot(): return jnp.dot(left, right, preferred_element_type=jnp.float32)]
    dot_general x7 -> x3, matrix products: 43.7 us -> 8.29 us  [contract_rows(): lax.dot_general(left, right, (((0,), (0,)), ((), ())), preferred_element_...]
    dot_general x9 -> x0, matrix products: 24.9 us -> none  [the longest x1 6.46 us: shards(): jnp.einsum('hqk,qhd->khd', probs_low, heads_grad, preferred_element_type=...]
    all_to_all x3 -> x1, waiting for transfers between devices: 2 us -> 20.5 us  [shards(): lax.all_to_all(shared_grads, 'dp', split_axis=2, concat_axis=1, tiled=True)]
  transfers between devices with their start and end apart: 8 -> 6, of which waited for: 1 -> 2; matrix products, arithmetic and copies ran while one was open for 39% -> 9% of each run, Pallas kernels for 41% -> 45%
where the time goes in v2:
time: 686 us; the launch traced here: 684 us
  Pallas kernels  467 us (68%)
  waiting for transfers between devices  90.2 us (13%)
  local copies, waits for them, and re-layouts  60.7 us (9%)
  other arithmetic  28.5 us (4%)
  matrix products  19.1 us (3%)
  between operations  14.4 us (2%)
    pallas_call x6, Pallas kernels, exchange(): pl.pallas_call(kernel, name=name, out_shape=flat((task.outputs for task i...  266 us
    pallas_call x1, Pallas kernels, run_weights(): pl.pallas_call(kernel, name='weights', grid=(steps,), in_specs=in_specs,...  70.3 us
    reduce_scatter x3, waiting for transfers between devices, scatter(): lax.psum_scatter(low(value), axes, scatter_dimension=dimension, tiled=True)  69.6 us
    pallas_call x1, Pallas kernels, run_experts(): pl.pallas_call(functools.partial(expert_kernel, experts), name='experts',...  66.2 us
    pallas_call x1, Pallas kernels, attend_back(): pl.pallas_call(attend_back_kernel, name='attend_back', grid=(heads // 2,)...  37.8 us
    unnamed x104, local copies, waits for them, and re-layouts  32.2 us
    pallas_call x1, Pallas kernels, attend(): pl.pallas_call(attend_kernel, name='attend', grid=(heads // 2,), in_specs...  27.5 us
    all_to_all x1, waiting for transfers between devices, shards(): lax.all_to_all(shared_grads, 'dp', split_axis=2, concat_axis=1, tiled=True)  20.5 us
  transfers between devices with their start and end apart: 6, of which 2 were waited for; matrix products, arithmetic and copies ran while one was open for 9% of the time, Pallas kernels for 45%

profile of v2, /device:TPU:0, one launch (start us, length us, event | category | flops | bytes accessed | tf_op | source)
XLA Modules:
  0.0 684.2 jit_solution(5123492270740892189)
XLA Ops:
  17.3 2.3 fusion.10
  21.3 23.0 %gather_keys.1 = bf16[8,2,128,576]{3,2,1,0:T(8,128)(2,1)} custom-call(bf16[2,128,576]{2,1,0:T(8,128)(2,1)} %pad_maximum_fusion.refs_0_), custom_call_target="tpu_custom_call" | custom-call | bytes 1179648 | tf_op jit(solution)/shard_map/gather_keys/pallas_call | solution.py:463
  44.7 2.8 convert_element_type.93
  51.9 27.5 %attend.1 = (bf16[256,1024]{1,0:T(8,128)(2,1)S(1)}, bf16[2048,1024]{1,0:T(8,128)(2,1)}, bf16[256,512]{1,0:T(8,128)(2,1)S(1)}, f32[256,512]{1,0:T(8,128)S(1)}, bf16[256,2048]{1,0:T(8,128)(2,1)S(1)}) custom-call(s32[1]{0:T(128)} %bitcast.base_ref, bf16[256,2048]{1,0:T(8,128)(2,1)S(1)} %copy-done.3, bf16[2048,768]{1,0:T(8,128)(2,1)} %wq_ref.1, ...), custom_call_target="tpu_custom_call" | custom-call | flops 7000000000 | bytes 20971520 | tf_op jit(solution)/shard_map/attend/pallas_call | solution.py:589
  82.6 24.1 %scatter_attn.1 = f32[64,2048]{1,0:T(8,128)} custom-call(bf16[4,64,2048]{2,1,0:T(8,128)(2,1)} %bitcast.67), custom_call_target="tpu_custom_call" | custom-call | bytes 4194304 | tf_op jit(solution)/shard_map/scatter_attn/pallas_call | solution.py:463
  110.8 54.6 %gather_ffn.1 = (bf16[8,4,64,2048]{3,2,1,0:T(8,128)(2,1)}, bf16[8,4,64,128]{3,2,1,0:T(8,128)(2,1)}) custom-call(bf16[64,2048]{1,0:T(8,128)(2,1)} %fusion.4.refs_0_, bf16[64,128]{1,0:T(8,128)(2,1)} %fusion.20.refs_1_), custom_call_target="tpu_custom_call" | custom-call | bytes 1114112 | tf_op jit(solution)/shard_map/gather_ffn/pallas_call | solution.py:463
  166.2 2.0 dynamic-slice_bitcast_fusion
  168.3 66.2 %experts.1 = (bf16[2048,896]{1,0:T(8,128)(2,1)}, bf16[2688,2048]{1,0:T(8,128)(2,1)}, bf16[2048,2048]{1,0:T(8,128)(2,1)}, bf16[2048,128]{1,0:T(8,128)(2,1)}) custom-call(s32[1]{0:T(128)} %bitcast.7.first_ref, bf16[2048,2048]{1,0:T(8,128)(2,1)} %bitcast.94, bf16[2048,2048]{1,0:T(8,128)(2,1)} %all-gather.3.cloned.1.call-done.g_ref.refs_1_, ...), custom_call_target="tpu_custom_call" | custom-call | flops 37580963840 | bytes 52428800 | tf_op jit(solution)/shard_map/experts/pallas_call | solution.py:834
  234.5 70.3 %weights.1 = (f32[2,352,2048]{2,1,0:T(8,128)}, f32[2,352,2048]{2,1,0:T(8,128)}, f32[2,352,2048]{2,1,0:T(8,128)}, bf16[3,88,2048]{2,1,0:T(8,128)(2,1)}, bf16[2048...) custom-call(bf16[2048,2048]{1,0:T(8,128)(2,1)} %bitcast.95, ...), custom_call_target="tpu_custom_call" | custom-call | flops 30064771072 | bytes 62914560 | tf_op jit(solution)/shard_map/weights/pallas_call | solution.py:985
  306.0 69.6 %reduce-scatter.4.cloned.1.call-done = bf16[256,2048]{1,0:T(8,128)(2,1)} async-done(((bf16[2048,2048]{1,0:T(8,128)(2,1)}), bf16[256,2048]{1,0:T(8,128)(2,1)}) %reduce-scatter.4.cloned.1.call-update) | async-done | bytes 1048592 | tf_op jit(solution)/shard_map/reduce_scatter | solution.py:90
  377.0 2.5 copy.94
  379.5 3.7 all-to-all-start
  383.5 2.5 multiply_reduce_fusion.2
  389.4 20.5 %all-to-all-done = bf16[3,88,2048]{1,0,2:T(4,128)(2,1)S(1)} async-done(((bf16[3,88,2048]{1,0,2:T(4,128)(2,1)}), bf16[3,88,2048]{1,0,2:T(4,128)(2,1)S(1)}, u32[]{:S(2)}, u32[]{:S(2)}) %all-to-all-start) | async-done | bytes 1081376 | tf_op jit(solution)/shard_map/all_to_all | solution.py:1188
  410.1 3.3 fusion.28
  413.4 3.6 copy.97
  420.5 2.1 fusion.27
  422.7 35.5 %gather_hidden.1 = bf16[4,64,2048]{2,1,0:T(8,128)(2,1)} custom-call(bf16[64,2048]{1,0:T(8,128)(2,1)} %get-tuple-element.166.refs_0_), custom_call_target="tpu_custom_call" | custom-call | bytes 1048576 | tf_op jit(solution)/shard_map/gather_hidden/pallas_call | solution.py:463
  458.2 3.3 convolution_convert_fusion.2
  461.5 37.8 %attend_back.1 = (bf16[256,768]{1,0:T(8,128)(2,1)}, bf16[512,1024]{1,0:T(8,128)(2,1)}, bf16[2048,576]{1,0:T(8,128)(2,1)}) custom-call(s32[1]{0:T(128)} %bitcast.base_ref, bf16[256,1024]{1,0:T(8,128)(2,1)} %copy-done.11, bf16[2048,1024]{1,0:T(8,128)(2,1)} %get-tuple-element.57.kv_ref, bf16[2048,576]{1,0:T(8,128)(2,1)} %bitcast.78, f32[256,512]{1,0:T(8,128)} %copy-done.12, ...), custom_call_target="tpu_custom_call" | custom-call | flops 10000000000 | bytes 20971520 | tf_op jit(solution)/shard_map/attend_back/pallas_call | solution.py:713
  499.3 3.1 convolution_convert_fusion.3
  502.5 2.7 convolution_convert_fusion
  505.2 73.0 %scatter_latent.1 = (f32[64,576]{1,0:T(8,128)}, f32[64,2048]{1,0:T(8,128)}, f32[2,128,768]{2,1,0:T(8,128)}, f32[2,32,1024]{2,1,0:T(8,128)}) custom-call(bf16[4,2,4,64,576]{4,3,2,1,0:T(8,128)(2,1)} %bitcast.79, bf16[4,64,2048]{2,1,0:T(8,128)(2,1)} %bitcast.81, bf16[4,2,2,128,768]{4,3,2,1,0:T(8,128)(2,1)} %bitcast.68, bf16[4,2,2,32,1024]{4,3,2,1,0:T(8,128)(2,1)} %bitcast.80), custom_call_target="tpu_custom_call" | custom-call | bytes 30408704 | tf_op jit(solution)/shard_map/scatter_latent/pallas_call | solution.py:463
  581.4 2.6 multiply_reduce_fusion.1
  584.8 2.3 convolution_convert_fusion.1
  587.1 4.3 copy.92
  591.4 1.9 add_convert_fusion.refs_2_
  593.4 55.4 %scatter_last.1 = (bf16[4,64,576]{2,1,0:T(8,128)(2,1)}, bf16[4,16,128]{2,1,0:T(8,128)(2,1)}, bf16[4,64,2048]{2,1,0:T(8,128)(2,1)}) custom-call(bf16[4,2,4,64,576]{4,3,2,1,0:T(8,128)(2,1)} %bitcast.69, bf16[4,2,4,16,128]{4,3,2,1,0:T(8,128)(2,1)} %bitcast.88, bf16[64,2048]{1,0:T(8,128)(2,1)} %add_convert_fusion.refs_2_), custom_call_target="tpu_custom_call" | custom-call | bytes 11010048 | tf_op jit(solution)/shard_map/scatter_last/pallas_call | solution.py:463
  656.8 2.3 copy.114
  661.7 6.0 copy.118
  667.8 6.0 copy.119
  673.8 2.9 copy.120
  (165 shorter events, 50.2 us)
Async XLA Ops:
  7.2 158.3 %copy-start = (bf16[704,2048]{1,0:T(8,128)(2,1)S(1)}, bf16[704,2048]{1,0:T(8,128)(2,1)}, u32[]{:S(2)}) copy-start(bf16[704,2048]{1,0:T(8,128)(2,1)} %param.28) | copy-start | bytes 8650756
  7.2 161.1 %all-gather.3.cloned.1.call-start = ((), (), s32[]{:S(2)}) async-start(), calls=%async_computation.4 | async-start | bytes 9437184 | tf_op jit(solution)/shard_map/all_gather | solution.py:86
  13.0 31.4 %copy-start.15 = (f32[256,576]{0,1:T(8,128)}, f32[256,576]{0,1:T(8,128)S(1)}, u32[]{:S(2)}) copy-start(f32[256,576]{0,1:T(8,128)S(1)} %fusion.32) | copy-start | bytes 1769476
  13.1 31.3 %copy-start.35 = (f32[256]{0:T(256)}, f32[256]{0:T(256)S(1)}, u32[]{:S(2)}) copy-start(f32[256]{0:T(256)S(1)} %add_rsqrt_fusion) | copy-start | bytes 3076
  21.3 26.1 %copy-start.40 = (s32[256,6]{0,1:T(8,128)S(1)}, s32[256,6]{0,1:T(8,128)}, u32[]{:S(2)}) copy-start(s32[256,6]{0,1:T(8,128)} %param.32) | copy-start | bytes 18436
  44.4 331.2 %reduce-scatter.4.cloned.1.call-start = ((), (), s32[]{:S(2)}) async-start(), calls=%async_computation.5 | async-start | bytes 9437184 | tf_op jit(solution)/shard_map/reduce_scatter | solution.py:90
  49.0 30.4 %copy-start.8 = (f32[256,64]{1,0:T(8,128)}, f32[256,64]{1,0:T(8,128)S(1)}, u32[]{:S(2)}) copy-start(f32[256,64]{1,0:T(8,128)S(1)} %get-tuple-element.195.cos_ref) | copy-start | bytes 196612
  49.0 30.3 %copy-start.9 = (f32[256,64]{1,0:T(8,128)}, f32[256,64]{1,0:T(8,128)S(1)}, u32[]{:S(2)}) copy-start(f32[256,64]{1,0:T(8,128)S(1)} %get-tuple-element.196.sin_ref) | copy-start | bytes 196612
  82.6 26.0 %copy-start.25 = (bf16[2048,16]{0,1:T(8,128)(2,1)S(1)}, bf16[2048,16]{0,1:T(8,128)(2,1)}, u32[]{:S(2)}) copy-start(bf16[2048,16]{0,1:T(8,128)(2,1)} %param.25) | copy-start | bytes 196612
  82.6 26.0 %copy-start.27 = (f32[2048]{0:T(1024)S(1)}, f32[2048]{0:T(1024)}, u32[]{:S(2)}) copy-start(f32[2048]{0:T(1024)} %param.24) | copy-start | bytes 24580
  108.6 274.8 %copy-start.30 = (f32[64]{0:T(128)}, f32[64]{0:T(128)S(1)}, u32[]{:S(2)}) copy-start(f32[64]{0:T(128)S(1)} %get-tuple-element.190) | copy-start | bytes 772
  109.2 125.3 %copy-start.31 = (f32[64]{0:T(128)}, f32[64]{0:T(128)S(1)}, u32[]{:S(2)}) copy-start(f32[64]{0:T(128)S(1)} %get-tuple-element.191) | copy-start | bytes 772
  304.8 70.9 %copy-start.34 = (f32[256]{0:T(256)S(1)}, f32[256]{0:T(256)}, u32[]{:S(2)}) copy-start(f32[256]{0:T(256)} %copy-done.33) | copy-start | bytes 3076
  304.8 71.7 %copy-start.36 = (f32[256]{0:T(256)S(1)}, f32[256]{0:T(256)}, u32[]{:S(2)}) copy-start(f32[256]{0:T(256)} %copy-done.35) | copy-start | bytes 3076
  304.8 72.3 %copy-start.18 = (bf16[3,88,2048]{2,1,0:T(8,128)(2,1)S(1)}, bf16[3,88,2048]{2,1,0:T(8,128)(2,1)}, u32[]{:S(2)}) copy-start(bf16[3,88,2048]{2,1,0:T(8,128)(2,1)} %get-tuple-element.72) | copy-start | bytes 3244036
  304.8 115.7 %reduce-scatter.6.cloned.1.call-start = ((), (), s32[]{:S(2)}) async-start(), calls=%async_computation.6 | async-start | bytes 1310720 | tf_op jit(solution)/shard_map/reduce_scatter | solution.py:90
  379.5 30.3 %all-to-all-start = ((bf16[3,88,2048]{1,0,2:T(4,128)(2,1)}), bf16[3,88,2048]{1,0,2:T(4,128)(2,1)S(1)}, u32[]{:S(2)}, u32[]{:S(2)}) async-start(bf16[3,88,2048]{1,0,2:T(4,128)(2,1)} %copy.94), calls=%async_computation.3 | async-start | bytes 4194304 | tf_op jit(solution)/shard_map/all_to_all | solution.py:1188
  383.3 271.8 %all-gather.5.cloned.1.call-start = ((), (), s32[]{:S(2)}) async-start(), calls=%async_computation.7 | async-start | bytes 1310720 | tf_op jit(solution)/shard_map/all_gather | solution.py:86
  413.4 7.2 %copy-start.17 = (f32[64,2048]{1,0:T(8,128)S(1)}, f32[64,2048]{1,0:T(8,128)}, u32[]{:S(2)}) copy-start(f32[64,2048]{1,0:T(8,128)} %get-tuple-element.193) | copy-start | bytes 1572868
  418.7 39.4 %copy-start.7 = (bf16[256,512]{1,0:T(8,128)(2,1)S(1)}, bf16[256,512]{1,0:T(8,128)(2,1)}, u32[]{:S(2)}) copy-start(bf16[256,512]{1,0:T(8,128)(2,1)} %copy-done.6) | copy-start | bytes 786436
  422.6 232.4 %reduce-scatter.8.cloned.1.call-start = ((), (), s32[]{:S(2)}) async-start(), calls=%async_computation.8 | async-start | bytes 2359296 | tf_op jit(solution)/shard_map/reduce_scatter | solution.py:90
  461.5 37.8 %copy-start.42 = (bf16[2048,768]{1,0:T(8,128)(2,1)S(1)}, bf16[2048,768]{1,0:T(8,128)(2,1)}, u32[]{:S(2)}) copy-start(bf16[2048,768]{1,0:T(8,128)(2,1)} %wq_ref.1) | copy-start | bytes 9437188
  505.2 73.0 %copy-start.38 = (f32[64]{0:T(128)S(1)}, f32[64]{0:T(128)}, u32[]{:S(2)}) copy-start(f32[64]{0:T(128)} %get-tuple-element.165) | copy-start | bytes 772
  505.2 75.1 %copy-start.41 = (f32[64]{0:T(128)S(1)}, f32[64]{0:T(128)}, u32[]{:S(2)}) copy-start(f32[64]{0:T(128)} %get-tuple-element.164) | copy-start | bytes 772
  505.2 76.2 %copy-start.28 = (f32[2048]{0:T(1024)S(1)}, f32[2048]{0:T(1024)}, u32[]{:S(2)}) copy-start(f32[2048]{0:T(1024)} %param.18) | copy-start | bytes 24580
  505.2 76.2 %copy-start.37 = (f32[64]{0:T(128)S(1)}, f32[64]{0:T(128)}, u32[]{:S(2)}) copy-start(f32[64]{0:T(128)} %get-tuple-element.163) | copy-start | bytes 772
  578.1 5.9 copy-start.23
  587.1 4.3 copy-start.39
  648.8 10.4 %copy-start.19 = (bf16[4,64,2048]{2,1,0:T(8,128)(2,1)S(1)}, bf16[4,64,2048]{2,1,0:T(8,128)(2,1)}, u32[]{:S(2)}) copy-start(bf16[4,64,2048]{2,1,0:T(8,128)(2,1)} %get-tuple-element.66) | copy-start | bytes 3145732
  652.6 7.5 %copy-start.20 = (f32[2,128,768]{2,1,0:T(8,128)S(1)}, f32[2,128,768]{2,1,0:T(8,128)}, u32[]{:S(2)}) copy-start(f32[2,128,768]{2,1,0:T(8,128)} %get-tuple-element.68) | copy-start | bytes 2359300
  661.7 12.0 %slice-start = ((s8[5767168]{0:T(1024)(128)(4,1)}), s8[4194304]{0:T(1024)(128)(4,1)S(1)}, s32[]{:S(2)}) async-start(s8[5767168]{0:T(1024)(128)(4,1)} %bitcast.71), calls=%async_computation.9 | async-start | bytes 8388608
  667.8 6.0 slice-start.1
  (19 other events, 49.0 us)
Sparse Core Ops, SparseCore 0:
  44.6 51.5 all-gather.2
  304.9 70.6 reduce-scatter.3
  377.9 27.2 reduce-scatter.5
  422.7 44.3 all-gather.4
  502.6 54.9 reduce-scatter.7

commit v3 on v2

--- a/solution.py
+++ b/solution.py
@@ -884,7 +884,7 @@
             preferred_element_type=jnp.float32,
         )
         for e in range(local_experts):
-            routed[e] = part[e * units : (e + 1) * units]
+            routed[e] = part[e * units : (e + 1) * units].astype(jnp.bfloat16)
         shared_ref[k] = part[taken : taken + shared_units].astype(jnp.bfloat16)
 
     @pl.when(lax.rem(pl.program_id(0), 2) == 0)
@@ -931,7 +931,7 @@
         column((3, shared_units, columns)),
         column((tokens, columns)),
     ]
-    out_shape = [struct((local_experts, units, width), jnp.float32)] * 3 + [
+    out_shape = [struct((local_experts, units, width), jnp.bfloat16)] * 3 + [
         struct((3, shared_units, width), jnp.bfloat16),
         struct((tokens, width), jnp.bfloat16),
     ]
@@ -1183,13 +1183,12 @@
             ],
             3,
         )
-        expert_gate_grad = expert_gate_grad.transpose(0, 2, 1)
-        expert_up_grad = expert_up_grad.transpose(0, 2, 1)
+        expert_gate_grad = expert_gate_grad.transpose(0, 2, 1).astype(jnp.float32)
+        expert_up_grad = expert_up_grad.transpose(0, 2, 1).astype(jnp.float32)
+        expert_down_grad = expert_down_grad.astype(jnp.float32)
         shared_grads = lax.all_to_all(
             shared_grads, "dp", split_axis=2, concat_axis=1, tiled=True
-        ).astype(jnp.float32)
-        shared_gate_grad, shared_up_grad = shared_grads[0].T, shared_grads[1].T
-        shared_down_grad = shared_grads[2]
+        )
         weight_grad = weight_grad[:, :experts]
     else:
         ffn_all = gather(jnp.concatenate([ffn_low, routes], 1), BOTH)
@@ -1279,8 +1278,7 @@
             low(down_grad[first:used_units]), "dp", split_axis=1, concat_axis=0, tiled=True
         ).astype(jnp.float32)
 
-    moe_out = scatter(scatter(moe_out, "dp"), "tensor")
-    block_out = gather(low(hidden + moe_out), "tensor")
+    moe_out = lax.psum_scatter(low(moe_out), "dp", scatter_dimension=0, tiled=True)
 
     inner_sum = jnp.sum(weight_grad * chosen, -1, keepdims=True)
     chosen_grad = route_scale * (weight_grad / chosen_sum - inner_sum / (chosen_sum * chosen_sum))
@@ -1313,6 +1311,12 @@
             cos_wide,
             sin_wide,
         )
+        moe_out, shared_grads, _ = lax.optimization_barrier(
+            (moe_out, shared_grads, query_grad_low)
+        )
+        shared_grads = shared_grads.astype(jnp.float32)
+        shared_gate_grad, shared_up_grad = shared_grads[0].T, shared_grads[1].T
+        shared_down_grad = shared_grads[2]
     else:
         heads_grad = low(contract_cols(attn_grad_low, out_weight)).reshape(tok_rows, head_count, VD)
         attn_probs = jnp.exp(attention_scores() - log_total)
@@ -1351,21 +1355,18 @@
             * factor
         )
         query_grad_low = low(query_grad.reshape(tok_rows, head_count * (NOPE + ROPE)))
+    block_out = low(hidden + scatter(moe_out, "tensor"))
     query_weight_grad = contract_rows(normed_low, query_grad_low)
     input_part = contract_cols(query_grad_low, query_weight)
     if direct:
-        own_grad, input_sum, query_weight_grad, latent_up_grad = exchange(
+        own_grad, input_sum = exchange(
             [
                 ScatterPlane(low(latent_grad).reshape(groups, parts, rows, R + ROPE), True),
                 ScatterLevels(low(input_part).reshape(parts, rows, model_width)),
-                ScatterPlane(low(query_weight_grad).reshape(groups, 2, model_width // 16, -1), False),
-                ScatterPlane(low(latent_up_grad).reshape(groups, 2, R // 16, -1), False),
             ],
             5,
             "scatter_latent",
         )
-        query_weight_grad = query_weight_grad.reshape(model_width // groups, -1)
-        latent_up_grad = latent_up_grad.reshape(R // groups, -1)
     else:
         if stride == 1:
             own_grad = scatter(scatter(latent_grad, "dp"), "tensor")
@@ -1400,24 +1401,38 @@
     small = jnp.concatenate([one.reshape(groups, -1) for one in small], 1)
     if direct:
         small = jnp.pad(low(small), ((0, 0), (0, parts * 2048 - small.shape[1])))
-        latent_down_grad, small, tokens_grad = exchange(
+        (
+            latent_down_grad,
+            small,
+            tokens_grad,
+            query_weight_grad,
+            latent_up_grad,
+            block_out,
+        ) = exchange(
             [
                 ScatterPlane(
                     low(latent_down_grad).reshape(groups, parts, rows, R + ROPE), True, True
                 ),
                 ScatterPlane(small.reshape(groups, parts, 16, 128), True, True),
                 GatherLevels(tokens_grad),
+                ScatterPlane(low(query_weight_grad).reshape(groups, 2, model_width // 16, -1), False),
+                ScatterPlane(low(latent_up_grad).reshape(groups, 2, R // 16, -1), False),
+                GatherLevels(block_out),
             ],
             6,
             "scatter_last",
         )
         latent_down_grad = latent_down_grad.reshape(-1, R + ROPE).astype(jnp.float32)
         small = small.reshape(-1).astype(jnp.float32)
+        query_weight_grad = query_weight_grad.reshape(model_width // groups, -1)
+        latent_up_grad = latent_up_grad.reshape(R // groups, -1)
+        block_out = block_out.reshape(tok_rows, model_width)
         tokens_grad = tokens_grad.reshape(tok_rows, model_width)
     else:
         latent_down_grad = lax.psum(scatter(latent_down_grad, "dp"), "tensor")
         small = lax.psum(scatter(small, "dp"), "tensor").reshape(-1)
         tokens_grad = gather(tokens_grad, "tensor")
+        block_out = gather(block_out, "tensor")
     offsets = [sum(sizes[:k]) for k in range(len(sizes))]
     norm_attn_grad, latent_gain_grad, norm_ffn_grad, router_grad = [
         small[start : start + size] for start, size in zip(offsets, sizes)

time: 686 us -> 601 us (0.88)
  waiting for transfers between devices: 90.2 us -> 12.9 us
  local copies, waits for them, and re-layouts: 60.7 us -> 42 us
  other arithmetic: 28.5 us -> 43.4 us
    reduce_scatter x3 -> x2, waiting for transfers between devices: 69.6 us -> 12.8 us  [scatter(): lax.psum_scatter(low(value), axes, scatter_dimension=dimension, tiled=True)]
    all_to_all x1, waiting for transfers between devices: 20.5 us -> 0.01 us  [shards(): lax.all_to_all(shared_grads, 'dp', split_axis=2, concat_axis=1, tiled=True)]
    convert_element_type x1 -> x4, other arithmetic: 0.27 us -> 15.2 us  [the longest x1 5.27 us: shards(): expert_gate_grad = expert_gate_grad.transpose(0, 2, 1).astype(jnp.float32)]
    unnamed x104 -> x73, local copies, waits for them, and re-layouts: 32.2 us -> 17.6 us
    slice x4 -> x0, local copies, waits for them, and re-layouts: 10.4 us -> none  [the longest x2 6.82 us: shards(): shared_down_grad = shared_grads[2]]
  transfers between devices with their start and end apart: 6 -> 5, of which waited for: 2 -> 1; matrix products, arithmetic and copies ran while one was open for 9% -> 11% of each run, Pallas kernels for 45% -> 36%
where the time goes in v3:
time: 601 us; the launch traced here: 600 us
  Pallas kernels  468 us (78%)
  other arithmetic  43.4 us (7%)
  local copies, waits for them, and re-layouts  42 us (7%)
  matrix products  14.5 us (2%)
  between operations  14.3 us (2%)
  waiting for transfers between devices  12.9 us (2%)
    pallas_call x6, Pallas kernels, exchange(): pl.pallas_call(kernel, name=name, out_shape=flat((task.outputs for task i...  266 us
    pallas_call x1, Pallas kernels, run_weights(): pl.pallas_call(kernel, name='weights', grid=(steps,), in_specs=in_specs,...  70.2 us
    pallas_call x1, Pallas kernels, run_experts(): pl.pallas_call(functools.partial(expert_kernel, experts), name='experts',...  66 us
    pallas_call x1, Pallas kernels, attend_back(): pl.pallas_call(attend_back_kernel, name='attend_back', grid=(heads // 2,)...  38 us
    pallas_call x1, Pallas kernels, attend(): pl.pallas_call(attend_kernel, name='attend', grid=(heads // 2,), in_specs...  27.5 us
    unnamed x73, local copies, waits for them, and re-layouts  17.6 us
    reduce_scatter x2, waiting for transfers between devices, scatter(): lax.psum_scatter(low(value), axes, scatter_dimension=dimension, tiled=True)  12.8 us
  transfers between devices with their start and end apart: 5, of which 1 were waited for; matrix products, arithmetic and copies ran while one was open for 11% of the time, Pallas kernels for 36%

profile of v3, /device:TPU:0, one launch (start us, length us, event | category | flops | bytes accessed | tf_op | source)
XLA Modules:
  0.0 600.1 jit_solution(2272275127182933742)
XLA Ops:
  7.8 1.8 multiply_reduce_fusion
  16.1 1.8 copy.78
  17.9 2.3 fusion.10
  22.0 23.0 %gather_keys.1 = bf16[8,2,128,576]{3,2,1,0:T(8,128)(2,1)} custom-call(bf16[2,128,576]{2,1,0:T(8,128)(2,1)} %pad_maximum_fusion.refs_0_), custom_call_target="tpu_custom_call" | custom-call | bytes 1179648 | tf_op jit(solution)/shard_map/gather_keys/pallas_call | solution.py:463
  45.3 2.8 convert_element_type.99
  52.5 27.5 %attend.1 = (bf16[256,1024]{1,0:T(8,128)(2,1)S(1)}, bf16[2048,1024]{1,0:T(8,128)(2,1)}, bf16[256,512]{1,0:T(8,128)(2,1)S(1)}, f32[256,512]{1,0:T(8,128)S(1)}, bf16[256,2048]{1,0:T(8,128)(2,1)S(1)}) custom-call(s32[1]{0:T(128)} %bitcast.base_ref, bf16[256,2048]{1,0:T(8,128)(2,1)S(1)} %copy-done.3, bf16[2048,768]{1,0:T(8,128)(2,1)} %wq_ref.1, ...), custom_call_target="tpu_custom_call" | custom-call | flops 7000000000 | bytes 20971520 | tf_op jit(solution)/shard_map/attend/pallas_call | solution.py:589
  83.2 24.1 %scatter_attn.1 = f32[64,2048]{1,0:T(8,128)} custom-call(bf16[4,64,2048]{2,1,0:T(8,128)(2,1)} %bitcast.73), custom_call_target="tpu_custom_call" | custom-call | bytes 4194304 | tf_op jit(solution)/shard_map/scatter_attn/pallas_call | solution.py:463
  110.9 54.6 %gather_ffn.1 = (bf16[8,4,64,2048]{3,2,1,0:T(8,128)(2,1)}, bf16[8,4,64,128]{3,2,1,0:T(8,128)(2,1)}) custom-call(bf16[64,2048]{1,0:T(8,128)(2,1)} %fusion.4.refs_0_, bf16[64,128]{1,0:T(8,128)(2,1)} %fusion.20.refs_1_), custom_call_target="tpu_custom_call" | custom-call | bytes 1114112 | tf_op jit(solution)/shard_map/gather_ffn/pallas_call | solution.py:463
  166.3 2.0 dynamic-slice_bitcast_fusion
  168.3 66.0 %experts.1 = (bf16[2048,896]{1,0:T(8,128)(2,1)}, bf16[2688,2048]{1,0:T(8,128)(2,1)}, bf16[2048,2048]{1,0:T(8,128)(2,1)}, bf16[2048,128]{1,0:T(8,128)(2,1)}) custom-call(s32[1]{0:T(128)} %bitcast.7.first_ref, bf16[2048,2048]{1,0:T(8,128)(2,1)} %bitcast.94, bf16[2048,2048]{1,0:T(8,128)(2,1)} %all-gather.2.cloned.1.call-done.g_ref.refs_1_, ...), custom_call_target="tpu_custom_call" | custom-call | flops 37580963840 | bytes 52428800 | tf_op jit(solution)/shard_map/experts/pallas_call | solution.py:834
  234.4 70.2 %weights.1 = (bf16[2,352,2048]{2,1,0:T(8,128)(2,1)}, bf16[2,352,2048]{2,1,0:T(8,128)(2,1)}, bf16[2,352,2048]{2,1,0:T(8,128)(2,1)}, bf16[3,88,2048]{2,1,0:T(8,128...) custom-call(bf16[2048,2048]{1,0:T(8,128)(2,1)} %bitcast.95, ...), custom_call_target="tpu_custom_call" | custom-call | flops 30064771072 | bytes 62914560 | tf_op jit(solution)/shard_map/weights/pallas_call | solution.py:985
  306.7 1.9 fusion.27
  308.6 23.5 %gather_hidden.1 = bf16[4,64,2048]{2,1,0:T(8,128)(2,1)} custom-call(bf16[64,2048]{1,0:T(8,128)(2,1)} %get-tuple-element.172.refs_0_), custom_call_target="tpu_custom_call" | custom-call | bytes 1048576 | tf_op jit(solution)/shard_map/gather_hidden/pallas_call | solution.py:463
  332.1 4.1 copy.86
  336.1 4.6 all-to-all-start
  340.8 2.1 convolution_convert_fusion.2
  342.9 38.0 %attend_back.1 = (bf16[256,768]{1,0:T(8,128)(2,1)}, bf16[512,1024]{1,0:T(8,128)(2,1)}, bf16[2048,576]{1,0:T(8,128)(2,1)}) custom-call(s32[1]{0:T(128)} %bitcast.base_ref, bf16[256,1024]{1,0:T(8,128)(2,1)} %copy-done.11, bf16[2048,1024]{1,0:T(8,128)(2,1)} %get-tuple-element.51.kv_ref, bf16[2048,576]{1,0:T(8,128)(2,1)} %bitcast.81, f32[256,512]{1,0:T(8,128)} %copy-done.12, ...), custom_call_target="tpu_custom_call" | custom-call | flops 10000000000 | bytes 20971520 | tf_op jit(solution)/shard_map/attend_back/pallas_call | solution.py:713
  381.0 3.0 convolution_convert_fusion.3
  384.0 48.9 %scatter_latent.1 = (f32[64,576]{1,0:T(8,128)}, f32[64,2048]{1,0:T(8,128)}) custom-call(bf16[4,2,4,64,576]{4,3,2,1,0:T(8,128)(2,1)} %bitcast.79, bf16[4,64,2048]{2,1,0:T(8,128)(2,1)} %bitcast.83), custom_call_target="tpu_custom_call" | custom-call | bytes 13631488 | tf_op jit(solution)/shard_map/scatter_latent/pallas_call | solution.py:463
  436.0 2.0 multiply_reduce_fusion.1
  440.5 2.3 convolution_convert_fusion.1
  442.7 4.4 copy.84
  447.1 5.2 convert_element_type.126
  452.3 2.7 convolution_convert_fusion
  455.0 4.0 copy.87
  459.0 1.9 add_convert_fusion.1.refs_2_
  460.9 5.3 convert_bitcast_fusion.1
  466.2 3.3 convert_bitcast_fusion
  474.1 12.8 %reduce-scatter.6.cloned.1.call-done = bf16[64,2048]{1,0:T(8,128)(2,1)} async-done(((bf16[256,2048]{1,0:T(8,128)(2,1)}), bf16[64,2048]{1,0:T(8,128)(2,1)}) %reduce-scatter.6.cloned.1.call-update) | async-done | bytes 262160 | tf_op jit(solution)/shard_map/reduce_scatter | solution.py:90
  488.7 92.3 %scatter_last.1 = (bf16[4,64,576]{2,1,0:T(8,128)(2,1)}, bf16[4,16,128]{2,1,0:T(8,128)(2,1)}, bf16[4,64,2048]{2,1,0:T(8,128)(2,1)}, f32[2,128,768]{2,1,0:T(8,128)...) custom-call(bf16[4,2,4,64,576]{4,3,2,1,0:T(8,128)(2,1)} %bitcast.75, bf16[4,2,4,16,128]{4,3,2,1,0:T(8,128)(2,1)} %bitcast.88, ...), custom_call_target="tpu_custom_call" | custom-call | bytes 28835840 | tf_op jit(solution)/shard_map/scatter_last/pallas_call | solution.py:463
  587.2 2.5 copy.101
  589.6 2.3 copy.102
  (131 shorter events, 42.8 us)
Async XLA Ops:
  7.2 158.4 %copy-start = (bf16[704,2048]{1,0:T(8,128)(2,1)S(1)}, bf16[704,2048]{1,0:T(8,128)(2,1)}, u32[]{:S(2)}) copy-start(bf16[704,2048]{1,0:T(8,128)(2,1)} %param.28) | copy-start | bytes 8650756
  7.2 161.1 %all-gather.2.cloned.1.call-start = ((), (), s32[]{:S(2)}) async-start(), calls=%async_computation.4 | async-start | bytes 9437184 | tf_op jit(solution)/shard_map/all_gather | solution.py:86
  7.2 3.9 copy-start.18
  11.2 4.1 copy-start.28
  12.0 1.0 copy-start.2
  13.0 32.0 %copy-start.16 = (f32[256,576]{0,1:T(8,128)}, f32[256,576]{0,1:T(8,128)S(1)}, u32[]{:S(2)}) copy-start(f32[256,576]{0,1:T(8,128)S(1)} %fusion.31) | copy-start | bytes 1769476
  22.0 26.1 %copy-start.29 = (s32[256,6]{0,1:T(8,128)S(1)}, s32[256,6]{0,1:T(8,128)}, u32[]{:S(2)}) copy-start(s32[256,6]{0,1:T(8,128)} %param.32) | copy-start | bytes 18436
  45.0 413.9 %reduce-scatter.4.cloned.1.call-start = ((), (), s32[]{:S(2)}) async-start(), calls=%async_computation.5 | async-start | bytes 9437184 | tf_op jit(solution)/shard_map/reduce_scatter | solution.py:1281
  49.6 30.4 %copy-start.8 = (f32[256,64]{1,0:T(8,128)}, f32[256,64]{1,0:T(8,128)S(1)}, u32[]{:S(2)}) copy-start(f32[256,64]{1,0:T(8,128)S(1)} %get-tuple-element.202.cos_ref) | copy-start | bytes 196612
  49.6 30.3 %copy-start.9 = (f32[256,64]{1,0:T(8,128)}, f32[256,64]{1,0:T(8,128)S(1)}, u32[]{:S(2)}) copy-start(f32[256,64]{1,0:T(8,128)S(1)} %get-tuple-element.203.sin_ref) | copy-start | bytes 196612
  49.6 1.4 copy-start.3
  51.0 1.4 copy-start.10
  83.2 25.5 %copy-start.25 = (bf16[2048,16]{0,1:T(8,128)(2,1)S(1)}, bf16[2048,16]{0,1:T(8,128)(2,1)}, u32[]{:S(2)}) copy-start(bf16[2048,16]{0,1:T(8,128)(2,1)} %param.25) | copy-start | bytes 196612
  83.2 25.5 %copy-start.26 = (f32[2048]{0:T(1024)S(1)}, f32[2048]{0:T(1024)}, u32[]{:S(2)}) copy-start(f32[2048]{0:T(1024)} %param.24) | copy-start | bytes 24580
  108.7 1.4 copy-start.13
  304.5 1.4 copy-start.23
  304.5 1.5 copy-start.14
  304.5 1.5 copy-start.21
  336.1 4.6 copy-start.7
  336.1 4.6 copy-start.15
  336.1 118.8 %all-to-all-start = ((bf16[3,88,2048]{1,0,2:T(4,128)(2,1)}), bf16[3,88,2048]{1,0,2:T(4,128)(2,1)}, u32[]{:S(2)}, u32[]{:S(2)}) async-start(bf16[3,88,2048]{1,0,2:T(4,128)(2,1)} %copy.86), calls=%async_computation.1 | async-start | bytes 4194304 | tf_op jit(solution)/shard_map/all_to_all | solution.py:1189
  340.7 128.8 %reduce-scatter.8.cloned.1.call-start = ((), (), s32[]{:S(2)}) async-start(), calls=%async_computation.7 | async-start | bytes 2359296 | tf_op jit(solution)/shard_map/reduce_scatter | solution.py:90
  342.9 144.1 %reduce-scatter.6.cloned.1.call-start = ((), (), s32[]{:S(2)}) async-start(), calls=%async_computation.6 | async-start | bytes 1310720 | tf_op jit(solution)/shard_map/reduce_scatter | solution.py:90
  342.9 38.1 %copy-start.30 = (bf16[2048,768]{1,0:T(8,128)(2,1)S(1)}, bf16[2048,768]{1,0:T(8,128)(2,1)}, u32[]{:S(2)}) copy-start(bf16[2048,768]{1,0:T(8,128)(2,1)} %wq_ref.1) | copy-start | bytes 9437188
  384.0 52.0 %copy-start.19 = (bf16[2048,576]{0,1:T(8,128)(2,1)S(1)}, bf16[2048,576]{0,1:T(8,128)(2,1)}, u32[]{:S(2)}) copy-start(bf16[2048,576]{0,1:T(8,128)(2,1)} %param.20) | copy-start | bytes 7077892
  384.0 52.0 %copy-start.27 = (f32[2048]{0:T(1024)S(1)}, f32[2048]{0:T(1024)}, u32[]{:S(2)}) copy-start(f32[2048]{0:T(1024)} %param.18) | copy-start | bytes 24580
  435.9 4.5 copy-start.4
  447.1 5.2 copy-start.22
  460.9 5.3 copy-start.17
  587.2 4.8 copy-start.20
  587.2 6.4 %copy-start.1 = (bf16[704,2048]{1,0:T(8,128)(2,1)S(1)}, bf16[704,2048]{1,0:T(8,128)(2,1)}, u32[]{:S(2)}) copy-start(bf16[704,2048]{1,0:T(8,128)(2,1)} %param.28) | copy-start | bytes 8650756
  587.2 5.6 copy-start.24
  (4 other events, 3.3 us)
Sparse Core Ops, SparseCore 0:
  45.2 51.5 all-gather.1
  304.7 94.5 reduce-scatter.3
  402.6 42.3 reduce-scatter.7
  459.1 27.7 reduce-scatter.5

commit v4 on v3

--- a/solution.py
+++ b/solution.py
@@ -435,7 +435,15 @@
     pl.semaphore_wait(barrier, 6)
 
 
-def exchange(tasks, collective_id, name):
+def held_back(walk, rounds):
+    for _ in range(rounds):
+        yield
+    yield from walk
+
+
+def exchange(tasks, collective_id, name, waits=None):
+    waits = waits or [0] * len(tasks)
+
     def kernel(*refs):
         place = Place()
         greet(place)
@@ -448,8 +456,8 @@
         outputs = take([len(task.outputs) for task in tasks])
         scratch = take([len(task.scratch) for task in tasks])
         running = [
-            task.steps(place, a, b, c)
-            for task, a, b, c in zip(tasks, inputs, outputs, scratch)
+            held_back(task.steps(place, a, b, c), wait)
+            for task, a, b, c, wait in zip(tasks, inputs, outputs, scratch, waits)
         ]
         while running:
             for walk in list(running):
@@ -1421,6 +1429,7 @@
             ],
             6,
             "scatter_last",
+            [0, 0, 0, 6, 6, 11],
         )
         latent_down_grad = latent_down_grad.reshape(-1, R + ROPE).astype(jnp.float32)
         small = small.reshape(-1).astype(jnp.float32)

time: 601 us -> 594 us (0.988)
  Pallas kernels: 468 us -> 459 us
    pallas_call x6, Pallas kernels: 266 us -> 258 us  [exchange(): pl.pallas_call(kernel, name=name, out_shape=flat((task.outputs for task i...]
  transfers between devices with their start and end apart: 5 -> 5, of which waited for: 1 -> 1; matrix products, arithmetic and copies ran while one was open for 11% -> 11% of each run, Pallas kernels for 36% -> 37%
where the time goes in v4:
time: 594 us; the launch traced here: 591 us
  Pallas kernels  459 us (77%)
  other arithmetic  43.4 us (7%)
  local copies, waits for them, and re-layouts  42 us (7%)
  matrix products  14.5 us (2%)
  between operations  14.3 us (2%)
  waiting for transfers between devices  12.9 us (2%)
    pallas_call x6, Pallas kernels, exchange(): pl.pallas_call(kernel, name=name, out_shape=flat((task.outputs for task i...  258 us
    pallas_call x1, Pallas kernels, run_weights(): pl.pallas_call(kernel, name='weights', grid=(steps,), in_specs=in_specs,...  70.2 us
    pallas_call x1, Pallas kernels, run_experts(): pl.pallas_call(functools.partial(expert_kernel, experts), name='experts',...  66 us
    pallas_call x1, Pallas kernels, attend_back(): pl.pallas_call(attend_back_kernel, name='attend_back', grid=(heads // 2,)...  38 us
    pallas_call x1, Pallas kernels, attend(): pl.pallas_call(attend_kernel, name='attend', grid=(heads // 2,), in_specs...  27.5 us
    unnamed x73, local copies, waits for them, and re-layouts  17.6 us
    reduce_scatter x2, waiting for transfers between devices, scatter(): lax.psum_scatter(low(value), axes, scatter_dimension=dimension, tiled=True)  12.8 us
  transfers between devices with their start and end apart: 5, of which 1 were waited for; matrix products, arithmetic and copies ran while one was open for 11% of the time, Pallas kernels for 37%

profile of v4, /device:TPU:0, one launch (start us, length us, event | category | flops | bytes accessed | tf_op | source)
XLA Modules:
  0.0 591.3 jit_solution(13519268943664183962)
XLA Ops:
  7.8 1.8 multiply_reduce_fusion
  16.1 1.8 copy.78
  17.9 2.3 fusion.10
  22.0 23.0 %gather_keys.1 = bf16[8,2,128,576]{3,2,1,0:T(8,128)(2,1)} custom-call(bf16[2,128,576]{2,1,0:T(8,128)(2,1)} %pad_maximum_fusion.refs_0_), custom_call_target="tpu_custom_call" | custom-call | bytes 1179648 | tf_op jit(solution)/shard_map/gather_keys/pallas_call | solution.py:471
  45.3 2.8 convert_element_type.99
  52.5 27.5 %attend.1 = (bf16[256,1024]{1,0:T(8,128)(2,1)S(1)}, bf16[2048,1024]{1,0:T(8,128)(2,1)}, bf16[256,512]{1,0:T(8,128)(2,1)S(1)}, f32[256,512]{1,0:T(8,128)S(1)}, bf16[256,2048]{1,0:T(8,128)(2,1)S(1)}) custom-call(s32[1]{0:T(128)} %bitcast.base_ref, bf16[256,2048]{1,0:T(8,128)(2,1)S(1)} %copy-done.3, bf16[2048,768]{1,0:T(8,128)(2,1)} %wq_ref.1, ...), custom_call_target="tpu_custom_call" | custom-call | flops 7000000000 | bytes 20971520 | tf_op jit(solution)/shard_map/attend/pallas_call | solution.py:597
  83.2 24.1 %scatter_attn.1 = f32[64,2048]{1,0:T(8,128)} custom-call(bf16[4,64,2048]{2,1,0:T(8,128)(2,1)} %bitcast.73), custom_call_target="tpu_custom_call" | custom-call | bytes 4194304 | tf_op jit(solution)/shard_map/scatter_attn/pallas_call | solution.py:471
  110.9 54.6 %gather_ffn.1 = (bf16[8,4,64,2048]{3,2,1,0:T(8,128)(2,1)}, bf16[8,4,64,128]{3,2,1,0:T(8,128)(2,1)}) custom-call(bf16[64,2048]{1,0:T(8,128)(2,1)} %fusion.4.refs_0_, bf16[64,128]{1,0:T(8,128)(2,1)} %fusion.20.refs_1_), custom_call_target="tpu_custom_call" | custom-call | bytes 1114112 | tf_op jit(solution)/shard_map/gather_ffn/pallas_call | solution.py:471
  166.3 2.0 dynamic-slice_bitcast_fusion
  168.3 66.0 %experts.1 = (bf16[2048,896]{1,0:T(8,128)(2,1)}, bf16[2688,2048]{1,0:T(8,128)(2,1)}, bf16[2048,2048]{1,0:T(8,128)(2,1)}, bf16[2048,128]{1,0:T(8,128)(2,1)}) custom-call(s32[1]{0:T(128)} %bitcast.7.first_ref, bf16[2048,2048]{1,0:T(8,128)(2,1)} %bitcast.94, bf16[2048,2048]{1,0:T(8,128)(2,1)} %all-gather.2.cloned.1.call-done.g_ref.refs_1_, ...), custom_call_target="tpu_custom_call" | custom-call | flops 37580963840 | bytes 52428800 | tf_op jit(solution)/shard_map/experts/pallas_call | solution.py:842
  234.4 70.2 %weights.1 = (bf16[2,352,2048]{2,1,0:T(8,128)(2,1)}, bf16[2,352,2048]{2,1,0:T(8,128)(2,1)}, bf16[2,352,2048]{2,1,0:T(8,128)(2,1)}, bf16[3,88,2048]{2,1,0:T(8,128...) custom-call(bf16[2048,2048]{1,0:T(8,128)(2,1)} %bitcast.95, ...), custom_call_target="tpu_custom_call" | custom-call | flops 30064771072 | bytes 62914560 | tf_op jit(solution)/shard_map/weights/pallas_call | solution.py:993
  306.7 1.9 fusion.27
  308.6 23.5 %gather_hidden.1 = bf16[4,64,2048]{2,1,0:T(8,128)(2,1)} custom-call(bf16[64,2048]{1,0:T(8,128)(2,1)} %get-tuple-element.172.refs_0_), custom_call_target="tpu_custom_call" | custom-call | bytes 1048576 | tf_op jit(solution)/shard_map/gather_hidden/pallas_call | solution.py:471
  332.1 4.1 copy.86
  336.1 4.6 all-to-all-start
  340.8 2.1 convolution_convert_fusion.2
  342.9 38.0 %attend_back.1 = (bf16[256,768]{1,0:T(8,128)(2,1)}, bf16[512,1024]{1,0:T(8,128)(2,1)}, bf16[2048,576]{1,0:T(8,128)(2,1)}) custom-call(s32[1]{0:T(128)} %bitcast.base_ref, bf16[256,1024]{1,0:T(8,128)(2,1)} %copy-done.11, bf16[2048,1024]{1,0:T(8,128)(2,1)} %get-tuple-element.51.kv_ref, bf16[2048,576]{1,0:T(8,128)(2,1)} %bitcast.81, f32[256,512]{1,0:T(8,128)} %copy-done.12, ...), custom_call_target="tpu_custom_call" | custom-call | flops 10000000000 | bytes 20971520 | tf_op jit(solution)/shard_map/attend_back/pallas_call | solution.py:721
  381.0 3.0 convolution_convert_fusion.3
  384.0 48.9 %scatter_latent.1 = (f32[64,576]{1,0:T(8,128)}, f32[64,2048]{1,0:T(8,128)}) custom-call(bf16[4,2,4,64,576]{4,3,2,1,0:T(8,128)(2,1)} %bitcast.79, bf16[4,64,2048]{2,1,0:T(8,128)(2,1)} %bitcast.83), custom_call_target="tpu_custom_call" | custom-call | bytes 13631488 | tf_op jit(solution)/shard_map/scatter_latent/pallas_call | solution.py:471
  436.0 2.0 multiply_reduce_fusion.1
  440.5 2.3 convolution_convert_fusion.1
  442.7 4.4 copy.84
  447.1 5.2 convert_element_type.126
  452.3 2.7 convolution_convert_fusion
  455.0 4.0 copy.87
  459.0 1.9 add_convert_fusion.1.refs_2_
  460.9 5.3 convert_bitcast_fusion.1
  466.2 3.3 convert_bitcast_fusion
  474.1 12.8 %reduce-scatter.6.cloned.1.call-done = bf16[64,2048]{1,0:T(8,128)(2,1)} async-done(((bf16[256,2048]{1,0:T(8,128)(2,1)}), bf16[64,2048]{1,0:T(8,128)(2,1)}) %reduce-scatter.6.cloned.1.call-update) | async-done | bytes 262160 | tf_op jit(solution)/shard_map/reduce_scatter | solution.py:90
  488.7 83.6 %scatter_last.1 = (bf16[4,64,576]{2,1,0:T(8,128)(2,1)}, bf16[4,16,128]{2,1,0:T(8,128)(2,1)}, bf16[4,64,2048]{2,1,0:T(8,128)(2,1)}, f32[2,128,768]{2,1,0:T(8,128)...) custom-call(bf16[4,2,4,64,576]{4,3,2,1,0:T(8,128)(2,1)} %bitcast.75, bf16[4,2,4,16,128]{4,3,2,1,0:T(8,128)(2,1)} %bitcast.88, ...), custom_call_target="tpu_custom_call" | custom-call | bytes 28835840 | tf_op jit(solution)/shard_map/scatter_last/pallas_call | solution.py:471
  578.4 2.5 copy.101
  580.9 2.3 copy.102
  (131 shorter events, 42.8 us)
Async XLA Ops:
  7.2 158.4 %copy-start = (bf16[704,2048]{1,0:T(8,128)(2,1)S(1)}, bf16[704,2048]{1,0:T(8,128)(2,1)}, u32[]{:S(2)}) copy-start(bf16[704,2048]{1,0:T(8,128)(2,1)} %param.28) | copy-start | bytes 8650756
  7.2 161.1 %all-gather.2.cloned.1.call-start = ((), (), s32[]{:S(2)}) async-start(), calls=%async_computation.4 | async-start | bytes 9437184 | tf_op jit(solution)/shard_map/all_gather | solution.py:86
  7.2 3.9 copy-start.18
  11.2 4.1 copy-start.28
  12.0 1.0 copy-start.2
  13.0 32.0 %copy-start.16 = (f32[256,576]{0,1:T(8,128)}, f32[256,576]{0,1:T(8,128)S(1)}, u32[]{:S(2)}) copy-start(f32[256,576]{0,1:T(8,128)S(1)} %fusion.31) | copy-start | bytes 1769476
  22.0 26.1 %copy-start.29 = (s32[256,6]{0,1:T(8,128)S(1)}, s32[256,6]{0,1:T(8,128)}, u32[]{:S(2)}) copy-start(s32[256,6]{0,1:T(8,128)} %param.32) | copy-start | bytes 18436
  45.0 413.9 %reduce-scatter.4.cloned.1.call-start = ((), (), s32[]{:S(2)}) async-start(), calls=%async_computation.5 | async-start | bytes 9437184 | tf_op jit(solution)/shard_map/reduce_scatter | solution.py:1289
  49.6 30.4 %copy-start.8 = (f32[256,64]{1,0:T(8,128)}, f32[256,64]{1,0:T(8,128)S(1)}, u32[]{:S(2)}) copy-start(f32[256,64]{1,0:T(8,128)S(1)} %get-tuple-element.202.cos_ref) | copy-start | bytes 196612
  49.6 30.3 %copy-start.9 = (f32[256,64]{1,0:T(8,128)}, f32[256,64]{1,0:T(8,128)S(1)}, u32[]{:S(2)}) copy-start(f32[256,64]{1,0:T(8,128)S(1)} %get-tuple-element.203.sin_ref) | copy-start | bytes 196612
  49.6 1.4 copy-start.3
  51.0 1.4 copy-start.10
  83.2 25.5 %copy-start.25 = (bf16[2048,16]{0,1:T(8,128)(2,1)S(1)}, bf16[2048,16]{0,1:T(8,128)(2,1)}, u32[]{:S(2)}) copy-start(bf16[2048,16]{0,1:T(8,128)(2,1)} %param.25) | copy-start | bytes 196612
  83.2 25.5 %copy-start.26 = (f32[2048]{0:T(1024)S(1)}, f32[2048]{0:T(1024)}, u32[]{:S(2)}) copy-start(f32[2048]{0:T(1024)} %param.24) | copy-start | bytes 24580
  108.7 1.4 copy-start.13
  304.5 1.4 copy-start.23
  304.5 1.5 copy-start.14
  304.5 1.5 copy-start.21
  336.1 4.6 copy-start.7
  336.1 4.6 copy-start.15
  336.1 118.8 %all-to-all-start = ((bf16[3,88,2048]{1,0,2:T(4,128)(2,1)}), bf16[3,88,2048]{1,0,2:T(4,128)(2,1)}, u32[]{:S(2)}, u32[]{:S(2)}) async-start(bf16[3,88,2048]{1,0,2:T(4,128)(2,1)} %copy.86), calls=%async_computation.1 | async-start | bytes 4194304 | tf_op jit(solution)/shard_map/all_to_all | solution.py:1197
  340.7 128.8 %reduce-scatter.8.cloned.1.call-start = ((), (), s32[]{:S(2)}) async-start(), calls=%async_computation.7 | async-start | bytes 2359296 | tf_op jit(solution)/shard_map/reduce_scatter | solution.py:90
  342.9 144.1 %reduce-scatter.6.cloned.1.call-start = ((), (), s32[]{:S(2)}) async-start(), calls=%async_computation.6 | async-start | bytes 1310720 | tf_op jit(solution)/shard_map/reduce_scatter | solution.py:90
  342.9 38.1 %copy-start.30 = (bf16[2048,768]{1,0:T(8,128)(2,1)S(1)}, bf16[2048,768]{1,0:T(8,128)(2,1)}, u32[]{:S(2)}) copy-start(bf16[2048,768]{1,0:T(8,128)(2,1)} %wq_ref.1) | copy-start | bytes 9437188
  384.0 52.0 %copy-start.19 = (bf16[2048,576]{0,1:T(8,128)(2,1)S(1)}, bf16[2048,576]{0,1:T(8,128)(2,1)}, u32[]{:S(2)}) copy-start(bf16[2048,576]{0,1:T(8,128)(2,1)} %param.20) | copy-start | bytes 7077892
  384.0 52.0 %copy-start.27 = (f32[2048]{0:T(1024)S(1)}, f32[2048]{0:T(1024)}, u32[]{:S(2)}) copy-start(f32[2048]{0:T(1024)} %param.18) | copy-start | bytes 24580
  435.9 4.5 copy-start.4
  447.1 5.2 copy-start.22
  460.9 5.3 copy-start.17
  578.4 4.8 copy-start.20
  578.4 6.4 %copy-start.1 = (bf16[704,2048]{1,0:T(8,128)(2,1)S(1)}, bf16[704,2048]{1,0:T(8,128)(2,1)}, u32[]{:S(2)}) copy-start(bf16[704,2048]{1,0:T(8,128)(2,1)} %param.28) | copy-start | bytes 8650756
  578.4 5.6 copy-start.24
  (4 other events, 3.2 us)
Sparse Core Ops, SparseCore 0:
  45.2 51.5 all-gather.1
  304.7 94.5 reduce-scatter.3
  402.6 42.3 reduce-scatter.7
  459.1 27.7 reduce-scatter.5
